TPU v7x, 32 devices: a whole 2x2x4 slice. The times are simulated.
32 devices in a mesh: section: 2 (over core), dp: 4 (over z), tensor: 4 (over y, x).
Axes of the slice: x: 2, y: 2, z: 4, core: 2. Of those that a mesh axis runs over, the one named last changes fastest.
Arguments:
- tokens: bfloat16 [2, 4, 2048, 1024], P(None, 'dp', 'tensor'), may hold values from -6 to 6
- cotangent: bfloat16 [2, 4, 2048, 1024], P(None, 'dp', 'tensor'), may hold values from -6 to 6
- doc_ids: int32 [2, 4, 2048], P(None, 'dp'), may hold values from 0 to 3, never falling along the last dimension, each value on 1 to 1024 neighbouring positions
- global_flags: int32 [2, 4, 32], P(None, 'dp'), may hold values from 0 to 2047, as said below
- w_attn: bfloat16 [2, 1024, 6, 1024], P('section', None, None, 'tensor'), may hold values from -1 to 1
- w_out: bfloat16 [2, 1024, 1024], P('section', 'tensor'), may hold values from -0.75 to 0.75
- w_up: bfloat16 [2, 1024, 4096], P('section', None, 'tensor'), may hold values from -0.1875 to 0.1875
- w_down: bfloat16 [2, 4096, 1024], P('section', 'tensor'), may hold values from -0.125 to 0.125
- ln_gain: float32 [2, 2, 1024], P('section'), may hold values from 0.5 to 1.5
- ln_bias: float32 [2, 2, 1024], P('section'), may hold values from -1.5 to 1.5
Outputs:
- layer_out: bfloat16 [2, 2, 4, 2048, 1024], P('section', None, 'dp', 'tensor')
- input_grad: bfloat16 [2, 2, 4, 2048, 1024], P('section', None, 'dp', 'tensor')
- grad_w_attn: float32 [2, 1024, 6, 1024], P('section', None, None, 'tensor')
- grad_w_out: float32 [2, 1024, 1024], P('section', 'tensor')
- grad_w_up: float32 [2, 1024, 4096], P('section', None, 'tensor')
- grad_w_down: float32 [2, 4096, 1024], P('section', 'tensor')
- grad_ln_gain: float32 [2, 2, 1024], P('section')
- grad_ln_bias: float32 [2, 2, 1024], P('section')
- clipped_qk: float32 [2, 1024, 4, 1024], P('section', None, None, 'tensor')
Inputs may be any that keep to these rules, and one draw needn't show every extreme that they name: `doc_ids`: ids never fall along a sequence. `global_flags`: the 32 positions of a sequence are distinct and rise.
All inputs are finite; a program needn't handle non-finite values.
Results may differ from a plain program's by a relative error of at most 0.03.
Values may be sent and summed in bfloat16 or wider, within the bound.
No kernel may reach another device: no remote copies, remote signals or barrier semaphores. Data moves between devices by JAX's collectives and lax.ppermute only.
A program may use at most 320 MiB of HBM per device.

v0:
```python
from functools import partial

import jax
import jax.numpy as jnp
from jax import lax
from jax.sharding import PartitionSpec as P

HEAD = 64
HALF = 512
QBLOCK = 512


masked_fill = -1e30
clip_limit = 10.0


def swapped(block, axis, distance):
    count = lax.axis_size(axis)
    route = []
    for low in range(count):
        high = low | 1 << distance
        if high != low and high < count:
            route += [(low, high), (high, low)]
    return lax.ppermute(block, axis, route)


def layer_norm(resid, gain, shift):
    centred = resid - jnp.mean(resid, -1, keepdims=True)
    spread = jnp.mean(centred * centred, -1, keepdims=True)
    return centred * lax.rsqrt(spread + 1e-05) * gain + shift


def times_transposed(left, right):
    return lax.dot_general(
        left, right, (((1,), (1,)), ((), ())), preferred_element_type=jnp.float32
    )


def rows_contracted(left, right):
    return lax.dot_general(
        left, right, (((0,), (0,)), ((), ())), preferred_element_type=jnp.float32
    )


def global_info(docs_row, glob_pos):
    length = docs_row.shape[0]
    glob_row = jnp.any(glob_pos[:, None] == jnp.arange(length, dtype=jnp.int32)[None, :], 0)
    glob_docs = jnp.take(docs_row, glob_pos, axis=0)
    return (glob_pos, glob_row, glob_docs)


def band_scores(parts, first_row, docs_row, info, far_keys):
    glob_pos, glob_row, glob_docs = info
    length = parts.shape[0]
    band = min(3 * QBLOCK, length)
    score_scale = parts.shape[-1] ** (-0.5)
    key_start = jnp.clip(first_row - QBLOCK, 0, length - band)
    rows = first_row + jnp.arange(QBLOCK, dtype=jnp.int32)
    cols = key_start + jnp.arange(band, dtype=jnp.int32)
    row_docs = lax.dynamic_slice_in_dim(docs_row, first_row, QBLOCK, 0)
    key_docs = lax.dynamic_slice_in_dim(docs_row, key_start, band, 0)
    near_mask = (row_docs[:, None] == key_docs[None, :]) & (
        jnp.abs(rows[:, None] - cols[None, :]) <= HALF
    )
    far_mask = (row_docs[:, None] == glob_docs[None, :]) & (
        jnp.abs(rows[:, None] - glob_pos[None, :]) > HALF
    )
    query = lax.dynamic_slice_in_dim(parts, first_row, QBLOCK, 0)[:, 0]
    band_rows = lax.dynamic_slice_in_dim(parts, key_start, band, 0)
    band_keys = band_rows[:, 1]
    band_vals = band_rows[:, 2]
    near_scores = (
        jnp.einsum("qhe,khe->hqk", query, band_keys, preferred_element_type=jnp.float32)
        * score_scale
    )
    far_scores = (
        jnp.einsum("qhe,ghe->hqg", query, far_keys, preferred_element_type=jnp.float32)
        * score_scale
    )
    near_masked = jnp.where(near_mask[None], near_scores, masked_fill)
    far_masked = jnp.where(far_mask[None], far_scores, masked_fill)
    return (key_start, query, band_keys, band_vals, near_masked, far_masked)


def global_scores(parts, docs_row, info):
    glob_pos, glob_row, glob_docs = info
    score_scale = parts.shape[-1] ** (-0.5)
    glob_queries = jnp.take(parts[:, 3], glob_pos, axis=0)
    scores = (
        jnp.einsum("ghe,khe->hgk", glob_queries, parts[:, 4], preferred_element_type=jnp.float32)
        * score_scale
    )
    same_doc = glob_docs[:, None] == docs_row[None, :]
    return (glob_queries, jnp.where(same_doc[None], scores, masked_fill))


def attend(parts, docs_row, info):
    glob_pos, glob_row, glob_docs = info
    length = parts.shape[0]
    starts = jnp.arange(length // QBLOCK, dtype=jnp.int32) * QBLOCK
    far_keys = jnp.take(parts[:, 1], glob_pos, axis=0)
    far_vals = jnp.take(parts[:, 2], glob_pos, axis=0)

    def one_block(first_row):
        key_start, query, band_keys, band_vals, near_masked, far_masked = band_scores(
            parts, first_row, docs_row, info, far_keys
        )
        row_max = jnp.maximum(jnp.max(near_masked, -1), jnp.max(far_masked, -1))
        near_exp = jnp.exp(near_masked - row_max[..., None])
        far_exp = jnp.exp(far_masked - row_max[..., None])
        denominator = jnp.sum(near_exp, -1) + jnp.sum(far_exp, -1)
        near_probs = (near_exp / denominator[..., None]).astype(jnp.bfloat16)
        far_probs = (far_exp / denominator[..., None]).astype(jnp.bfloat16)
        context = jnp.einsum(
            "hqk,khe->qhe", near_probs, band_vals, preferred_element_type=jnp.float32
        )
        context = context + jnp.einsum(
            "hqg,ghe->qhe", far_probs, far_vals, preferred_element_type=jnp.float32
        )
        return (context, row_max + jnp.log(denominator), row_max)

    local_ctx, local_sums, local_max = lax.map(one_block, starts)
    local_ctx = local_ctx.reshape(length, parts.shape[2], parts.shape[3])
    glob_queries, glob_masked = global_scores(parts, docs_row, info)
    glob_max = jnp.max(glob_masked, -1)
    glob_exp = jnp.exp(glob_masked - glob_max[..., None])
    glob_den = jnp.sum(glob_exp, -1)
    glob_probs = (glob_exp / glob_den[..., None]).astype(jnp.bfloat16)
    glob_ctx = jnp.einsum(
        "hgk,khe->ghe", glob_probs, parts[:, 5], preferred_element_type=jnp.float32
    )
    context = local_ctx.at[glob_pos].set(glob_ctx)
    peak_logits = jnp.stack([jnp.max(local_max, (0, 2)), jnp.max(glob_max, -1)])
    return (
        context.reshape(length, -1).astype(jnp.bfloat16),
        (local_sums, glob_max + jnp.log(glob_den)),
        peak_logits,
    )


def attend_back(parts, log_sums, grad_context, docs_row, info):
    glob_pos, glob_row, glob_docs = info
    local_sums, glob_sums = log_sums
    length = parts.shape[0]
    band = min(3 * QBLOCK, length)
    score_scale = parts.shape[-1] ** (-0.5)
    far_keys = jnp.take(parts[:, 1], glob_pos, axis=0)
    far_vals = jnp.take(parts[:, 2], glob_pos, axis=0)
    grad_local = jnp.where(glob_row[:, None, None], jnp.zeros_like(grad_context), grad_context)

    def one_block(carry, block_index):
        grad_k, grad_v, grad_far_k, grad_far_v = carry
        first_row = block_index * QBLOCK
        key_start, query, band_keys, band_vals, near_masked, far_masked = band_scores(
            parts, first_row, docs_row, info, far_keys
        )
        block_sums = lax.dynamic_index_in_dim(local_sums, block_index, 0, False)
        near_probs = jnp.exp(near_masked - block_sums[..., None])
        far_probs = jnp.exp(far_masked - block_sums[..., None])
        grad_out = lax.dynamic_slice_in_dim(grad_local, first_row, QBLOCK, 0)
        band_grad_v = jnp.einsum(
            "hqk,qhe->khe",
            near_probs.astype(jnp.bfloat16),
            grad_out,
            preferred_element_type=jnp.float32,
        )
        grad_far_v = grad_far_v + jnp.einsum(
            "hqg,qhe->ghe",
            far_probs.astype(jnp.bfloat16),
            grad_out,
            preferred_element_type=jnp.float32,
        )
        near_grad_p = jnp.einsum(
            "qhe,khe->hqk", grad_out, band_vals, preferred_element_type=jnp.float32
        )
        far_grad_p = jnp.einsum(
            "qhe,ghe->hqg", grad_out, far_vals, preferred_element_type=jnp.float32
        )
        row_dot = jnp.sum(near_grad_p * near_probs, -1) + jnp.sum(far_grad_p * far_probs, -1)
        near_grad_s = (near_probs * (near_grad_p - row_dot[..., None])).astype(jnp.bfloat16)
        far_grad_s = (far_probs * (far_grad_p - row_dot[..., None])).astype(jnp.bfloat16)
        grad_q = jnp.einsum(
            "hqk,khe->qhe", near_grad_s, band_keys, preferred_element_type=jnp.float32
        )
        grad_q = (
            grad_q
            + jnp.einsum("hqg,ghe->qhe", far_grad_s, far_keys, preferred_element_type=jnp.float32)
        ) * score_scale
        band_grad_k = (
            jnp.einsum("hqk,qhe->khe", near_grad_s, query, preferred_element_type=jnp.float32)
            * score_scale
        )
        grad_far_k = (
            grad_far_k
            + jnp.einsum("hqg,qhe->ghe", far_grad_s, query, preferred_element_type=jnp.float32)
            * score_scale
        )
        grad_k = lax.dynamic_update_slice_in_dim(
            grad_k, lax.dynamic_slice_in_dim(grad_k, key_start, band, 0) + band_grad_k, key_start, 0
        )
        grad_v = lax.dynamic_update_slice_in_dim(
            grad_v, lax.dynamic_slice_in_dim(grad_v, key_start, band, 0) + band_grad_v, key_start, 0
        )
        return ((grad_k, grad_v, grad_far_k, grad_far_v), grad_q)

    zero_full = jnp.zeros(parts[:, 0].shape, jnp.float32)
    zero_far = jnp.zeros(far_keys.shape, jnp.float32)
    blocks = jnp.arange(length // QBLOCK, dtype=jnp.int32)
    carry, grad_q = lax.scan(one_block, (zero_full, zero_full, zero_far, zero_far), blocks)
    grad_k = carry[0].at[glob_pos].add(carry[2])
    grad_v = carry[1].at[glob_pos].add(carry[3])
    grad_q = grad_q.reshape(length, parts.shape[2], parts.shape[3])
    glob_queries, glob_masked = global_scores(parts, docs_row, info)
    glob_probs = jnp.exp(glob_masked - glob_sums[..., None])
    glob_grad_out = jnp.take(grad_context, glob_pos, axis=0)
    grad_gv = jnp.einsum(
        "hgk,ghe->khe",
        glob_probs.astype(jnp.bfloat16),
        glob_grad_out,
        preferred_element_type=jnp.float32,
    )
    glob_grad_p = jnp.einsum(
        "ghe,khe->hgk", glob_grad_out, parts[:, 5], preferred_element_type=jnp.float32
    )
    glob_grad_s = (
        glob_probs * (glob_grad_p - jnp.sum(glob_grad_p * glob_probs, -1, keepdims=True))
    ).astype(jnp.bfloat16)
    glob_grad_q = (
        jnp.einsum("hgk,khe->ghe", glob_grad_s, parts[:, 4], preferred_element_type=jnp.float32)
        * score_scale
    )
    grad_gk = (
        jnp.einsum("hgk,ghe->khe", glob_grad_s, glob_queries, preferred_element_type=jnp.float32)
        * score_scale
    )
    grad_gq = zero_full.at[glob_pos].set(glob_grad_q)
    stacked = jnp.stack([grad_q, grad_k, grad_v, grad_gq, grad_gk, grad_gv], 1)
    return stacked.reshape(length, -1).astype(jnp.bfloat16)


def pass_section(value):
    return swapped(value, "section", 0)


def shards(tokens, cotangent, doc_ids, global_flags, w_attn, w_out, w_up, w_down, ln_gain, ln_bias):
    section_index = lax.axis_index("section")
    micro_count = tokens.shape[0]
    own_rows = tokens.shape[2]
    width = tokens.shape[3]
    attn_matrix = w_attn[0].reshape(width, -1)
    out_matrix = w_out[0]
    gains = ln_gain[0]
    shifts = ln_bias[0]
    up_matrix, down_matrix = (w_up[0], w_down[0])
    received_act = jnp.zeros((own_rows, width), jnp.bfloat16)
    received_grad = jnp.zeros((own_rows, width), jnp.bfloat16)
    outputs_acc = jnp.zeros((micro_count, own_rows, width), jnp.bfloat16)
    grads_in_acc = jnp.zeros((micro_count, own_rows, width), jnp.bfloat16)
    saved_list = []
    weight_acc = None
    norm_acc = None
    peak_acc = None
    token_rows = tokens[:, 0]
    cot_rows = cotangent[:, 0]
    docs_rows = doc_ids[:, 0]
    flag_rows = global_flags[:, 0]
    order = [("forward", 0)]
    for micro_index in range(micro_count):
        order.append(("forward", micro_index + 1))
        order.append(("backward", micro_index))
    order.append(("backward", micro_count))
    for phase_kind, phase in order:
        if phase_kind == "forward":
            fwd_index = phase - section_index
            fwd_valid = (fwd_index >= 0) & (fwd_index < micro_count)
            fwd_slot = jnp.clip(fwd_index, 0, micro_count - 1)
            own_tokens = lax.dynamic_index_in_dim(token_rows, fwd_slot, 0, False)
            layer_input = jnp.where(section_index == 0, own_tokens, received_act)
            docs_now = lax.dynamic_index_in_dim(docs_rows, fwd_slot, 0, False)
            info = global_info(docs_now, lax.dynamic_index_in_dim(flag_rows, fwd_slot, 0, False))
            layer_x_full = lax.all_gather(layer_input, "tensor", axis=0, tiled=True)
            layer_seq_len = layer_x_full.shape[0]
            layer_projected = jnp.dot(
                layer_x_full, attn_matrix, preferred_element_type=jnp.float32
            ).astype(jnp.bfloat16)
            layer_context, layer_log_sums, peak_logits = attend(
                layer_projected.reshape(layer_seq_len, 6, -1, HEAD), docs_now, info
            )
            attn_own = lax.psum_scatter(
                jnp.dot(layer_context, out_matrix, preferred_element_type=jnp.float32),
                "tensor",
                scatter_dimension=0,
                tiled=True,
            )
            layer_resid_one = layer_input.astype(jnp.float32) + attn_own
            hidden = layer_norm(layer_resid_one, gains[0], shifts[0])
            hidden_low = hidden.astype(jnp.bfloat16)
            layer_hidden_rows = lax.all_gather(hidden_low, "tensor", axis=0, tiled=True)
            layer_up_value = jnp.dot(
                layer_hidden_rows, up_matrix, preferred_element_type=jnp.float32
            )
            layer_activated = jax.nn.gelu(layer_up_value, approximate=False).astype(jnp.bfloat16)
            mlp_own = lax.psum_scatter(
                jnp.dot(layer_activated, down_matrix, preferred_element_type=jnp.float32),
                "tensor",
                scatter_dimension=0,
                tiled=True,
            )
            layer_resid_two = hidden + mlp_own
            output = layer_norm(layer_resid_two, gains[1], shifts[1])
            layer_saved = (
                layer_x_full,
                layer_projected,
                layer_log_sums,
                layer_context,
                layer_resid_one,
                layer_hidden_rows,
                layer_up_value,
                layer_activated,
                layer_resid_two,
            )
            layer_output, saved, peak_logits = (
                output.astype(jnp.bfloat16),
                layer_saved,
                peak_logits,
            )
            if peak_acc is None:
                peak_acc = jnp.where(fwd_valid, peak_logits, masked_fill)
            else:
                peak_acc = jnp.where(fwd_valid, jnp.maximum(peak_acc, peak_logits), peak_acc)
            previous_out = lax.dynamic_index_in_dim(outputs_acc, fwd_slot, 0, False)
            outputs_acc = lax.dynamic_update_index_in_dim(
                outputs_acc, jnp.where(fwd_valid, layer_output, previous_out), fwd_slot, 0
            )
            saved_list.append((saved, docs_now, info))
            if phase < micro_count:
                received_act = pass_section(layer_output)
        else:
            back_index = phase - 1 + section_index
            back_valid = (back_index >= 0) & (back_index < micro_count)
            back_slot = jnp.clip(back_index, 0, micro_count - 1)
            newer = saved_list[min(phase + 1, len(saved_list) - 1)]
            older = saved_list[max(phase - 1, 0)]
            chosen = jax.tree.map(
                lambda later_item, earlier_item: jnp.where(
                    section_index == 1, later_item, earlier_item
                ),
                newer,
                older,
            )
            grad_source = jnp.where(
                section_index == 1,
                lax.dynamic_index_in_dim(cot_rows, back_slot, 0, False),
                received_grad,
            )
            (
                x_full,
                projected,
                log_sums,
                context,
                resid_one,
                hidden_rows,
                up_value,
                activated,
                resid_two,
            ) = chosen[0]
            seq_len = x_full.shape[0]
            _, norm_two_back = jax.vjp(layer_norm, resid_two, gains[1], shifts[1])
            grad_two, gain_two, shift_two = norm_two_back(grad_source.astype(jnp.float32))
            grad_mlp = grad_two.astype(jnp.bfloat16)
            grad_mlp_rows = lax.all_gather(grad_mlp, "tensor", axis=0, tiled=True)
            grad_down = rows_contracted(activated, grad_mlp_rows)
            grad_act = times_transposed(grad_mlp_rows, down_matrix)
            _, gelu_back = jax.vjp(partial(jax.nn.gelu, approximate=False), up_value)
            grad_up_value = gelu_back(grad_act)[0].astype(jnp.bfloat16)
            grad_upw = rows_contracted(hidden_rows, grad_up_value)
            grad_hidden = (
                lax.psum_scatter(
                    times_transposed(grad_up_value, up_matrix),
                    "tensor",
                    scatter_dimension=0,
                    tiled=True,
                )
                + grad_two
            )
            _, norm_one_back = jax.vjp(layer_norm, resid_one, gains[0], shifts[0])
            grad_one, gain_one, shift_one = norm_one_back(grad_hidden)
            grad_attn_full = lax.all_gather(
                grad_one.astype(jnp.bfloat16), "tensor", axis=0, tiled=True
            )
            grad_outw = rows_contracted(context, grad_attn_full)
            grad_context = times_transposed(grad_attn_full, out_matrix).astype(jnp.bfloat16)
            grad_proj = attend_back(
                projected.reshape(seq_len, 6, -1, HEAD),
                log_sums,
                grad_context.reshape(seq_len, -1, HEAD),
                chosen[1],
                chosen[2],
            )
            grad_attnw = rows_contracted(x_full, grad_proj)
            grad_input = (
                lax.psum_scatter(
                    times_transposed(grad_proj, attn_matrix),
                    "tensor",
                    scatter_dimension=0,
                    tiled=True,
                )
                + grad_one
            )
            weight_terms = (grad_attnw, grad_outw, grad_upw, grad_down)
            norm_terms = (jnp.stack([gain_one, gain_two]), jnp.stack([shift_one, shift_two]))
            grad_input, weight_terms, norm_terms = (grad_input, weight_terms, norm_terms)
            weight_terms = jax.tree.map(
                lambda update_term: jnp.where(back_valid, update_term, jnp.zeros_like(update_term)),
                weight_terms,
            )
            norm_terms = jax.tree.map(
                lambda update_term: jnp.where(back_valid, update_term, jnp.zeros_like(update_term)),
                norm_terms,
            )
            if weight_acc is None:
                weight_acc = weight_terms
                norm_acc = norm_terms
            else:
                weight_acc = jax.tree.map(
                    lambda running, update_term: running + update_term, weight_acc, weight_terms
                )
                norm_acc = jax.tree.map(
                    lambda running, update_term: running + update_term, norm_acc, norm_terms
                )
            grad_low = grad_input.astype(jnp.bfloat16)
            previous_grad = lax.dynamic_index_in_dim(grads_in_acc, back_slot, 0, False)
            grads_in_acc = lax.dynamic_update_index_in_dim(
                grads_in_acc, jnp.where(back_valid, grad_low, previous_grad), back_slot, 0
            )
            if phase < micro_count:
                received_grad = pass_section(grad_low)
    peaks_all = lax.pmax(peak_acc, "dp")
    acc_attn, acc_out, acc_up, acc_down = weight_acc
    summed = lax.psum((acc_attn, acc_out, acc_up, acc_down), "dp")
    gain_sum, shift_sum = lax.psum(norm_acc, ("dp", "tensor"))
    factors = jnp.sqrt(clip_limit / jnp.maximum(peaks_all, clip_limit))
    columns = jnp.repeat(factors, HEAD, axis=1)
    attn_local = w_attn[0].astype(jnp.float32)
    clipped = jnp.stack(
        [
            attn_local[:, 0] * columns[0][None, :],
            attn_local[:, 1] * columns[0][None, :],
            attn_local[:, 3] * columns[1][None, :],
            attn_local[:, 4] * columns[1][None, :],
        ],
        1,
    )
    layer_out = outputs_acc[None, :, None]
    input_grad = grads_in_acc[None, :, None]
    return (
        layer_out,
        input_grad,
        summed[0].reshape(1, width, 6, -1),
        summed[1][None],
        summed[2][None],
        summed[3][None],
        gain_sum[None],
        shift_sum[None],
        clipped[None],
    )


def solution(mesh):
    in_specs = (
        P(None, "dp", "tensor", None),
        P(None, "dp", "tensor", None),
        P(None, "dp", None),
        P(None, "dp", None),
        P("section", None, None, "tensor"),
        P("section", "tensor", None),
        P("section", None, "tensor"),
        P("section", "tensor", None),
        P("section", None, None),
        P("section", None, None),
    )
    out_specs = (
        P("section", None, "dp", "tensor", None),
        P("section", None, "dp", "tensor", None),
        P("section", None, None, "tensor"),
        P("section", "tensor", None),
        P("section", None, "tensor"),
        P("section", "tensor", None),
        P("section", None, None),
        P("section", None, None),
        P("section", None, None, "tensor"),
    )
    return jax.shard_map(shards, mesh=mesh, in_specs=in_specs, out_specs=out_specs, check_vma=False)
```

profile of v0, /device:TPU:0, one launch (start us, length us, event | category | flops | bytes accessed | tf_op | source)
XLA Modules:
  0.0 4103.7 jit_solution(4887691331030546349)
XLA Ops:
  20.3 45.6 %all-gather.36.cloned.1.call-done = bf16[1,1,2048,1024]{3,2,1,0:T(8,128)(2,1)} async-done(((bf16[1,1,512,1024]{3,2,1,0:T(8,128)(2,1)}), bf16[1,1,2048,1024]{3,2,1,0:T(8,128)(2,1)}) %all-gather.36.cloned.1.call-update) | async-done | bytes 4194320 | tf_op jit(solution)/shard_map/all_gather | solution.py:281
  98.9 92.0 %while.111 = (s32[]{:T(128)}, f32[4,512,4,64]{1,3,2,0:T(8,128)}, f32[4,4,512]{2,1,0:T(4,128)S(1)}, f32[4,4,512]{2,1,0:T(4,128)S(1)}, s32[4]{0:T(128)S(1)}, /*ind...) while((s32[]{:T(128)}, f32[4,512,4,64]{1,3,2,0:T(8,128)}, ...), condition=%wide.region_5.8_spmd, body=%wide.region_0.7_spmd.sunk | while | flops 864501760 | bytes 95949416 | solution.py:122
  216.5 85.8 %reduce-scatter.13.cloned.1.call-done = f32[512,1024]{1,0:T(8,128)} async-done(((f32[2048,1024]{1,0:T(8,128)}), f32[512,1024]{1,0:T(8,128)}) %reduce-scatter.13.cloned.1.call-update) | async-done | bytes 2097168 | tf_op jit(solution)/shard_map/reduce_scatter | solution.py:289
  307.3 52.8 %all-gather.14.cloned.1.call-done = bf16[2048,1024]{1,0:T(8,128)(2,1)} async-done(((bf16[512,1024]{1,0:T(8,128)(2,1)}), bf16[2048,1024]{1,0:T(8,128)(2,1)}) %all-gather.14.cloned.1.call-update) | async-done | bytes 4194320 | tf_op jit(solution)/shard_map/all_gather | solution.py:298
  393.5 86.5 %reduce-scatter.15.cloned.1.call-done = f32[512,1024]{1,0:T(8,128)} async-done(((f32[2048,1024]{1,0:T(8,128)}), f32[512,1024]{1,0:T(8,128)}) %reduce-scatter.15.cloned.1.call-update) | async-done | bytes 2097168 | tf_op jit(solution)/shard_map/reduce_scatter | solution.py:303
  490.9 52.0 %all-gather.16.cloned.1.call-done = bf16[2048,1024]{1,0:T(8,128)(2,1)} async-done(((bf16[512,1024]{1,0:T(8,128)(2,1)}), bf16[2048,1024]{1,0:T(8,128)(2,1)}) %all-gather.16.cloned.1.call-update) | async-done | bytes 4194320 | tf_op jit(solution)/shard_map/all_gather | solution.py:281
  576.1 92.0 %while.112 = (s32[]{:T(128)}, f32[4,512,4,64]{1,3,2,0:T(8,128)}, f32[4,4,512]{2,1,0:T(4,128)S(1)}, f32[4,4,512]{2,1,0:T(4,128)S(1)}, s32[4]{0:T(128)S(1)}, /*ind...) while((s32[]{:T(128)}, f32[4,512,4,64]{1,3,2,0:T(8,128)}, ...), condition=%wide.region_20.23_spmd, body=%wide.region_15.22_spmd.sunk | while | flops 864501760 | bytes 95949416 | solution.py:122
  695.8 86.3 %reduce-scatter.17.cloned.1.call-done = f32[512,1024]{1,0:T(8,128)} async-done(((f32[2048,1024]{1,0:T(8,128)}), f32[512,1024]{1,0:T(8,128)}) %reduce-scatter.17.cloned.1.call-update) | async-done | bytes 2097168 | tf_op jit(solution)/shard_map/reduce_scatter | solution.py:289
  793.9 52.8 %all-gather.18.cloned.1.call-done = bf16[2048,1024]{1,0:T(8,128)(2,1)} async-done(((bf16[512,1024]{1,0:T(8,128)(2,1)}), bf16[2048,1024]{1,0:T(8,128)(2,1)}) %all-gather.18.cloned.1.call-update) | async-done | bytes 4194320 | tf_op jit(solution)/shard_map/all_gather | solution.py:298
  880.2 86.5 %reduce-scatter.19.cloned.1.call-done = f32[512,1024]{1,0:T(8,128)} async-done(((f32[2048,1024]{1,0:T(8,128)}), f32[512,1024]{1,0:T(8,128)}) %reduce-scatter.19.cloned.1.call-update) | async-done | bytes 2097168 | tf_op jit(solution)/shard_map/reduce_scatter | solution.py:303
  1126.6 92.3 %while.113 = (s32[]{:T(128)}, f32[4,512,4,64]{1,3,2,0:T(8,128)}, f32[4,4,512]{2,1,0:T(4,128)S(1)}, f32[4,4,512]{2,1,0:T(4,128)S(1)}, s32[4]{0:T(128)S(1)}, /*ind...) while((s32[]{:T(128)}, f32[4,512,4,64]{1,3,2,0:T(8,128)}, ...), condition=%wide.region_35.38_spmd, body=%wide.region_30.37_spmd.sunk | while | flops 864501760 | bytes 95949416 | solution.py:122
  1254.4 78.4 %reduce-scatter.21.cloned.1.call-done = f32[512,1024]{1,0:T(8,128)} async-done(((f32[2048,1024]{1,0:T(8,128)}), f32[512,1024]{1,0:T(8,128)}) %reduce-scatter.21.cloned.1.call-update) | async-done | bytes 2097168 | tf_op jit(solution)/shard_map/reduce_scatter | solution.py:289
  1421.4 342.6 %while.114 = (s32[]{:T(128)}, f32[2048,4,64]{0,2,1:T(8,128)}, f32[2048,4,64]{0,2,1:T(8,128)}, f32[32,4,64]{2,0,1:T(8,128)S(1)}, f32[32,4,64]{2,0,1:T(8,128)S(1)}...) while((s32[]{:T(128)}, f32[2048,4,64]{0,2,1:T(8,128)}, ...), condition=%wide.region_59.62_spmd.clone, body=%wide.region_56.61_spmd.clone.sunk | while | flops 2089738240 | bytes 188961584 | solution.py:209
  1860.1 52.8 %reduce-scatter.27.cloned.1.call-done = f32[512,1024]{1,0:T(8,128)} async-done(((f32[2048,1024]{1,0:T(8,128)}), f32[512,1024]{1,0:T(8,128)}) %reduce-scatter.27.cloned.1.call-update) | async-done | bytes 2097168 | tf_op jit(solution)/shard_map/reduce_scatter | solution.py:402
  1918.0 84.5 %reduce-scatter.23.cloned.1.call-done = f32[512,1024]{1,0:T(8,128)} async-done(((f32[2048,1024]{1,0:T(8,128)}), f32[512,1024]{1,0:T(8,128)}) %reduce-scatter.23.cloned.1.call-update) | async-done | bytes 2097168 | tf_op jit(solution)/shard_map/reduce_scatter | solution.py:303
  2020.5 52.8 %all-gather.28.cloned.1.call-done = bf16[2048,1024]{1,0:T(8,128)(2,1)} async-done(((bf16[512,1024]{1,0:T(8,128)(2,1)}), bf16[2048,1024]{1,0:T(8,128)(2,1)}) %all-gather.28.cloned.1.call-update) | async-done | bytes 4194320 | tf_op jit(solution)/shard_map/all_gather | solution.py:371
  2111.5 84.0 %reduce-scatter.29.cloned.1.call-done = f32[512,1024]{1,0:T(8,128)} async-done(((f32[2048,1024]{1,0:T(8,128)}), f32[512,1024]{1,0:T(8,128)}) %reduce-scatter.29.cloned.1.call-update) | async-done | bytes 2097168 | tf_op jit(solution)/shard_map/reduce_scatter | solution.py:378
  2274.3 344.9 %while.115 = (s32[]{:T(128)}, f32[2048,4,64]{0,2,1:T(8,128)}, f32[2048,4,64]{0,2,1:T(8,128)}, f32[32,4,64]{2,0,1:T(8,128)S(1)}, f32[32,4,64]{2,0,1:T(8,128)S(1)}...) while((s32[]{:T(128)}, f32[2048,4,64]{0,2,1:T(8,128)}, ...), condition=%wide.region_78.81_spmd.clone, body=%wide.region_75.80_spmd.clone.sunk | while | flops 2089738240 | bytes 188961584 | solution.py:209
  2687.2 85.2 %reduce-scatter.31.cloned.1.call-done = f32[512,1024]{1,0:T(8,128)} async-done(((f32[2048,1024]{1,0:T(8,128)}), f32[512,1024]{1,0:T(8,128)}) %reduce-scatter.31.cloned.1.call-update) | async-done | bytes 2097168 | tf_op jit(solution)/shard_map/reduce_scatter | solution.py:402
  2785.9 52.8 %all-gather.32.cloned.1.call-done = bf16[2048,1024]{1,0:T(8,128)(2,1)} async-done(((bf16[512,1024]{1,0:T(8,128)(2,1)}), bf16[2048,1024]{1,0:T(8,128)(2,1)}) %all-gather.32.cloned.1.call-update) | async-done | bytes 4194320 | tf_op jit(solution)/shard_map/all_gather | solution.py:371
  3039.8 344.6 %while.116 = (s32[]{:T(128)}, f32[2048,4,64]{0,2,1:T(8,128)}, f32[2048,4,64]{0,2,1:T(8,128)}, f32[32,4,64]{2,0,1:T(8,128)S(1)}, f32[32,4,64]{2,0,1:T(8,128)S(1)}...) while((s32[]{:T(128)}, f32[2048,4,64]{0,2,1:T(8,128)}, ...), condition=%wide.region_96.99_spmd.clone, body=%wide.region_93.98_spmd.clone.sunk | while | flops 2089738240 | bytes 188961584 | solution.py:209
  3526.8 81.0 %all-reduce = (f32[1,2,1024]{2,1,0:T(2,128)}, f32[1,2,1024]{2,1,0:T(2,128)}) all-reduce(f32[1,2,1024]{2,1,0:T(2,128)S(1)} %fusion.393, f32[1,2,1024]{2,1,0:T(2,128)S(1)} %fusion.396), channel_id=1, replica_groups=mesh['section'=2,'dp'=4,'tensor'=4] {'dp','tensor'}, use_global_device_ids=true, to_apply=%region_112.115 | all-reduce | flops 4096 | bytes 32768 | tf_op jit(solution)/shard_map/psum | solution.py:441
  3607.8 390.2 %all-reduce.4.cloned.1.call-done = (f32[1,1024,6,256]{1,3,2,0:T(8,128)}, f32[1,256,1024]{2,1,0:T(8,128)}, f32[1,1024,1024]{2,1,0:T(8,128)}, f32[1,1024,1024]{2,1,0:T(8,128)}) async-done(((f32[1,1024,6,256]{1,3,2,0:T(8,128)}, f32[1,256,1024]{2,1,0:T(8,128)}, f32[1,1024,1024]{2,1,0:T(8,128)}, f32[1,1024,1024]{2,1,0:T(8,128)}), (f32[1,1024,6,256]{1,3,2,0:T(8,128)}, f32[1,256,1024]{2,1,0:T(8,128)}, ...) | async-done | bytes 15728656 | tf_op jit(solution)/shard_map/psum | solution.py:440
  4004.6 82.0 %reduce-scatter.35.cloned.1.call-done = f32[512,1024]{1,0:T(8,128)} async-done(((f32[2048,1024]{1,0:T(8,128)}), f32[512,1024]{1,0:T(8,128)}) %reduce-scatter.35.cloned.1.call-update) | async-done | bytes 2097168 | tf_op jit(solution)/shard_map/reduce_scatter | solution.py:402
  (1494 shorter events, 2428.1 us)
Async XLA Ops:
  9.7 292.6 %reduce-scatter.13.cloned.1.call-start = ((), (), s32[]{:S(2)}) async-start(), calls=%async_computation.12 | async-start | bytes 10485760 | tf_op jit(solution)/shard_map/reduce_scatter | solution.py:289
  215.8 144.4 %all-gather.14.cloned.1.call-start = ((), (), s32[]{:S(2)}) async-start(), calls=%async_computation.13 | async-start | bytes 5242880 | tf_op jit(solution)/shard_map/all_gather | solution.py:298
  307.3 172.7 %reduce-scatter.15.cloned.1.call-start = ((), (), s32[]{:S(2)}) async-start(), calls=%async_computation.14 | async-start | bytes 10485760 | tf_op jit(solution)/shard_map/reduce_scatter | solution.py:303
  393.4 149.5 %all-gather.16.cloned.1.call-start = ((), (), s32[]{:S(2)}) async-start(), calls=%async_computation.15 | async-start | bytes 5242880 | tf_op jit(solution)/shard_map/all_gather | solution.py:281
  490.1 292.0 %reduce-scatter.17.cloned.1.call-start = ((), (), s32[]{:S(2)}) async-start(), calls=%async_computation.16 | async-start | bytes 10485760 | tf_op jit(solution)/shard_map/reduce_scatter | solution.py:289
  695.5 151.2 %all-gather.18.cloned.1.call-start = ((), (), s32[]{:S(2)}) async-start(), calls=%async_computation.17 | async-start | bytes 5242880 | tf_op jit(solution)/shard_map/all_gather | solution.py:298
  793.9 172.8 %reduce-scatter.19.cloned.1.call-start = ((), (), s32[]{:S(2)}) async-start(), calls=%async_computation.18 | async-start | bytes 10485760 | tf_op jit(solution)/shard_map/reduce_scatter | solution.py:303
  880.1 149.5 %all-gather.24.cloned.1.call-start = ((), (), s32[]{:S(2)}) async-start(), calls=%async_computation.23 | async-start | bytes 5242880 | tf_op jit(solution)/shard_map/all_gather | solution.py:371
  976.9 107.8 %all-gather.20.cloned.1.call-start = ((), (), s32[]{:S(2)}) async-start(), calls=%async_computation.19 | async-start | bytes 5242880 | tf_op jit(solution)/shard_map/all_gather | solution.py:281
  990.7 257.9 %reduce-scatter.25.cloned.1.call-start = ((), (), s32[]{:S(2)}) async-start(), calls=%async_computation.24 | async-start | bytes 10485760 | tf_op jit(solution)/shard_map/reduce_scatter | solution.py:378
  1065.0 267.8 %reduce-scatter.21.cloned.1.call-start = ((), (), s32[]{:S(2)}) async-start(), calls=%async_computation.20 | async-start | bytes 10485760 | tf_op jit(solution)/shard_map/reduce_scatter | solution.py:289
  1246.1 156.6 %all-gather.26.cloned.1.call-start = ((), (), s32[]{:S(2)}) async-start(), calls=%async_computation.25 | async-start | bytes 5242880 | tf_op jit(solution)/shard_map/all_gather | solution.py:388
  1349.8 476.7 %all-gather.22.cloned.1.call-start = ((), (), s32[]{:S(2)}) async-start(), calls=%async_computation.21 | async-start | bytes 5242880 | tf_op jit(solution)/shard_map/all_gather | solution.py:298
  1377.3 535.6 %reduce-scatter.27.cloned.1.call-start = ((), (), s32[]{:S(2)}) async-start(), calls=%async_computation.26 | async-start | bytes 10485760 | tf_op jit(solution)/shard_map/reduce_scatter | solution.py:402
  1826.4 176.2 %reduce-scatter.23.cloned.1.call-start = ((), (), s32[]{:S(2)}) async-start(), calls=%async_computation.22 | async-start | bytes 10485760 | tf_op jit(solution)/shard_map/reduce_scatter | solution.py:303
  1860.1 213.2 %all-gather.28.cloned.1.call-start = ((), (), s32[]{:S(2)}) async-start(), calls=%async_computation.27 | async-start | bytes 5242880 | tf_op jit(solution)/shard_map/all_gather | solution.py:371
  2020.4 175.1 %reduce-scatter.29.cloned.1.call-start = ((), (), s32[]{:S(2)}) async-start(), calls=%async_computation.28 | async-start | bytes 10485760 | tf_op jit(solution)/shard_map/reduce_scatter | solution.py:378
  2108.9 147.2 %all-gather.30.cloned.1.call-start = ((), (), s32[]{:S(2)}) async-start(), calls=%async_computation.29 | async-start | bytes 5242880 | tf_op jit(solution)/shard_map/all_gather | solution.py:388
  2203.3 569.1 %reduce-scatter.31.cloned.1.call-start = ((), (), s32[]{:S(2)}) async-start(), calls=%async_computation.30 | async-start | bytes 10485760 | tf_op jit(solution)/shard_map/reduce_scatter | solution.py:402
  2685.8 152.9 %all-gather.32.cloned.1.call-start = ((), (), s32[]{:S(2)}) async-start(), calls=%async_computation.31 | async-start | bytes 5242880 | tf_op jit(solution)/shard_map/all_gather | solution.py:371
  2785.8 175.1 %reduce-scatter.33.cloned.1.call-start = ((), (), s32[]{:S(2)}) async-start(), calls=%async_computation.32 | async-start | bytes 10485760 | tf_op jit(solution)/shard_map/reduce_scatter | solution.py:378
  2874.3 147.2 %all-gather.34.cloned.1.call-start = ((), (), s32[]{:S(2)}) async-start(), calls=%async_computation.33 | async-start | bytes 5242880 | tf_op jit(solution)/shard_map/all_gather | solution.py:388
  2968.7 1029.3 %all-reduce.4.cloned.1.call-start = ((), (), s32[]{:S(2)}) async-start(), calls=%async_computation.36 | async-start | bytes 31457280 | tf_op jit(solution)/shard_map/psum | solution.py:440
  3466.3 620.3 %reduce-scatter.35.cloned.1.call-start = ((), (), s32[]{:S(2)}) async-start(), calls=%async_computation.34 | async-start | bytes 10485760 | tf_op jit(solution)/shard_map/reduce_scatter | solution.py:402
  (282 other events, 5963.2 us)
Sparse Core Ops, SparseCore 0:
  10.5 55.3 all-gather.35
  215.9 86.4 reduce-scatter.12
  307.4 52.6 all-gather.13
  393.5 86.4 reduce-scatter.14
  490.2 52.6 all-gather.15
  695.6 86.4 reduce-scatter.16
  794.0 52.6 all-gather.17
  880.3 86.4 reduce-scatter.18
  977.0 52.6 all-gather.23
  1031.9 52.6 all-gather.19
  1087.8 86.4 reduce-scatter.24
  1246.2 86.5 reduce-scatter.20
  1349.9 52.6 all-gather.25
  1405.0 52.6 all-gather.21
  1826.5 86.3 reduce-scatter.26
  1916.1 86.4 reduce-scatter.22
  2020.5 52.6 all-gather.27
  2109.1 86.4 reduce-scatter.28
  2203.4 52.6 all-gather.29
  2685.9 86.4 reduce-scatter.30
  2874.5 86.4 reduce-scatter.32
  2968.8 52.6 all-gather.33
  3466.4 531.5 all-reduce.3
  4001.4 85.2 reduce-scatter.34
  (1 shorter events, 52.6 us)
where the time goes:
time: 4140 us; the launch traced here: 4100 us
  waiting for transfers between devices  1660 us (40%)
  matrix products  1090 us (26%)
  local copies, waits for them, and re-layouts  817 us (20%)
  other arithmetic  359 us (9%)
  blocking collectives  92.9 us (2%)
  loops' own time  66.5 us (2%)
    psum x1, waiting for transfers between devices, shards(): summed = lax.psum((acc_attn, acc_out, acc_up, acc_down), 'dp')  390 us
    reduce_scatter x3, waiting for transfers between devices, shards(): lax.psum_scatter(jnp.dot(layer_activated, down_matrix, preferred_element_...  258 us
    reduce_scatter x3, waiting for transfers between devices, shards(): lax.psum_scatter(jnp.dot(layer_context, out_matrix, preferred_element_typ...  251 us
    reduce_scatter x3, waiting for transfers between devices, shards(): lax.psum_scatter(times_transposed(grad_proj, attn_matrix), 'tensor', scat...  220 us
    dot_general x24, matrix products, band_scores(): jnp.einsum('qhe,khe->hqk', query, band_keys, preferred_element_type=jnp.f...  164 us
    dot_general x12, matrix products, times_transposed(): lax.dot_general(left, right, (((1,), (1,)), ((), ())), preferred_element_...  146 us
    all_gather x3, waiting for transfers between devices, shards(): grad_mlp_rows = lax.all_gather(grad_mlp, 'tensor', axis=0, tiled=True)  144 us
    dot_general x12, matrix products, one_block(): jnp.einsum('qhe,khe->hqk', grad_out, band_vals, preferred_element_type=jn...  142 us
  transfers between devices with their start and end apart: 29, of which 26 were waited for; matrix products, arithmetic and copies ran while one was open for 22% of the time, Pallas kernels for 0%

commit v1 on v0

v1 whole, which is shorter than its diff:
```python
import math
from functools import partial

import jax
import jax.numpy as jnp
from jax import lax
from jax.experimental import pallas as pl
from jax.experimental.pallas import tpu as pltpu
from jax.sharding import PartitionSpec as P

HEAD = 64
HALF = 512
QTILE = 256
KTILE = 256
VMEM_BYTES = 56 * 1024 * 1024

masked_fill = -1e30
clip_limit = 10.0
score_scale = HEAD ** (-0.5)

NN = (((1,), (0,)), ((), ()))
NT = (((1,), (1,)), ((), ()))
TN = (((0,), (0,)), ((), ()))


def mm(left, right, dims=NN, out=jnp.float32):
    return lax.dot_general(left, right, dims, preferred_element_type=jnp.float32).astype(out)


def tile_bias(first_key, first_query, key_docs, query_docs, keys, queries):
    key_pos = first_key + lax.broadcasted_iota(jnp.int32, (keys, queries), 0)
    query_pos = first_query + lax.broadcasted_iota(jnp.int32, (keys, queries), 1)
    gap = jnp.abs(key_pos - query_pos)
    return jnp.where((key_docs == query_docs) & (gap <= HALF), 0.0, masked_fill)


def far_bias(glob_pos, first_query, glob_docs, query_docs, globs, queries):
    query_pos = first_query + lax.broadcasted_iota(jnp.int32, (globs, queries), 1)
    gap = jnp.abs(glob_pos - query_pos)
    return jnp.where((glob_docs == query_docs) & (gap > HALF), 0.0, masked_fill)


def one_hot_rows(glob_pos, length):
    globs = glob_pos.shape[0]
    hit = lax.broadcasted_iota(jnp.int32, (globs, length), 1) == glob_pos
    return jnp.where(hit, 1.0, 0.0).astype(jnp.bfloat16)


def true_unit(place, order_ref, plan):
    inner, parts, _ = plan
    part, rest = place // (2 * inner), place % (2 * inner)
    side = (rest % 2) ^ order_ref[0]
    lane = (rest // 2) ^ order_ref[1]
    return (side * inner + lane) * parts + part


def local_unit(unit, order_ref, plan):
    inner, parts, _ = plan
    block, part = lax.div(unit, parts), lax.rem(unit, parts)
    side = lax.div(block, inner) ^ order_ref[0]
    lane = lax.rem(block, inner) ^ order_ref[1]
    return part * (2 * inner) + lane * 2 + side


def join_pieces(order_ref, pieces, joined_ref, sems, plan):
    rows = plan[2]
    copies = []
    place = 0
    for piece in pieces:
        for index in range(piece.shape[0] // rows):
            start = pl.multiple_of(true_unit(place, order_ref, plan) * rows, rows)
            copies.append(
                pltpu.make_async_copy(
                    piece.at[pl.ds(index * rows, rows), :],
                    joined_ref.at[pl.ds(start, rows), :],
                    sems.at[place],
                )
            )
            place += 1
    for copy in copies:
        copy.start()
    for copy in copies:
        copy.wait()


def store_local(out_ref, tile, cols, value, order_ref, plan):
    rows = plan[2]
    size = min(rows, value.shape[0])
    for index in range(value.shape[0] // size):
        row = tile * value.shape[0] + index * size
        place = local_unit(lax.div(row, rows), order_ref, plan)
        start = pl.multiple_of(place * rows + lax.rem(row, rows), size)
        out_ref[pl.ds(start, size), cols] = value[index * size : (index + 1) * size]


def diagonal_sum(blocks, heads, rows):
    owner = lax.broadcasted_iota(jnp.int32, (rows, heads * HEAD), 1) // HEAD
    total = jnp.zeros((rows, heads * HEAD), jnp.float32)
    for head in range(heads):
        total = total + jnp.where(owner == head, blocks[head * rows : (head + 1) * rows], 0.0)
    return total


def attend_kernel(
    heads,
    plan,
    count,
    order_ref,
    first_ref,
    last_ref,
    *refs,
):
    pieces, refs = refs[:count], refs[count:]
    attend_body(heads, plan, order_ref, first_ref, last_ref, pieces, *refs)


def attend_body(
    heads,
    plan,
    order_ref,
    first_ref,
    last_ref,
    pieces,
    doc_row_ref,
    doc_col_ref,
    pos_col_ref,
    gdoc_col_ref,
    gdoc_row_ref,
    ctx_ref,
    lse_ref,
    glse_ref,
    peak_ref,
    gpeak_ref,
    proj,
    values_t,
    hot,
    far_keys,
    far_values_t,
    gctx_t,
    gstack,
    gscores,
    wide,
    acc,
    top,
    total,
    sems,
):
    length = proj.shape[0]
    width = heads * HEAD
    globs = pos_col_ref.shape[0]
    step = pl.program_id(0)

    @pl.when(step == 0)
    def _():
        join_pieces(order_ref, pieces, proj, sems, plan)
        wide[...] = jnp.zeros_like(wide)
        gstack[...] = jnp.zeros_like(gstack)
        hot[...] = one_hot_rows(pos_col_ref[...], length)
        hot_all = hot[...]
        far_keys[...] = mm(hot_all, proj[:, width : 2 * width], out=jnp.bfloat16)
        far_values_t[...] = mm(hot_all, proj[:, 2 * width : 3 * width]).T.astype(jnp.bfloat16)
        queries = (mm(hot_all, proj[:, 3 * width : 4 * width]) * score_scale).astype(jnp.bfloat16)
        for head in range(heads):
            cols = slice(head * HEAD, (head + 1) * HEAD)
            gstack[head * globs : (head + 1) * globs, cols] = queries[:, cols]

        def score_tile(tile, best):
            rows = pl.ds(pl.multiple_of(tile * KTILE, KTILE), KTILE)
            values_t[:, rows] = proj[rows, 2 * width : 3 * width].T
            scores = mm(proj[rows, 4 * width : 5 * width], gstack[...], NT)
            scores = jnp.where(doc_col_ref[rows, :] == gdoc_row_ref[...], scores, masked_fill)
            gscores[rows, :] = scores
            return jnp.maximum(best, jnp.max(scores, 0, keepdims=True))

        best = lax.fori_loop(
            0, length // KTILE, score_tile, jnp.full((1, heads * globs), masked_fill, jnp.float32)
        )

        def sum_tile(tile, sums):
            rows = pl.ds(pl.multiple_of(tile * KTILE, KTILE), KTILE)
            weights = jnp.exp(gscores[rows, :] - best)
            gscores[rows, :] = weights
            return sums + jnp.sum(weights, 0, keepdims=True)

        sums = lax.fori_loop(
            0, length // KTILE, sum_tile, jnp.zeros((1, heads * globs), jnp.float32)
        )

        def value_tile(tile, blocks):
            rows = pl.ds(pl.multiple_of(tile * KTILE, KTILE), KTILE)
            probs = (gscores[rows, :] / sums).T.astype(jnp.bfloat16)
            return blocks + mm(probs, proj[rows, 5 * width : 6 * width])

        blocks = lax.fori_loop(
            0, length // KTILE, value_tile, jnp.zeros((heads * globs, width), jnp.float32)
        )
        gctx_t[...] = diagonal_sum(blocks, heads, globs).T.astype(jnp.bfloat16)
        glse_ref[...] = best + jnp.log(sums)
        gpeak_ref[...] = best

    start = pl.multiple_of(step * QTILE, QTILE)
    query_rows = pl.ds(start, QTILE)
    query_t = proj[query_rows, 0:width].T * score_scale
    for head in range(heads):
        rows = slice(head * HEAD, (head + 1) * HEAD)
        wide[rows, head * QTILE : (head + 1) * QTILE] = query_t[rows].astype(jnp.bfloat16)
    query_docs = doc_row_ref[:, query_rows]

    scores = mm(far_keys[...], wide[...])
    bias = far_bias(pos_col_ref[...], start, gdoc_col_ref[...], query_docs, globs, QTILE)
    for head in range(heads):
        cols = slice(head * QTILE, (head + 1) * QTILE)
        rows = slice(head * HEAD, (head + 1) * HEAD)
        part = scores[:, cols] + bias
        best = jnp.max(part, 0, keepdims=True)
        weights = jnp.exp(part - best)
        top[:, cols] = best
        total[:, cols] = jnp.sum(weights, 0, keepdims=True)
        acc[rows, :] = mm(far_values_t[rows, :], weights.astype(jnp.bfloat16))

    def key_tile(tile, carry):
        key_start = pl.multiple_of(tile * KTILE, KTILE)
        keys = pl.ds(key_start, KTILE)
        scores = mm(proj[keys, width : 2 * width], wide[...])
        bias = tile_bias(key_start, start, doc_col_ref[keys, :], query_docs, KTILE, QTILE)
        for head in range(heads):
            cols = slice(head * QTILE, (head + 1) * QTILE)
            rows = slice(head * HEAD, (head + 1) * HEAD)
            part = scores[:, cols] + bias
            old = top[:, cols]
            best = jnp.maximum(old, jnp.max(part, 0, keepdims=True))
            weights = jnp.exp(part - best)
            shrink = jnp.exp(old - best)
            top[:, cols] = best
            total[:, cols] = total[:, cols] * shrink + jnp.sum(weights, 0, keepdims=True)
            acc[rows, :] = acc[rows, :] * shrink + mm(
                values_t[rows, keys], weights.astype(jnp.bfloat16)
            )
        return carry

    lax.fori_loop(first_ref[step], last_ref[step], key_tile, 0)

    hot_tile = hot[:, query_rows]
    is_glob = jnp.max(hot_tile.astype(jnp.float32), 0, keepdims=True) > 0.5
    for head in range(heads):
        cols = slice(head * QTILE, (head + 1) * QTILE)
        rows = slice(head * HEAD, (head + 1) * HEAD)
        acc[rows, :] = acc[rows, :] / total[:, cols]
        lse_ref[head : head + 1, :] = top[:, cols] + jnp.log(total[:, cols])
    merged = jnp.where(is_glob, mm(gctx_t[...], hot_tile), acc[...])
    store_local(ctx_ref, step, slice(None), merged.T.astype(jnp.bfloat16), order_ref, plan)

    @pl.when(step == 0)
    def _():
        peak_ref[...] = top[...]

    @pl.when(step > 0)
    def _():
        peak_ref[...] = jnp.maximum(peak_ref[...], top[...])


def whole_block(shape):
    return pl.BlockSpec(shape, lambda *_: (0,) * len(shape), pipeline_mode=pl.Buffered(1))


def attend(proj, info, plan):
    length = sum(piece.shape[0] for piece in proj)
    columns = proj[0].shape[1]
    heads = columns // (6 * HEAD)
    width = heads * HEAD
    order, first, last, doc_row, doc_col, pos_col, gdoc_col, gdoc_row, _ = info
    globs = pos_col.shape[0]
    tiles = length // QTILE
    bf16, f32 = jnp.bfloat16, jnp.float32

    anywhere = pl.BlockSpec(memory_space=pl.ANY)
    return pl.pallas_call(
        partial(attend_kernel, heads, plan, len(proj)),
        out_shape=(
            jax.ShapeDtypeStruct((length, width), bf16),
            jax.ShapeDtypeStruct((heads, length), f32),
            jax.ShapeDtypeStruct((1, heads * globs), f32),
            jax.ShapeDtypeStruct((1, heads * QTILE), f32),
            jax.ShapeDtypeStruct((1, heads * globs), f32),
        ),
        grid_spec=pltpu.PrefetchScalarGridSpec(
            num_scalar_prefetch=3,
            grid=(tiles,),
            in_specs=[anywhere] * len(proj) + [
                whole_block((1, length)),
                whole_block((length, 1)),
                whole_block((globs, 1)),
                whole_block((globs, 1)),
                whole_block((1, heads * globs)),
            ],
            out_specs=(
                whole_block((length, width)),
                pl.BlockSpec((heads, QTILE), lambda step, *_: (0, step)),
                pl.BlockSpec((1, heads * globs), lambda *_: (0, 0)),
                pl.BlockSpec((1, heads * QTILE), lambda *_: (0, 0)),
                pl.BlockSpec((1, heads * globs), lambda *_: (0, 0)),
            ),
            scratch_shapes=[
                pltpu.VMEM((length, columns), bf16),
                pltpu.VMEM((width, length), bf16),
                pltpu.VMEM((globs, length), bf16),
                pltpu.VMEM((globs, width), bf16),
                pltpu.VMEM((width, globs), bf16),
                pltpu.VMEM((width, globs), bf16),
                pltpu.VMEM((heads * globs, width), bf16),
                pltpu.VMEM((length, heads * globs), f32),
                pltpu.VMEM((width, heads * QTILE), bf16),
                pltpu.VMEM((width, QTILE), f32),
                pltpu.VMEM((1, heads * QTILE), f32),
                pltpu.VMEM((1, heads * QTILE), f32),
                pltpu.SemaphoreType.DMA((length // plan[2],)),
            ],
        ),
        compiler_params=pltpu.CompilerParams(
            dimension_semantics=("arbitrary",), vmem_limit_bytes=VMEM_BYTES
        ),
        cost_estimate=pl.CostEstimate(
            flops=20 * length * 1024 * width, bytes_accessed=14 * length * width,
            transcendentals=length * 1024 * heads,
        ),
        name="attend",
    )(order, first, last, *proj, doc_row, doc_col, pos_col, gdoc_col, gdoc_row)


def attend_back_kernel(
    heads,
    plan,
    counts,
    order_ref,
    first_ref,
    last_ref,
    *refs,
):
    pieces, refs = refs[: counts[0]], refs[counts[0] :]
    grad_pieces, refs = refs[: counts[1]], refs[counts[1] :]
    attend_back_body(heads, plan, order_ref, first_ref, last_ref, pieces, grad_pieces, *refs)


def attend_back_body(
    heads,
    plan,
    order_ref,
    first_ref,
    last_ref,
    pieces,
    grad_pieces,
    ctx_piece_ref,
    lse_ref,
    glse_ref,
    doc_row_ref,
    doc_col_ref,
    pos_col_ref,
    gdoc_col_ref,
    gdoc_row_ref,
    plain_col_ref,
    out_ref,
    proj,
    ctx,
    grad,
    keys_t,
    hot,
    far_keys,
    far_keys_t,
    far_values,
    far_key_grad,
    far_value_grad,
    key_grad,
    value_grad,
    gquery,
    gout,
    gquery_grad,
    wide,
    wide_grad,
    stack,
    stack_grad,
    probs_low,
    grads_low,
    query_grad_t,
    proj_sems,
    ctx_sems,
    grad_sems,
):
    length = proj.shape[0]
    width = heads * HEAD
    globs = pos_col_ref.shape[0]
    tiles = length // KTILE
    step = pl.program_id(0)
    bf16 = jnp.bfloat16

    def store(tile, block, value):
        cols = slice(block * width, (block + 1) * width)
        store_local(out_ref, tile, cols, value.astype(bf16), order_ref, plan)

    @pl.when(step == 0)
    def _():
        join_pieces(order_ref, pieces, proj, proj_sems, plan)
        join_pieces(order_ref, [ctx_piece_ref], ctx, ctx_sems, plan)
        join_pieces(order_ref, grad_pieces, grad, grad_sems, plan)
        for ref in (wide, wide_grad, stack, stack_grad, gquery, gout):
            ref[...] = jnp.zeros_like(ref)
        for ref in (key_grad, value_grad, far_key_grad, far_value_grad):
            ref[...] = jnp.zeros_like(ref)
        gquery_grad[...] = jnp.zeros_like(gquery_grad)
        hot[...] = one_hot_rows(pos_col_ref[...], length)
        hot_all = hot[...]
        near = mm(hot_all, proj[:, width : 2 * width])
        far_keys[...] = near.astype(bf16)
        far_keys_t[...] = near.T.astype(bf16)
        far_values[...] = mm(hot_all, proj[:, 2 * width : 3 * width], out=bf16)
        queries = (mm(hot_all, proj[:, 3 * width : 4 * width]) * score_scale).astype(bf16)
        out_grad = mm(hot_all, grad[...])
        glob_ctx = mm(hot_all, ctx[...])
        product = out_grad * glob_ctx
        owner = lax.broadcasted_iota(jnp.int32, (globs, width), 1) // HEAD
        dots = []
        for head in range(heads):
            cols = slice(head * HEAD, (head + 1) * HEAD)
            rows = slice(head * globs, (head + 1) * globs)
            gquery[rows, cols] = queries[:, cols]
            gout[rows, cols] = out_grad[:, cols].astype(bf16)
            own = jnp.where(owner == head, product, 0.0)
            dots.append(jnp.sum(own, 1, keepdims=True))
        dot_row = jnp.broadcast_to(jnp.concatenate(dots, 0), (heads * globs, 128)).T[0:1]

        def glob_tile(tile, carry):
            rows = pl.ds(pl.multiple_of(tile * KTILE, KTILE), KTILE)
            keys_t[:, rows] = proj[rows, width : 2 * width].T
            scores = mm(proj[rows, 4 * width : 5 * width], gquery[...], NT)
            scores = jnp.where(doc_col_ref[rows, :] == gdoc_row_ref[...], scores, masked_fill)
            probs = jnp.exp(scores - glse_ref[...])
            grad_p = mm(proj[rows, 5 * width : 6 * width], gout[...], NT)
            grad_s = probs * (grad_p - dot_row)
            store(tile, 5, mm(probs.astype(bf16), gout[...]))
            store(tile, 4, mm(grad_s.astype(bf16), gquery[...]))
            gquery_grad[...] += mm(grad_s.T.astype(bf16), proj[rows, 4 * width : 5 * width])
            return carry

        lax.fori_loop(0, tiles, glob_tile, 0)
        query_grad = diagonal_sum(gquery_grad[...], heads, globs) * score_scale
        query_grad = query_grad.astype(bf16)

        def spread_tile(tile, carry):
            rows = pl.ds(pl.multiple_of(tile * KTILE, KTILE), KTILE)
            store(tile, 3, mm(hot[:, rows], query_grad, TN))
            return carry

        lax.fori_loop(0, tiles, spread_tile, 0)

    start = pl.multiple_of(step * QTILE, QTILE)
    query_rows = pl.ds(start, QTILE)
    query = proj[query_rows, 0:width].astype(jnp.float32) * score_scale
    query_t = query.T.astype(bf16)
    query = query.astype(bf16)
    grad_out = grad[query_rows, :].astype(jnp.float32) * plain_col_ref[query_rows, :]
    grad_out_t = grad_out.T
    product_t = grad_out_t * ctx[query_rows, :].astype(jnp.float32).T
    grad_out = grad_out.astype(bf16)
    grad_out_t = grad_out_t.astype(bf16)
    dots = []
    for head in range(heads):
        own = slice(head * HEAD, (head + 1) * HEAD)
        cols = slice(head * QTILE, (head + 1) * QTILE)
        wide[own, cols] = query_t[own]
        wide_grad[own, cols] = grad_out_t[own]
        stack[cols, own] = query[:, own]
        stack_grad[cols, own] = grad_out[:, own]
        dots.append(jnp.sum(product_t[own], 0, keepdims=True))
    query_docs = doc_row_ref[:, query_rows]

    def parts(scores, grad_p, bias, head):
        cols = slice(head * QTILE, (head + 1) * QTILE)
        shift = lse_ref[head : head + 1, query_rows]
        probs = jnp.exp(scores[:, cols] + bias - shift)
        grad_s = probs * (grad_p[:, cols] - dots[head])
        return probs.astype(bf16), grad_s.astype(bf16)

    scores = mm(far_keys[...], wide[...])
    grad_p = mm(far_values[...], wide_grad[...])
    bias = far_bias(pos_col_ref[...], start, gdoc_col_ref[...], query_docs, globs, QTILE)
    for head in range(heads):
        cols = slice(head * QTILE, (head + 1) * QTILE)
        own = slice(head * HEAD, (head + 1) * HEAD)
        probs, grad_s = parts(scores, grad_p, bias, head)
        probs_low[0:globs, cols] = probs
        grads_low[0:globs, cols] = grad_s
        query_grad_t[own, :] = mm(far_keys_t[own, :], grad_s)
    far_value_grad[...] += mm(probs_low[0:globs, :], stack_grad[...])
    far_key_grad[...] += mm(grads_low[0:globs, :], stack[...])

    def key_tile(tile, carry):
        key_start = pl.multiple_of(tile * KTILE, KTILE)
        keys = pl.ds(key_start, KTILE)
        scores = mm(proj[keys, width : 2 * width], wide[...])
        grad_p = mm(proj[keys, 2 * width : 3 * width], wide_grad[...])
        bias = tile_bias(key_start, start, doc_col_ref[keys, :], query_docs, KTILE, QTILE)
        for head in range(heads):
            cols = slice(head * QTILE, (head + 1) * QTILE)
            own = slice(head * HEAD, (head + 1) * HEAD)
            probs, grad_s = parts(scores, grad_p, bias, head)
            probs_low[:, cols] = probs
            grads_low[:, cols] = grad_s
            query_grad_t[own, :] += mm(keys_t[own, keys], grad_s)
        value_grad[keys, :] += mm(probs_low[...], stack_grad[...])
        key_grad[keys, :] += mm(grads_low[...], stack[...])
        return carry

    lax.fori_loop(first_ref[step], last_ref[step], key_tile, 0)
    store(step, 0, (query_grad_t[...] * score_scale).T)

    @pl.when(step == pl.num_programs(0) - 1)
    def _():
        far_key = far_key_grad[...].astype(bf16)
        far_value = far_value_grad[...].astype(bf16)

        def close_tile(tile, carry):
            rows = pl.ds(pl.multiple_of(tile * KTILE, KTILE), KTILE)
            hot_tile = hot[:, rows]
            key_sum = key_grad[rows, :] + mm(hot_tile, far_key, TN)
            value_sum = value_grad[rows, :] + mm(hot_tile, far_value, TN)
            store(tile, 1, key_sum)
            store(tile, 2, value_sum)
            return carry

        lax.fori_loop(0, tiles, close_tile, 0)


def attend_back(proj, context, log_sums, grad_context, info, plan):
    length = context.shape[0]
    columns = proj[0].shape[1]
    heads = columns // (6 * HEAD)
    width = heads * HEAD
    order, first, last, doc_row, doc_col, pos_col, gdoc_col, gdoc_row, plain_col = info
    globs = pos_col.shape[0]
    tiles = length // QTILE
    bf16, f32 = jnp.bfloat16, jnp.float32
    wide = heads * QTILE
    anywhere = pl.BlockSpec(memory_space=pl.ANY)
    return pl.pallas_call(
        partial(attend_back_kernel, heads, plan, (len(proj), len(grad_context))),
        out_shape=jax.ShapeDtypeStruct((length, columns), bf16),
        grid_spec=pltpu.PrefetchScalarGridSpec(
            num_scalar_prefetch=3,
            grid=(tiles,),
            in_specs=[anywhere] * (len(proj) + len(grad_context) + 1) + [
                whole_block((heads, length)),
                whole_block((1, heads * globs)),
                whole_block((1, length)),
                whole_block((length, 1)),
                whole_block((globs, 1)),
                whole_block((globs, 1)),
                whole_block((1, heads * globs)),
                whole_block((length, 1)),
            ],
            out_specs=whole_block((length, columns)),
            scratch_shapes=[
                pltpu.VMEM((length, columns), bf16),
                pltpu.VMEM((length, width), bf16),
                pltpu.VMEM((length, width), bf16),
                pltpu.VMEM((width, length), bf16),
                pltpu.VMEM((globs, length), bf16),
                pltpu.VMEM((globs, width), bf16),
                pltpu.VMEM((width, globs), bf16),
                pltpu.VMEM((globs, width), bf16),
                pltpu.VMEM((globs, width), f32),
                pltpu.VMEM((globs, width), f32),
                pltpu.VMEM((length, width), f32),
                pltpu.VMEM((length, width), f32),
                pltpu.VMEM((heads * globs, width), bf16),
                pltpu.VMEM((heads * globs, width), bf16),
                pltpu.VMEM((heads * globs, width), f32),
                pltpu.VMEM((width, wide), bf16),
                pltpu.VMEM((width, wide), bf16),
                pltpu.VMEM((wide, width), bf16),
                pltpu.VMEM((wide, width), bf16),
                pltpu.VMEM((KTILE, wide), bf16),
                pltpu.VMEM((KTILE, wide), bf16),
                pltpu.VMEM((width, QTILE), f32),
                pltpu.SemaphoreType.DMA((length // plan[2],)),
                pltpu.SemaphoreType.DMA((length // plan[2],)),
                pltpu.SemaphoreType.DMA((length // plan[2],)),
            ],
        ),
        compiler_params=pltpu.CompilerParams(
            dimension_semantics=("arbitrary",), vmem_limit_bytes=VMEM_BYTES
        ),
        cost_estimate=pl.CostEstimate(
            flops=60 * length * 1024 * width, bytes_accessed=28 * length * width,
            transcendentals=length * 1024 * heads,
        ),
        name="attend_back",
    )(
        order, first, last, *proj, *grad_context, context, *log_sums,
        doc_row, doc_col, pos_col, gdoc_col, gdoc_row, plain_col,
    )


def sequence_info(docs_row, glob_pos, order, heads):
    length = docs_row.shape[0]
    tiles = length // QTILE
    firsts = jnp.arange(tiles, dtype=jnp.int32) * QTILE
    tile_docs = docs_row.reshape(tiles, QTILE)
    doc_start = jnp.sum(docs_row[None, :] < tile_docs[:, :1], 1, dtype=jnp.int32)
    doc_end = jnp.sum(docs_row[None, :] <= tile_docs[:, -1:], 1, dtype=jnp.int32)
    first = jnp.maximum(firsts - HALF, doc_start) // KTILE
    last = (jnp.minimum(firsts + QTILE + HALF, doc_end) + KTILE - 1) // KTILE
    hit = glob_pos[:, None] == jnp.arange(length, dtype=jnp.int32)[None, :]
    glob_docs = jnp.sum(jnp.where(hit, docs_row[None, :], 0), 1, dtype=jnp.int32)
    plain_col = jnp.where(jnp.any(hit, 0), 0.0, 1.0)[:, None]
    return (
        order,
        first,
        last,
        docs_row[None, :],
        docs_row[:, None],
        glob_pos[:, None],
        glob_docs[:, None],
        jnp.tile(glob_docs, heads)[None, :],
        plain_col.astype(jnp.float32),
    )


def norm_forward(resid, gain, shift):
    centred = resid - jnp.mean(resid, -1, keepdims=True)
    scale = lax.rsqrt(jnp.mean(centred * centred, -1, keepdims=True) + 1e-05)
    normed = centred * scale
    return normed * gain + shift, normed, scale


def norm_backward(grad, normed, scale, gain):
    weighted = grad * gain
    mean_one = jnp.mean(weighted, -1, keepdims=True)
    mean_two = jnp.mean(weighted * normed, -1, keepdims=True)
    grad_in = (weighted - mean_one - normed * mean_two) * scale
    return grad_in, jnp.stack([jnp.sum(grad * normed, 0), jnp.sum(grad, 0)])


def gelu_pair(up):
    cdf = 0.5 * (1.0 + lax.erf(up * (0.5**0.5)))
    slope = cdf + up * (jnp.exp(-0.5 * up * up) * (1.0 / math.sqrt(2.0 * math.pi)))
    return (up * cdf).astype(jnp.bfloat16), slope.astype(jnp.bfloat16)


def after(value, *others):
    return lax.optimization_barrier((value,) + others)[0]


def shards(tokens, cotangent, doc_ids, global_flags, w_attn, w_out, w_up, w_down, ln_gain, ln_bias):
    bf16, f32 = jnp.bfloat16, jnp.float32
    sections = lax.axis_size("section")
    slots = lax.axis_size("tensor")
    copies = lax.axis_size("dp")
    micro = tokens.shape[0]
    inner = slots // micro
    section = lax.axis_index("section")
    slot = lax.axis_index("tensor")
    row = slot // inner
    lane = slot % inner
    width = tokens.shape[3]
    chunk = tokens.shape[2]
    rows = min(QTILE, chunk)
    parts = chunk // rows
    plan = (inner, parts, rows)
    crossed = inner == 2
    joint = ("section", "tensor")
    groups = [[a * inner + b for b in range(inner)] for a in range(micro)]

    def device(s, a, b):
        return s * slots + a * inner + b

    def route(value, link):
        pairs = []
        for s in range(sections):
            for a in range(micro):
                for b in range(inner):
                    target = link(s, a, b)
                    if target is not None and target != (s, a, b):
                        pairs.append((device(s, a, b), device(*target)))
        return lax.ppermute(value, joint, pairs)

    def other_core(value):
        return lax.ppermute(value, "section", [(0, 1), (1, 0)])

    def other_row(value):
        return route(value, lambda s, a, b: (s, 1 - a, b))

    def other_lane(value):
        return route(value, lambda s, a, b: (s, a, 1 - b))

    class ByLane:
        home = section == row
        swap = staticmethod(other_lane)

        @staticmethod
        def keeper(s, a, b):
            return a

        @staticmethod
        def across(s, a, b):
            return (s, 1 - a, b)

    class ByRow:
        home = section == lane
        swap = staticmethod(other_row)

        @staticmethod
        def keeper(s, a, b):
            return b

        @staticmethod
        def across(s, a, b):
            return (s, a, 1 - b)

    split_attn = ByLane
    split_mlp = ByRow if crossed else ByLane

    def gather(own, split, hop=None):
        near = jnp.concatenate([own, other_core(own)], 0)
        if not crossed:
            if inner == 1:
                return [near]
            return [lax.all_gather(near, "tensor", axis=0, tiled=True, axis_index_groups=groups)]
        if hop is None:
            hop = split.swap(own)
        return [near, jnp.concatenate([hop, other_core(hop)], 0)]

    def scatter(partials, split):
        if not crossed:
            blocks = partials[0].reshape(inner, 2, rows, -1)
            ours, theirs = blocks[:, 0], blocks[:, 1].astype(bf16)
            total = (ours + other_core(theirs).astype(f32)).reshape(inner * rows, -1)
            if inner == 1:
                return total
            return lax.psum_scatter(
                total.astype(bf16), "tensor", scatter_dimension=0, tiled=True,
                axis_index_groups=groups,
            ).astype(f32)
        near, far = partials
        leaving = far[:rows] + other_core(far[rows:].astype(bf16)).astype(f32)
        staying = near[:rows] + other_core(near[rows:].astype(bf16)).astype(f32)
        return staying + split.swap(leaving.astype(bf16)).astype(f32)

    def cut(array):
        per_part = 2 * inner * rows
        per_group = 2 * rows if crossed else per_part
        return [
            [array[p * per_part + g : p * per_part + g + per_group] for g in range(0, per_part, per_group)]
            for p in range(parts)
        ]

    def joined(pieces):
        return jnp.concatenate([piece for part in pieces for piece in part], 0)

    def flat(pieces):
        return [piece for part in pieces for piece in part]

    def part_rows(array):
        return [array[p * rows : (p + 1) * rows] for p in range(parts)]

    def own_rows(array):
        mine = lax.dynamic_index_in_dim(array[:, 0], row, 0, False)
        theirs = lax.dynamic_index_in_dim(array[:, 0], 1 - row, 0, False)
        moved = route(theirs, lambda s, a, b: (s, 1 - a, b) if s == a else None)
        return mine, moved

    def fetch(weight, layer, split):
        def across(s, a, b):
            if s != layer:
                return None
            _, a2, b2 = split.across(s, a, b)
            return (split.keeper(s, a, b), a2, b2)

        def within(s, a, b):
            return (split.keeper(s, a, b), a, b) if s == layer else None

        far = route(weight, across)
        near = route(weight, within)
        return jnp.where(split.home, jnp.where(section == layer, weight, near), far)

    mine, moved = own_rows(tokens)
    own = part_rows(jnp.where(ByLane.home, mine, moved))
    hops = [None] * parts
    if crossed:
        early = route(mine, lambda s, a, b: (s, a, 1 - b) if s == a else None)
        late = route(moved, lambda s, a, b: (s, a, 1 - b) if s != a else None)
        hops = part_rows(jnp.where(ByLane.home, early, late))
    attn_table = w_attn[0].reshape(width, -1)
    weights = [[None] * 4 for _ in range(sections)]
    weights[0][0] = fetch(after(attn_table, moved), 0, split_attn)
    weights[0][1] = fetch(after(w_out[0], weights[0][0]), 0, split_attn)
    weights[0][2] = fetch(after(w_up[0], hops[0]) if crossed else w_up[0], 0, split_mlp)
    weights[0][3] = fetch(after(w_down[0], weights[0][2]), 0, split_mlp)
    weights[1][0] = fetch(after(attn_table, weights[0][1]), 1, split_attn)
    weights[1][1] = fetch(after(w_out[0], weights[1][0]), 1, split_attn)

    heads = w_attn.shape[3] // HEAD
    docs = lax.dynamic_index_in_dim(doc_ids[:, 0], row, 0, False)
    flags = lax.dynamic_index_in_dim(global_flags[:, 0], row, 0, False)
    order = jnp.stack([section, lane if crossed else jnp.zeros_like(lane)]).astype(jnp.int32)
    info = sequence_info(docs, flags, order, heads)

    gains_own = jnp.stack([ln_gain[0], ln_bias[0]])
    gains_other = other_core(gains_own)
    norms = [jnp.where(section == layer, gains_own, gains_other) for layer in range(sections)]

    saved, outputs, peaks = [], [], []
    for layer in range(sections):
        gains, shifts = norms[layer]
        inputs = [gather(own[p], split_attn, hops[p] if layer == 0 else None) for p in range(parts)]
        proj = [[mm(piece, weights[layer][0], NN, bf16) for piece in part] for part in inputs]
        context, lse, glse, peak, gpeak = attend(flat(proj), info, plan)
        peaks.append(
            jnp.stack([jnp.max(peak.reshape(heads, -1), 1), jnp.max(gpeak.reshape(heads, -1), 1)])
        )
        context_parts = cut(context)
        attn_sums = [
            scatter([mm(piece, weights[layer][1]) for piece in part], split_attn)
            for part in context_parts
        ]
        if layer == 0:
            weights[1][2] = fetch(after(w_up[0], attn_sums[-1]), 1, split_mlp)
        hidden_rows, acts, slopes, norms_one, norms_two, outs = [], [], [], [], [], []
        for p in range(parts):
            hidden, normed, scale = norm_forward(
                own[p].astype(f32) + attn_sums[p], gains[0], shifts[0]
            )
            norms_one.append((normed, scale))
            hidden_rows.append(gather(hidden.astype(bf16), split_mlp))
            pairs = [gelu_pair(mm(piece, weights[layer][2])) for piece in hidden_rows[p]]
            acts.append([act for act, _ in pairs])
            slopes.append([slope for _, slope in pairs])
            mlp_sum = scatter([mm(act, weights[layer][3]) for act in acts[p]], split_mlp)
            out, normed, scale = norm_forward(hidden + mlp_sum, gains[1], shifts[1])
            norms_two.append((normed, scale))
            outs.append(out.astype(bf16))
        if layer == 0:
            weights[1][3] = fetch(after(w_down[0], weights[1][2], outs[-1]), 1, split_mlp)
        own = outs
        outputs.append(jnp.concatenate(outs, 0))
        saved.append(
            (inputs, proj, context, (lse, glse), norms_one, hidden_rows, acts, slopes, norms_two)
        )

    def to_owner(grad, split):
        half = grad.shape[0] // 2
        upper, lower = grad[:half], grad[half:]

        def first_link(s, a, b):
            if s == split.keeper(s, a, b):
                return (1 - s, a, b)
            return split.across(s, a, b)

        def second_link(s, a, b):
            if s == split.keeper(s, a, b):
                return None
            _, a2, b2 = split.across(s, a, b)
            return (1 - s, a2, b2)

        first = route(jnp.where(split.home, lower, upper), first_link)
        second = route(lower, second_link)
        part = first.astype(f32) + jnp.where(split.home, upper, second).astype(f32)
        return part.astype(bf16)

    mine, moved = own_rows(after(cotangent, outputs[0]))
    grad_out = part_rows(jnp.where(ByLane.home, mine, moved).astype(f32))
    weight_sums = [[None] * 4 for _ in range(sections)]
    norm_sums = [None] * sections
    input_grads = [None] * sections
    earlier_sums = ()

    def dp_sum(layer, which, terms):
        nonlocal earlier_sums
        terms = lax.optimization_barrier(tuple(terms) + earlier_sums)[: len(terms)]
        sums = lax.psum(tuple(terms), "dp")
        earlier_sums = tuple(sums)
        for index, value in zip(which, sums):
            weight_sums[layer][index] = value

    for layer in reversed(range(sections)):
        attn_w, out_w, up_w, down_w = weights[layer]
        gains, _ = norms[layer]
        inputs, proj, context, log_sums, norms_one, hidden_rows, acts, slopes, norms_two = saved[layer]
        grad_mlp, grad_up, grad_attn, grad_context, grads_one = [], [], [], [], []
        sums_one = sums_two = 0.0
        for p in range(parts):
            grad_two, sums = norm_backward(grad_out[p], *norms_two[p], gains[1])
            sums_two = sums_two + sums
            grad_mlp.append(gather(grad_two.astype(bf16), split_mlp))
            grad_up.append(
                [
                    (mm(piece, down_w, NT) * slope.astype(f32)).astype(bf16)
                    for piece, slope in zip(grad_mlp[p], slopes[p])
                ]
            )
            grad_hidden = scatter([mm(piece, up_w, NT) for piece in grad_up[p]], split_mlp) + grad_two
            grad_one, sums = norm_backward(grad_hidden, *norms_one[p], gains[0])
            sums_one = sums_one + sums
            grads_one.append(grad_one)
            grad_attn.append(gather(grad_one.astype(bf16), split_attn))
            grad_context.append([mm(piece, out_w, NT, bf16) for piece in grad_attn[p]])
        norm_sums[layer] = jnp.stack([sums_one, sums_two])
        grad_mlp, grad_up = joined(grad_mlp), joined(grad_up)
        grad_down_w = mm(joined(acts), grad_mlp, TN, bf16)
        grad_up_w = mm(joined(hidden_rows), grad_up, TN, bf16)
        mlp_terms = (to_owner(grad_up_w, split_mlp), to_owner(grad_down_w, split_mlp))
        dp_sum(layer, (2, 3), mlp_terms)
        grad_proj = attend_back(flat(proj), context, log_sums, flat(grad_context), info, plan)
        grad_attn_w = mm(joined(inputs), grad_proj, TN, bf16)
        grad_out_w = mm(context, joined(grad_attn), TN, bf16)
        attn_terms = (to_owner(grad_attn_w, split_attn), to_owner(grad_out_w, split_attn))
        dp_sum(layer, (0, 1), attn_terms)
        if layer == 0:
            grad_proj = after(grad_proj, grad_attn_w)
        grad_low = []
        for p, part in enumerate(cut(grad_proj)):
            grad_in = scatter([mm(piece, attn_w, NT) for piece in part], split_attn) + grads_one[p]
            grad_low.append(grad_in.astype(bf16))
        grad_out = [piece.astype(f32) for piece in grad_low]
        input_grads[layer] = jnp.concatenate(grad_low, 0)

    def pick(values):
        return jnp.where(section == 0, values[0], values[1])

    def placed_rows(chunks):
        result = []
        for index in range(micro):
            arrived = []
            for layer in range(sections):
                moved = route(chunks[layer], lambda s, a, b: (layer, s, b) if a == index else None)
                stays = (section == layer) & ByLane.home & (row == index)
                arrived.append(jnp.where(stays, chunks[layer], moved))
            result.append(pick(arrived))
        return jnp.stack(result)[None, :, None]

    def placed_weight(index, split):
        terms = [weight_sums[layer][index] for layer in range(sections)]
        mine = pick(terms)
        theirs = other_core(pick(terms[::-1]))
        first = jnp.where(split.home, mine, theirs)
        second = jnp.where(split.home, theirs, mine)
        return jnp.concatenate([first, second], 0).astype(f32)

    def dp_butterfly(value, combine):
        if copies & (copies - 1):
            gathered = lax.all_gather(value, "dp", axis=0)
            total = gathered[0]
            for index in range(1, copies):
                total = combine(total, gathered[index])
            return total
        distance = 1
        while distance < copies:
            pairs = [(d, d ^ distance) for d in range(copies)]
            value = combine(value, lax.ppermute(value, "dp", pairs))
            distance *= 2
        return value

    norm_sum = pick(norm_sums) + other_core(pick(norm_sums[::-1]))
    if crossed:
        norm_sum = norm_sum + other_row(norm_sum)
        norm_sum = norm_sum + other_lane(norm_sum)
    else:
        norm_sum = lax.psum(norm_sum, "tensor")
    norm_sum = dp_butterfly(norm_sum, jnp.add)

    peak_all = jnp.stack(peaks)
    peak_all = jnp.maximum(peak_all, other_row(peak_all))
    peak_all = dp_butterfly(peak_all, jnp.maximum)
    peak_here = jnp.where(ByLane.home, pick(peak_all), other_core(pick(peak_all[::-1])))
    factors = jnp.sqrt(clip_limit / jnp.maximum(peak_here, clip_limit))
    columns = jnp.repeat(factors, HEAD, axis=1)
    attn_local = w_attn[0].astype(f32)
    clipped = jnp.stack(
        [
            attn_local[:, 0] * columns[0][None, :],
            attn_local[:, 1] * columns[0][None, :],
            attn_local[:, 3] * columns[1][None, :],
            attn_local[:, 4] * columns[1][None, :],
        ],
        1,
    )
    return (
        placed_rows(outputs),
        placed_rows(input_grads),
        placed_weight(0, split_attn).reshape(1, width, 6, -1),
        placed_weight(1, split_attn)[None],
        placed_weight(2, split_mlp)[None],
        placed_weight(3, split_mlp)[None],
        norm_sum[:, 0][None],
        norm_sum[:, 1][None],
        clipped[None],
    )


def solution(mesh):
    in_specs = (
        P(None, "dp", "tensor", None),
        P(None, "dp", "tensor", None),
        P(None, "dp", None),
        P(None, "dp", None),
        P("section", None, None, "tensor"),
        P("section", "tensor", None),
        P("section", None, "tensor"),
        P("section", "tensor", None),
        P("section", None, None),
        P("section", None, None),
    )
    out_specs = (
        P("section", None, "dp", "tensor", None),
        P("section", None, "dp", "tensor", None),
        P("section", None, None, "tensor"),
        P("section", "tensor", None),
        P("section", None, "tensor"),
        P("section", "tensor", None),
        P("section", None, None),
        P("section", None, None),
        P("section", None, None, "tensor"),
    )
    return jax.shard_map(shards, mesh=mesh, in_specs=in_specs, out_specs=out_specs, check_vma=False)
```

time: 4140 us -> 1170 us (0.28)
  waiting for transfers between devices: 1660 us -> 366 us
  matrix products: 1090 us -> 173 us
  local copies, waits for them, and re-layouts: 817 us -> 82.6 us
  other arithmetic: 359 us -> 120 us
  starting transfers between devices: 2.29 us -> 233 us
  Pallas kernels: 0 us -> 169 us
  blocking collectives: 92.9 us -> 0 us
  loops' own time: 66.5 us -> 0 us
    dot_general x225 -> x72, matrix products: 1090 us -> 173 us  [mm(): lax.dot_general(left, right, dims, preferred_element_type=jnp.float32)]
    reduce_scatter x12 -> x0, waiting for transfers between devices: 826 us -> none  [the longest x3 258 us: shards(): lax.psum_scatter(jnp.dot(layer_activated, down_matrix, preferred_element_...]
    all_gather x12 -> x0, waiting for transfers between devices: 433 us -> none  [the longest x3 144 us: shards(): grad_mlp_rows = lax.all_gather(grad_mlp, 'tensor', axis=0, tiled=True)]
    dynamic_update_slice x48 -> x0, local copies, waits for them, and re-layouts: 365 us -> none  [the longest x24 128 us: attend(): local_ctx, local_sums, local_max = lax.map(one_block, starts)]
    psum x1 -> x4, waiting for transfers between devices: 390 us -> 49.8 us  [dp_sum(): sums = lax.psum(tuple(terms), 'dp')]
    ppermute x4 -> x152, waiting for transfers between devices: 5.56 us -> 316 us  [the longest x77 307 us: route(): return lax.ppermute(value, joint, pairs)]
    ppermute x4 -> x152, starting transfers between devices: 0.01 us -> 233 us  [the longest x77 132 us: route(): return lax.ppermute(value, joint, pairs)]
    pallas_call x0 -> x4, Pallas kernels: none -> 169 us  [the longest x2 102 us: attend_back(): pl.pallas_call(partial(attend_back_kernel, heads, plan, (len(proj), len(g...]
  transfers between devices with their start and end apart: 29 -> 156, of which waited for: 26 -> 48; matrix products, arithmetic and copies ran while one was open for 22% -> 29% of each run, Pallas kernels for 0% -> 15%
where the time goes in v1:
time: 1170 us; the launch traced here: 1160 us
  waiting for transfers between devices  366 us (31%)
  starting transfers between devices  233 us (20%)
  matrix products  173 us (15%)
  Pallas kernels  169 us (14%)
  other arithmetic  120 us (10%)
  local copies, waits for them, and re-layouts  82.6 us (7%)
  between operations  17.4 us (1%)
    ppermute x77, waiting for transfers between devices, route(): return lax.ppermute(value, joint, pairs)  307 us
    dot_general x72, matrix products, mm(): lax.dot_general(left, right, dims, preferred_element_type=jnp.float32)  173 us
    ppermute x77, starting transfers between devices, route(): return lax.ppermute(value, joint, pairs)  132 us
    pallas_call x2, Pallas kernels, attend_back(): pl.pallas_call(partial(attend_back_kernel, heads, plan, (len(proj), len(g...  102 us
    ppermute x71, starting transfers between devices, other_core(): return lax.ppermute(value, 'section', [(0, 1), (1, 0)])  87.4 us
    pallas_call x2, Pallas kernels, attend(): pl.pallas_call(partial(attend_kernel, heads, plan, len(proj)), out_shape=...  66.9 us
    psum x4, waiting for transfers between devices, dp_sum(): sums = lax.psum(tuple(terms), 'dp')  49.8 us
    unnamed x362, local copies, waits for them, and re-layouts  46.6 us
  transfers between devices with their start and end apart: 156, of which 48 were waited for; matrix products, arithmetic and copies ran while one was open for 29% of the time, Pallas kernels for 15%

profile of v1, /device:TPU:0, one launch (start us, length us, event | category | flops | bytes accessed | tf_op | source)
XLA Modules:
  0.0 1160.9 jit_solution(1068973442694630076)
XLA Ops:
  14.6 11.3 collective-permute-done
  104.6 33.4 %attend.2 = (bf16[2048,256]{1,0:T(8,128)(2,1)}, f32[4,2048]{1,0:T(4,128)}, f32[1,128]{1,0:T(1,128)}, f32[1,1024]{1,0:T(1,128)}, f32[1,128]{1,0:T(1,128)}) custom-call(s32[2]{0:T(128)} %pad_add_fusion.order_ref, s32[8]{0:T(128)} %get-tuple-element.302.first_ref, s32[8]{0:T(128)} %get-tuple-element.301.last_ref, ...), custom_call_target="tpu_custom_call" | custom-call | flops 10737418240 | bytes 7340032 | tf_op jit(solution)/shard_map/attend/pallas_call | solution.py:277
  161.9 10.5 collective-permute-done.13
  178.7 9.8 collective-permute-done.21
  192.7 16.9 %collective-permute-start.22 = (bf16[256,1024]{1,0:T(8,128)(2,1)S(1)}, bf16[256,1024]{1,0:T(8,128)(2,1)S(1)}, u32[]{:S(2)}, u32[]{:S(2)}) collective-permute-start(bf16[256,1024]{1,0:T(8,128)(2,1)S(1)} %collective-permute-done.21), channel_id=1, source_target_pairs={{0,16},{16,0},{1,17},{17,1},{2,18},{18,2},{3,19},{19,3},{4,20},{20... | collective-permute-start | bytes 1572872 | tf_op jit(solution)/shard_map/ppermute | solution.py:686
  265.4 11.2 collective-permute-done.33
  280.1 13.4 %collective-permute-done.38 = bf16[256,1024]{1,0:T(8,128)(2,1)S(1)} collective-permute-done((bf16[256,1024]{1,0:T(8,128)(2,1)S(1)}, bf16[256,1024]{1,0:T(8,128)(2,1)S(1)}, u32[]{:S(2)}, u32[]{:S(2)}) %collective-permute-start.38) | collective-permute-done | bytes 524320 | tf_op jit(solution)/shard_map/ppermute | solution.py:683
  324.4 33.5 %attend.3 = (bf16[2048,256]{1,0:T(8,128)(2,1)}, f32[4,2048]{1,0:T(4,128)}, f32[1,128]{1,0:T(1,128)}, f32[1,1024]{1,0:T(1,128)}, f32[1,128]{1,0:T(1,128)}) custom-call(s32[2]{0:T(128)} %pad_add_fusion.order_ref, s32[8]{0:T(128)} %get-tuple-element.302.first_ref, s32[8]{0:T(128)} %get-tuple-element.301.last_ref, ...), custom_call_target="tpu_custom_call" | custom-call | flops 10737418240 | bytes 7340032 | tf_op jit(solution)/shard_map/attend/pallas_call | solution.py:277
  393.7 14.2 %slice_multiply_fusion.3 = (f32[1024,1,256]{2,1,0:T(1,128)S(1)}, f32[1024,1,256]{2,1,0:T(1,128)S(1)}, f32[1024,1,256]{2,1,0:T(1,128)S(1)}, f32[1024,1,256]{2,1,0:T(1,128)S(1)}) fusion(f32[1024,6,256]{2,1,0:T(8,128)} %bitcast_convert_fusion, f32[256]{0:T(256)S(1)} %broadcast_in_dim.50, f32[256]{0:T(256)S(1)} %broadcast_in_dim.52), kind=kLoop, calls=%fused_computation.194 | loop fusion | flops 1048576 | bytes 8390656 | tf_op jit(solution)/shard_map/mul | solution.py:978
  415.2 9.4 collective-permute-done.47
  425.9 9.1 collective-permute-done.60
  479.9 10.3 collective-permute-done.66
  496.0 10.9 collective-permute-done.73
  586.6 11.4 collective-permute-done.137
  607.9 23.9 %collective-permute-done.135 = bf16[512,1024]{1,0:T(8,128)(2,1)S(1)} collective-permute-done((bf16[512,1024]{1,0:T(8,128)(2,1)S(1)}, bf16[512,1024]{1,0:T(8,128)(2,1)S(1)}, u32[]{:S(2)}, u32[]{:S(2)}) %collective-permute-start.135) | collective-permute-done | bytes 1048608 | tf_op jit(solution)/shard_map/ppermute | solution.py:683
  643.6 50.7 %attend_back.2 = bf16[2048,1536]{1,0:T(8,128)(2,1)} custom-call(s32[2]{0:T(128)} %pad_add_fusion.order_ref, s32[8]{0:T(128)} %get-tuple-element.302.first_ref, s32[8]{0:T(128)} %get-tuple-element.301.last_ref, bf16[512,1536]{1,0:T(8,128)(2,1)} %convolution_convert_fusion.5.refs_0_, bf16[512,1536]{1,0:T(8,128)(2,1)} %convolution_convert_fusion.4.refs_1_, ...), custom_call_target="tpu_custom_call" | custom-call | flops 32212254720 | bytes 14680064 | tf_op jit(solution)/shard_map/attend_back/pallas_call | solution.py:543
  734.9 10.3 collective-permute-done.91
  749.2 26.0 %collective-permute-done.94 = bf16[256,1024]{1,0:T(8,128)(2,1)} collective-permute-done((bf16[256,1024]{1,0:T(8,128)(2,1)S(1)}, bf16[256,1024]{1,0:T(8,128)(2,1)}, u32[]{:S(2)}, u32[]{:S(2)}) %collective-permute-start.94) | collective-permute-done | bytes 524320 | tf_op jit(solution)/shard_map/ppermute | solution.py:683
  814.2 9.1 collective-permute-done.97
  879.6 29.8 %collective-permute-done.145 = f32[2,2,1024]{2,0,1:T(2,128)S(1)} collective-permute-done((f32[2,2,1024]{2,0,1:T(2,128)S(1)}, f32[2,2,1024]{2,0,1:T(2,128)S(1)}, u32[]{:S(2)}, u32[]{:S(2)}) %collective-permute-start.145) | collective-permute-done | bytes 16416 | tf_op jit(solution)/shard_map/ppermute | solution.py:683
  926.3 50.9 %attend_back.3 = bf16[2048,1536]{1,0:T(8,128)(2,1)} custom-call(s32[2]{0:T(128)} %pad_add_fusion.order_ref, s32[8]{0:T(128)} %get-tuple-element.302.first_ref, s32[8]{0:T(128)} %get-tuple-element.301.last_ref, bf16[512,1536]{1,0:T(8,128)(2,1)} %convolution_convert_fusion.9.refs_0_, bf16[512,1536]{1,0:T(8,128)(2,1)} %convolution_convert_fusion.8.refs_1_, ...), custom_call_target="tpu_custom_call" | custom-call | flops 32212254720 | bytes 14680064 | tf_op jit(solution)/shard_map/attend_back/pallas_call | solution.py:543
  977.3 9.2 convolution_convert_fusion.1
  1004.6 30.0 %collective-permute-start.116 = (bf16[256,1024]{1,0:T(8,128)(2,1)}, bf16[256,1024]{1,0:T(8,128)(2,1)}, u32[]{:S(2)}, u32[]{:S(2)}) collective-permute-start(bf16[256,1024]{1,0:T(8,128)(2,1)} %slice.937), channel_id=1, source_target_pairs={{0,16},{16,0},{1,17},{17,1},{2,18},{18,2},{3,19},{19,3},{4,20},{20... | collective-permute-start | bytes 1572872 | tf_op jit(solution)/shard_map/ppermute | solution.py:686
  1074.2 49.8 %all-reduce.9.cloned.1.call-done = (bf16[512,1536]{1,0:T(8,128)(2,1)}, bf16[128,1024]{1,0:T(8,128)(2,1)}) async-done(((bf16[512,1536]{1,0:T(8,128)(2,1)}, bf16[128,1024]{1,0:T(8,128)(2,1)}), (bf16[512,1536]{1,0:T(8,128)(2,1)}, bf16[128,1024]{1,0:T(8,128)(2,1)})) %all-reduce.9.cloned.1.call-update) | async-done | bytes 1835024 | tf_op jit(solution)/shard_map/psum | solution.py:878
  (963 shorter events, 648.4 us)
Async XLA Ops:
  7.2 772.6 %all-reduce.15.cloned.1.call-start = ((), (), s32[]{:S(2)}) async-start(), calls=%async_computation.3 | async-start | bytes 4194304 | tf_op jit(solution)/shard_map/psum | solution.py:878
  75.3 72.2 %collective-permute-start.17 = (bf16[1024,1024]{1,0:T(8,128)(2,1)}, bf16[1024,1024]{1,0:T(8,128)(2,1)}, u32[]{:S(2)}, u32[]{:S(2)}) collective-permute-start(bf16[1024,1024]{1,0:T(8,128)(2,1)} %bitcast.209), channel_id=1, source_target_pairs={{0,1},{1,16},{2,3},{3,18},{4,5},{5,20},{6,7},{7,22},{8,9},{9,24},{... | collective-permute-start | bytes 6291464 | tf_op jit(solution)/shard_map/ppermute | solution.py:683
  80.0 69.4 %collective-permute-start.16 = (bf16[1024,1024]{1,0:T(8,128)(2,1)}, bf16[1024,1024]{1,0:T(8,128)(2,1)}, u32[]{:S(2)}, u32[]{:S(2)}) collective-permute-start(bf16[1024,1024]{1,0:T(8,128)(2,1)} %bitcast.210), channel_id=1, source_target_pairs={{1,17},{3,19},{5,21},{7,23},{9,25},{11,27},{13,29},{15,31}} | collective-permute-start | bytes 6291464 | tf_op jit(solution)/shard_map/ppermute | solution.py:683
  84.3 57.3 %collective-permute-start.10 = (bf16[256,1024]{1,0:T(8,128)(2,1)}, bf16[256,1024]{1,0:T(8,128)(2,1)}, u32[]{:S(2)}, u32[]{:S(2)}) collective-permute-start(bf16[256,1024]{1,0:T(8,128)(2,1)} %bitcast.11), channel_id=1, source_target_pairs={{0,2},{1,3},{2,16},{3,17},{4,6},{5,7},{6,20},{7,21},{8,10},{9,11},... | collective-permute-start | bytes 1572872 | tf_op jit(solution)/shard_map/ppermute | solution.py:683
  88.2 53.4 %collective-permute-start.9 = (bf16[256,1024]{1,0:T(8,128)(2,1)}, bf16[256,1024]{1,0:T(8,128)(2,1)}, u32[]{:S(2)}, u32[]{:S(2)}) collective-permute-start(bf16[256,1024]{1,0:T(8,128)(2,1)} %bitcast.11), channel_id=1, source_target_pairs={{2,18},{3,19},{6,22},{7,23},{10,26},{11,27},{14,30},{15,31}} | collective-permute-start | bytes 1572872 | tf_op jit(solution)/shard_map/ppermute | solution.py:683
  153.6 56.0 %collective-permute-start.18 = (bf16[1024,1024]{1,0:T(8,128)(2,1)}, bf16[1024,1024]{1,0:T(8,128)(2,1)S(1)}, u32[]{:S(2)}, u32[]{:S(2)}) collective-permute-start(bf16[1024,1024]{1,0:T(8,128)(2,1)} %bitcast.15), channel_id=1, source_target_pairs={{1,17},{3,19},{5,21},{7,23},{9,25},{11,27},{13,29},{15,31}} | collective-permute-start | bytes 6291464 | tf_op jit(solution)/shard_map/ppermute | solution.py:683
  154.4 87.2 %collective-permute-start.37 = (bf16[1024,1536]{0,1:T(8,128)(2,1)S(1)}, bf16[1024,1536]{0,1:T(8,128)(2,1)S(1)}, u32[]{:S(2)}, u32[]{:S(2)}) collective-permute-start(bf16[1024,1536]{0,1:T(8,128)(2,1)S(1)} %bitcast.206), channel_id=1, source_target_pairs={{16,2},{17,3},{18,16},{19,17},{20,6},{21,7},{22,20},{23,21},{24,10... | collective-permute-start | bytes 9437192 | tf_op jit(solution)/shard_map/ppermute | solution.py:683
  177.4 64.7 %collective-permute-start.36 = (bf16[1024,1536]{0,1:T(8,128)(2,1)S(1)}, bf16[1024,1536]{0,1:T(8,128)(2,1)S(1)}, u32[]{:S(2)}, u32[]{:S(2)}) collective-permute-start(bf16[1024,1536]{0,1:T(8,128)(2,1)S(1)} %bitcast.207), channel_id=1, source_target_pairs={{16,0},{17,1},{20,4},{21,5},{24,8},{25,9},{28,12},{29,13}} | collective-permute-start | bytes 9437192 | tf_op jit(solution)/shard_map/ppermute | solution.py:683
  188.5 62.0 %collective-permute-start.50 = (bf16[1024,1024]{1,0:T(8,128)(2,1)S(1)}, bf16[1024,1024]{1,0:T(8,128)(2,1)S(1)}, u32[]{:S(2)}, u32[]{:S(2)}) collective-permute-start(bf16[1024,1024]{1,0:T(8,128)(2,1)S(1)} %bitcast.212), channel_id=1, source_target_pairs={{16,1},{17,16},{18,3},{19,18},{20,5},{21,20},{22,7},{23,22},{24,9}... | collective-permute-start | bytes 6291464 | tf_op jit(solution)/shard_map/ppermute | solution.py:683
  298.7 225.6 %collective-permute-start.68 = (bf16[512,1024]{1,0:T(8,128)(2,1)}, bf16[512,1024]{1,0:T(8,128)(2,1)}, u32[]{:S(2)}, u32[]{:S(2)}) collective-permute-start(bf16[512,1024]{1,0:T(8,128)(2,1)} %pad_maximum_fusion.1), channel_id=1, source_target_pairs={{2,0},{3,1},{18,2},{19,3},{6,4},{7,5},{22,6},{23,7},{10,8},{11,9},... | collective-permute-start | bytes 3145736 | tf_op jit(solution)/shard_map/ppermute | solution.py:683
  304.7 108.0 %collective-permute-start.52 = (bf16[1024,1024]{1,0:T(8,128)(2,1)}, bf16[1024,1024]{1,0:T(8,128)(2,1)}, u32[]{:S(2)}, u32[]{:S(2)}) collective-permute-start(bf16[1024,1024]{1,0:T(8,128)(2,1)} %bitcast.15), channel_id=1, source_target_pairs={{16,1},{17,16},{18,3},{19,18},{20,5},{21,20},{22,7},{23,22},{24,9}... | collective-permute-start | bytes 6291464 | tf_op jit(solution)/shard_map/ppermute | solution.py:683
  311.8 101.0 %collective-permute-start.51 = (bf16[1024,1024]{1,0:T(8,128)(2,1)}, bf16[1024,1024]{1,0:T(8,128)(2,1)}, u32[]{:S(2)}, u32[]{:S(2)}) collective-permute-start(bf16[1024,1024]{1,0:T(8,128)(2,1)} %bitcast.15), channel_id=1, source_target_pairs={{16,0},{18,2},{20,4},{22,6},{24,8},{26,10},{28,12},{30,14}} | collective-permute-start | bytes 6291464 | tf_op jit(solution)/shard_map/ppermute | solution.py:683
  473.2 51.2 %collective-permute-start.34 = (bf16[512,1024]{1,0:T(8,128)(2,1)}, bf16[512,1024]{1,0:T(8,128)(2,1)S(1)}, u32[]{:S(2)}, u32[]{:S(2)}) collective-permute-start(bf16[512,1024]{1,0:T(8,128)(2,1)} %pad_maximum_fusion.1), channel_id=1, source_target_pairs={{16,2},{17,3},{20,6},{21,7},{24,10},{25,11},{28,14},{29,15}} | collective-permute-start | bytes 3145736 | tf_op jit(solution)/shard_map/ppermute | solution.py:683
  575.9 55.8 %collective-permute-start.135 = (bf16[512,1024]{1,0:T(8,128)(2,1)S(1)}, bf16[512,1024]{1,0:T(8,128)(2,1)S(1)}, u32[]{:S(2)}, u32[]{:S(2)}) collective-permute-start(bf16[512,1024]{1,0:T(8,128)(2,1)S(1)} %get-tuple-element.231), channel_id=1, source_target_pairs={{0,16},{1,0},{2,18},{3,2},{16,17},{17,1},{18,19},{19,3},{4,20},{5,... | collective-permute-start | bytes 3145736 | tf_op jit(solution)/shard_map/ppermute | solution.py:683
  633.4 281.1 %all-reduce.13.cloned.1.call-start = ((), (), s32[]{:S(2)}) async-start(), calls=%async_computation.2 | async-start | bytes 3670016 | tf_op jit(solution)/shard_map/psum | solution.py:878
  726.0 50.1 %collective-permute-start.132 = (bf16[512,1536]{1,0:T(8,128)(2,1)S(1)}, bf16[512,1536]{1,0:T(8,128)(2,1)S(1)}, u32[]{:S(2)}, u32[]{:S(2)}) collective-permute-start(bf16[512,1536]{1,0:T(8,128)(2,1)S(1)} %get-tuple-element.222), channel_id=1, source_target_pairs={{2,16},{3,17},{16,2},{17,3},{6,20},{7,21},{20,6},{21,7},{10,24},{1... | collective-permute-start | bytes 4718600 | tf_op jit(solution)/shard_map/ppermute | solution.py:683
  797.7 246.9 %all-reduce.11.cloned.1.call-start = ((), (), s32[]{:S(2)}) async-start(), calls=%async_computation.1 | async-start | bytes 4194304 | tf_op jit(solution)/shard_map/psum | solution.py:878
  851.4 61.4 %collective-permute-start.128 = (bf16[512,1024]{1,0:T(8,128)(2,1)S(1)}, bf16[512,1024]{1,0:T(8,128)(2,1)S(1)}, u32[]{:S(2)}, u32[]{:S(2)}) collective-permute-start(bf16[512,1024]{1,0:T(8,128)(2,1)S(1)} %get-tuple-element.226), channel_id=1, source_target_pairs={{1,16},{3,18},{16,1},{18,3},{5,20},{7,22},{20,5},{22,7},{9,24},{11... | collective-permute-start | bytes 3145736 | tf_op jit(solution)/shard_map/ppermute | solution.py:683
  854.0 58.9 %collective-permute-start.127 = (bf16[512,1024]{1,0:T(8,128)(2,1)S(1)}, bf16[512,1024]{1,0:T(8,128)(2,1)S(1)}, u32[]{:S(2)}, u32[]{:S(2)}) collective-permute-start(bf16[512,1024]{1,0:T(8,128)(2,1)S(1)} %get-tuple-element.227), channel_id=1, source_target_pairs={{0,16},{1,0},{2,18},{3,2},{16,17},{17,1},{18,19},{19,3},{4,20},{5,... | collective-permute-start | bytes 3145736 | tf_op jit(solution)/shard_map/ppermute | solution.py:683
  914.5 209.5 %all-reduce.9.cloned.1.call-start = ((), (), s32[]{:S(2)}) async-start(), calls=%async_computation | async-start | bytes 3670016 | tf_op jit(solution)/shard_map/psum | solution.py:878
  1047.3 80.7 %collective-permute-start.122 = (bf16[512,1024]{1,0:T(8,128)(2,1)}, bf16[512,1024]{1,0:T(8,128)(2,1)}, u32[]{:S(2)}, u32[]{:S(2)}) collective-permute-start(bf16[512,1024]{1,0:T(8,128)(2,1)} %pad_maximum_fusion.5), channel_id=1, source_target_pairs={{2,16},{3,17},{6,20},{7,21},{10,24},{11,25},{14,28},{15,29}} | collective-permute-start | bytes 3145736 | tf_op jit(solution)/shard_map/ppermute | solution.py:683
  1056.6 71.4 %collective-permute-start.120 = (bf16[512,1024]{1,0:T(8,128)(2,1)}, bf16[512,1024]{1,0:T(8,128)(2,1)}, u32[]{:S(2)}, u32[]{:S(2)}) collective-permute-start(bf16[512,1024]{1,0:T(8,128)(2,1)} %pad_maximum_fusion.5), channel_id=1, source_target_pairs={{0,16},{1,17},{16,18},{17,19},{4,20},{5,21},{20,22},{21,23},{8,24}... | collective-permute-start | bytes 3145736 | tf_op jit(solution)/shard_map/ppermute | solution.py:683
  1068.1 59.9 %collective-permute-start.121 = (bf16[512,1024]{1,0:T(8,128)(2,1)}, bf16[512,1024]{1,0:T(8,128)(2,1)}, u32[]{:S(2)}, u32[]{:S(2)}) collective-permute-start(bf16[512,1024]{1,0:T(8,128)(2,1)} %pad_maximum_fusion.4), channel_id=1, source_target_pairs={{2,0},{3,1},{18,2},{19,3},{6,4},{7,5},{22,6},{23,7},{10,8},{11,9},... | collective-permute-start | bytes 3145736 | tf_op jit(solution)/shard_map/ppermute | solution.py:683
  1069.5 58.5 %collective-permute-start.119 = (bf16[512,1024]{1,0:T(8,128)(2,1)}, bf16[512,1024]{1,0:T(8,128)(2,1)}, u32[]{:S(2)}, u32[]{:S(2)}) collective-permute-start(bf16[512,1024]{1,0:T(8,128)(2,1)} %pad_maximum_fusion.4), channel_id=1, source_target_pairs={{16,2},{17,3},{20,6},{21,7},{24,10},{25,11},{28,14},{29,15}} | collective-permute-start | bytes 3145736 | tf_op jit(solution)/shard_map/ppermute | solution.py:683
  (290 other events, 4818.3 us)
Sparse Core Ops, SparseCore 0:
  633.5 85.9 all-reduce.14
  797.8 78.5 all-reduce.12
  914.6 85.0 all-reduce.10
  1044.8 79.1 all-reduce.8

commit v2 on v1

--- a/solution.py
+++ b/solution.py
@@ -11,7 +11,7 @@
 HEAD = 64
 HALF = 512
 QTILE = 256
-KTILE = 256
+KTILE = 512
 VMEM_BYTES = 56 * 1024 * 1024
 
 masked_fill = -1e30
@@ -589,7 +589,7 @@
             dimension_semantics=("arbitrary",), vmem_limit_bytes=VMEM_BYTES
         ),
         cost_estimate=pl.CostEstimate(
-            flops=60 * length * 1024 * width, bytes_accessed=28 * length * width,
+            flops=4 * length * 1024 * width, bytes_accessed=4 * length * width,
             transcendentals=length * 1024 * heads,
         ),
         name="attend_back",
@@ -649,6 +649,44 @@
     return lax.optimization_barrier((value,) + others)[0]
 
 
+def unpack_kernel(blocks, each, per_half, home_ref, mine_ref, theirs_ref, out_ref):
+    upper = pl.program_id(0) < per_half
+    take_mine = upper == (home_ref[0] == 1)
+    for index in range(blocks):
+        cols = slice(index * each, (index + 1) * each)
+        value = jnp.where(
+            take_mine, mine_ref[:, cols].astype(jnp.float32), theirs_ref[:, cols].astype(jnp.float32)
+        )
+        out_ref[index] = value
+
+
+def unpack(home, mine, theirs, blocks, each):
+    half, columns = mine.shape
+    tile = min(128, half)
+    per_half = half // tile
+    source = pl.BlockSpec((tile, columns), lambda step, _: (lax.rem(step, per_half), 0))
+    return pl.pallas_call(
+        partial(unpack_kernel, blocks, each, per_half),
+        out_shape=jax.ShapeDtypeStruct((blocks, 2 * half, each), jnp.float32),
+        grid_spec=pltpu.PrefetchScalarGridSpec(
+            num_scalar_prefetch=1,
+            grid=(2 * per_half,),
+            in_specs=[source, source],
+            out_specs=pl.BlockSpec((blocks, tile, each), lambda step, _: (0, step, 0)),
+        ),
+        compiler_params=pltpu.CompilerParams(dimension_semantics=("arbitrary",)),
+        name="unpack",
+    )(home, mine, theirs)
+
+
+def gated(value, *others):
+    zero = 0.0
+    for other in others:
+        corner = lax.slice(other, (0,) * other.ndim, (1,) * other.ndim)
+        zero = zero + corner.reshape(()).astype(jnp.float32) * 0.0
+    return (value.astype(jnp.float32) + zero).astype(value.dtype)
+
+
 def shards(tokens, cotangent, doc_ids, global_flags, w_attn, w_out, w_up, w_down, ln_gain, ln_bias):
     bf16, f32 = jnp.bfloat16, jnp.float32
     sections = lax.axis_size("section")
@@ -719,30 +757,51 @@
     split_mlp = ByRow if crossed else ByLane
 
     def gather(own, split, hop=None):
-        near = jnp.concatenate([own, other_core(own)], 0)
+        with jax.named_scope("gsec"):
+            near = jnp.concatenate([own, other_core(own)], 0)
         if not crossed:
             if inner == 1:
                 return [near]
             return [lax.all_gather(near, "tensor", axis=0, tiled=True, axis_index_groups=groups)]
         if hop is None:
-            hop = split.swap(own)
-        return [near, jnp.concatenate([hop, other_core(hop)], 0)]
-
-    def scatter(partials, split):
+            with jax.named_scope("ghop"):
+                hop = split.swap(own)
+        with jax.named_scope("gsec2"):
+            return [near, jnp.concatenate([hop, other_core(hop)], 0)]
+
+    def scatter_begin(partials, gates=()):
         if not crossed:
             blocks = partials[0].reshape(inner, 2, rows, -1)
             ours, theirs = blocks[:, 0], blocks[:, 1].astype(bf16)
             total = (ours + other_core(theirs).astype(f32)).reshape(inner * rows, -1)
+            return total.astype(bf16), None
+        near, far = partials
+        with jax.named_scope("ssec"):
+            leaving = far[:rows] + other_core(far[rows:].astype(bf16)).astype(f32)
+            leaving = gated(leaving, *gates)
+        with jax.named_scope("ssec2"):
+            staying = near[:rows] + other_core(near[rows:].astype(bf16)).astype(f32)
+        return leaving.astype(bf16), staying
+
+    def scatter_end(begun, split):
+        leaving, staying = begun
+        if not crossed:
             if inner == 1:
-                return total
+                return leaving.astype(f32)
             return lax.psum_scatter(
-                total.astype(bf16), "tensor", scatter_dimension=0, tiled=True,
-                axis_index_groups=groups,
+                leaving, "tensor", scatter_dimension=0, tiled=True, axis_index_groups=groups
             ).astype(f32)
-        near, far = partials
-        leaving = far[:rows] + other_core(far[rows:].astype(bf16)).astype(f32)
-        staying = near[:rows] + other_core(near[rows:].astype(bf16)).astype(f32)
-        return staying + split.swap(leaving.astype(bf16)).astype(f32)
+        with jax.named_scope("shop"):
+            return staying + split.swap(leaving).astype(f32)
+
+    def scatter_all(begun, split):
+        sums = [scatter_end(item, split) for item in begun]
+        if not crossed:
+            return sums
+        return [
+            gated(item, begun[p + 1][0]) if p + 1 < len(sums) else item
+            for p, item in enumerate(sums)
+        ]
 
     def cut(array):
         per_part = 2 * inner * rows
@@ -781,27 +840,43 @@
         near = route(weight, within)
         return jnp.where(split.home, jnp.where(section == layer, weight, near), far)
 
+    attn_table = w_attn[0].reshape(width, -1)
+    mlp_pack = jnp.concatenate([w_up[0], w_down[0].reshape(width, -1)], 1)
+
+    def attn_unpack(pack):
+        columns = w_attn.shape[2] * w_attn.shape[3]
+        return pack[:, :columns], pack[:, columns:].reshape(w_out.shape[1:])
+
+    def mlp_unpack(pack):
+        columns = w_up.shape[2]
+        return pack[:, :columns], pack[:, columns:].reshape(w_down.shape[1:])
+
     mine, moved = own_rows(tokens)
     own = part_rows(jnp.where(ByLane.home, mine, moved))
-    hops = [None] * parts
+    hops = []
     if crossed:
         early = route(mine, lambda s, a, b: (s, a, 1 - b) if s == a else None)
         late = route(moved, lambda s, a, b: (s, a, 1 - b) if s != a else None)
         hops = part_rows(jnp.where(ByLane.home, early, late))
-    attn_table = w_attn[0].reshape(width, -1)
-    weights = [[None] * 4 for _ in range(sections)]
-    weights[0][0] = fetch(after(attn_table, moved), 0, split_attn)
-    weights[0][1] = fetch(after(w_out[0], weights[0][0]), 0, split_attn)
-    weights[0][2] = fetch(after(w_up[0], hops[0]) if crossed else w_up[0], 0, split_mlp)
-    weights[0][3] = fetch(after(w_down[0], weights[0][2]), 0, split_mlp)
-    weights[1][0] = fetch(after(attn_table, weights[0][1]), 1, split_attn)
-    weights[1][1] = fetch(after(w_out[0], weights[1][0]), 1, split_attn)
+    attn_weights = [None] * sections
+    mlp_weights = [None] * sections
+    with jax.named_scope("W0attn"):
+        first_weight = fetch(attn_table, 0, split_attn)
+    with jax.named_scope("W0out"):
+        second_weight = fetch(after(w_out[0], *hops), 0, split_attn)
+    with jax.named_scope("W0mlp"):
+        arriving = fetch(after(mlp_pack, *own, *hops), 0, split_mlp)
 
     heads = w_attn.shape[3] // HEAD
     docs = lax.dynamic_index_in_dim(doc_ids[:, 0], row, 0, False)
     flags = lax.dynamic_index_in_dim(global_flags[:, 0], row, 0, False)
     order = jnp.stack([section, lane if crossed else jnp.zeros_like(lane)]).astype(jnp.int32)
     info = sequence_info(docs, flags, order, heads)
+    attn_pack = jnp.concatenate([attn_table, w_out[0].reshape(width, -1)], 1)
+    first_weight, second_weight, attn_pack, mlp_pack, *info = lax.optimization_barrier(
+        (first_weight, second_weight, attn_pack, mlp_pack, *info)
+    )
+    attn_weights[0] = (first_weight, second_weight)
 
     gains_own = jnp.stack([ln_gain[0], ln_bias[0]])
     gains_other = other_core(gains_own)
@@ -810,45 +885,68 @@
     saved, outputs, peaks = [], [], []
     for layer in range(sections):
         gains, shifts = norms[layer]
-        inputs = [gather(own[p], split_attn, hops[p] if layer == 0 else None) for p in range(parts)]
-        proj = [[mm(piece, weights[layer][0], NN, bf16) for piece in part] for part in inputs]
-        context, lse, glse, peak, gpeak = attend(flat(proj), info, plan)
-        peaks.append(
-            jnp.stack([jnp.max(peak.reshape(heads, -1), 1), jnp.max(gpeak.reshape(heads, -1), 1)])
-        )
-        context_parts = cut(context)
-        attn_sums = [
-            scatter([mm(piece, weights[layer][1]) for piece in part], split_attn)
-            for part in context_parts
-        ]
+        attn_w, out_w = attn_weights[layer]
+        with jax.named_scope(f"F{layer}in"):
+            inputs = [
+                gather(own[p], split_attn, hops[p] if layer == 0 and crossed else None)
+                for p in range(parts)
+            ]
+            proj = [[mm(piece, attn_w, NN, bf16) for piece in part] for part in inputs]
+        context, lse, glse, *tops = attend(flat(proj), info, plan)
+        peaks.append(tops)
         if layer == 0:
-            weights[1][2] = fetch(after(w_up[0], attn_sums[-1]), 1, split_mlp)
-        hidden_rows, acts, slopes, norms_one, norms_two, outs = [], [], [], [], [], []
+            with jax.named_scope("W1attn"):
+                pack = fetch(after(attn_pack, *flat(proj)), 1, split_attn)
+            context, arriving, pack = lax.optimization_barrier((context, arriving, pack))
+            mlp_weights[0], attn_weights[1] = mlp_unpack(arriving), attn_unpack(pack)
+        else:
+            with jax.named_scope("W1mlp"):
+                pack = fetch(after(mlp_pack, *flat(proj)), 1, split_mlp)
+            with jax.named_scope("COT"):
+                mine, moved = own_rows(after(cotangent, *flat(proj)))
+            context, pack, mine, moved = lax.optimization_barrier((context, pack, mine, moved))
+            mlp_weights[1] = mlp_unpack(pack)
+            grad_out = part_rows(jnp.where(ByLane.home, mine, moved).astype(f32))
+        up_w, down_w = mlp_weights[layer]
+        with jax.named_scope(f"F{layer}out"):
+            sums = scatter_all(
+                [scatter_begin([mm(piece, out_w) for piece in part]) for part in cut(context)],
+                split_attn,
+            )
+        hidden, hidden_low, norms_one = [], [], []
         for p in range(parts):
-            hidden, normed, scale = norm_forward(
-                own[p].astype(f32) + attn_sums[p], gains[0], shifts[0]
-            )
-            norms_one.append((normed, scale))
-            hidden_rows.append(gather(hidden.astype(bf16), split_mlp))
-            pairs = [gelu_pair(mm(piece, weights[layer][2])) for piece in hidden_rows[p]]
-            acts.append([act for act, _ in pairs])
-            slopes.append([slope for _, slope in pairs])
-            mlp_sum = scatter([mm(act, weights[layer][3]) for act in acts[p]], split_mlp)
-            out, normed, scale = norm_forward(hidden + mlp_sum, gains[1], shifts[1])
-            norms_two.append((normed, scale))
-            outs.append(out.astype(bf16))
-        if layer == 0:
-            weights[1][3] = fetch(after(w_down[0], weights[1][2], outs[-1]), 1, split_mlp)
+            with jax.named_scope(f"F{layer}norm1"):
+                value = gated(sums[p], hidden_low[-1]) if p else sums[p]
+                value, normed, scale = norm_forward(own[p].astype(f32) + value, gains[0], shifts[0])
+                hidden.append(value)
+                hidden_low.append(value.astype(bf16))
+                norms_one.append((normed, scale))
+        hidden_rows, acts, slopes, begun = [], [], [], []
+        for p in range(parts):
+            with jax.named_scope(f"F{layer}mlp{p}"):
+                hidden_rows.append(gather(hidden_low[p], split_mlp))
+                pairs = [gelu_pair(mm(piece, up_w)) for piece in hidden_rows[p]]
+                acts.append([act for act, _ in pairs])
+                slopes.append([slope for _, slope in pairs])
+                begun.append(
+                    scatter_begin([mm(act, down_w) for act in acts[p]], hidden_low[p + 1 : p + 2])
+                )
+        with jax.named_scope(f"F{layer}mlp"):
+            sums = scatter_all(begun, split_mlp)
+        outs, norms_two = [], []
+        for p in range(parts):
+            with jax.named_scope(f"F{layer}norm2"):
+                value = gated(sums[p], outs[-1]) if p else sums[p]
+                value, normed, scale = norm_forward(hidden[p] + value, gains[1], shifts[1])
+                norms_two.append((normed, scale))
+                outs.append(value.astype(bf16))
         own = outs
         outputs.append(jnp.concatenate(outs, 0))
         saved.append(
             (inputs, proj, context, (lse, glse), norms_one, hidden_rows, acts, slopes, norms_two)
         )
 
-    def to_owner(grad, split):
-        half = grad.shape[0] // 2
-        upper, lower = grad[:half], grad[half:]
-
+    def to_owner(upper, lower, split, gates=()):
         def first_link(s, a, b):
             if s == split.keeper(s, a, b):
                 return (1 - s, a, b)
@@ -860,89 +958,154 @@
             _, a2, b2 = split.across(s, a, b)
             return (1 - s, a2, b2)
 
-        first = route(jnp.where(split.home, lower, upper), first_link)
+        first = route(gated(jnp.where(split.home, lower, upper), *gates), first_link)
         second = route(lower, second_link)
         part = first.astype(f32) + jnp.where(split.home, upper, second).astype(f32)
         return part.astype(bf16)
 
-    mine, moved = own_rows(after(cotangent, outputs[0]))
-    grad_out = part_rows(jnp.where(ByLane.home, mine, moved).astype(f32))
-    weight_sums = [[None] * 4 for _ in range(sections)]
+    earlier = ()
+
+    def dp_sum(*terms):
+        nonlocal earlier
+        terms = [after(term, *earlier) for term in terms]
+        earlier = lax.psum(tuple(terms), "dp")
+        return earlier
+
+    def pick(values):
+        return jnp.where(section == 0, values[0], values[1])
+
+    def placed(chunk, layer):
+        arrived = []
+        for index in range(micro):
+            moved = route(chunk, lambda s, a, b: (layer, s, b) if a == index else None)
+            stays = (section == layer) & ByLane.home & (row == index)
+            arrived.append(jnp.where(stays, chunk, moved))
+        return arrived
+
+    def send_attn(pack, gates):
+        half = width // 2
+        return to_owner(pack[:half], pack[half:], split_attn, gates)
+
+    attn_sums = [None] * sections
+    mlp_sums = [None] * sections
     norm_sums = [None] * sections
-    input_grads = [None] * sections
-    earlier_sums = ()
-
-    def dp_sum(layer, which, terms):
-        nonlocal earlier_sums
-        terms = lax.optimization_barrier(tuple(terms) + earlier_sums)[: len(terms)]
-        sums = lax.psum(tuple(terms), "dp")
-        earlier_sums = tuple(sums)
-        for index, value in zip(which, sums):
-            weight_sums[layer][index] = value
-
+    out_rows = [None] * sections
+    grad_rows = [None] * sections
     for layer in reversed(range(sections)):
-        attn_w, out_w, up_w, down_w = weights[layer]
+        (attn_w, out_w), (up_w, down_w) = attn_weights[layer], mlp_weights[layer]
         gains, _ = norms[layer]
         inputs, proj, context, log_sums, norms_one, hidden_rows, acts, slopes, norms_two = saved[layer]
-        grad_mlp, grad_up, grad_attn, grad_context, grads_one = [], [], [], [], []
-        sums_one = sums_two = 0.0
+        grads_two, low, sums_two = [], [], []
         for p in range(parts):
-            grad_two, sums = norm_backward(grad_out[p], *norms_two[p], gains[1])
-            sums_two = sums_two + sums
-            grad_mlp.append(gather(grad_two.astype(bf16), split_mlp))
-            grad_up.append(
+            with jax.named_scope(f"B{layer}norm2"):
+                value = gated(grad_out[p], low[-1]) if p else grad_out[p]
+                value, sums = norm_backward(value, *norms_two[p], gains[1])
+                grads_two.append(value)
+                low.append(value.astype(bf16))
+                sums_two.append(sums)
+        grad_mlp, grad_up, begun = [], [], []
+        for p in range(parts):
+            with jax.named_scope(f"B{layer}mlp{p}"):
+                grad_mlp.append(gather(low[p], split_mlp))
+                grad_up.append(
+                    [
+                        (mm(piece, down_w, NT) * slope.astype(f32)).astype(bf16)
+                        for piece, slope in zip(grad_mlp[p], slopes[p])
+                    ]
+                )
+                begun.append(
+                    scatter_begin([mm(piece, up_w, NT) for piece in grad_up[p]], low[p + 1 : p + 2])
+                )
+        with jax.named_scope(f"B{layer}mlp"):
+            sums = scatter_all(begun, split_mlp)
+        with jax.named_scope(f"B{layer}wmlp"):
+            grad_up_w = mm(joined(hidden_rows), joined(grad_up), TN, bf16)
+            grad_down_w = mm(joined(acts), joined(grad_mlp), TN, bf16)
+            sums[-1] = gated(sums[-1], grad_up_w, grad_down_w)
+        grads_one, low, sums_one = [], [], []
+        for p in range(parts):
+            with jax.named_scope(f"B{layer}norm1"):
+                value = gated(sums[p], low[-1]) if p else sums[p]
+                value, total = norm_backward(value + grads_two[p], *norms_one[p], gains[0])
+                grads_one.append(value)
+                low.append(value.astype(bf16))
+                sums_one.append(total)
+        norm_sums[layer] = (sums_one, sums_two)
+        grad_attn, grad_context = [], []
+        for p in range(parts):
+            with jax.named_scope(f"B{layer}ctx{p}"):
+                grad_attn.append(gather(low[p], split_attn))
+                grad_context.append([mm(piece, out_w, NT, bf16) for piece in grad_attn[p]])
+        with jax.named_scope(f"B{layer}wmlp"):
+            mlp_parts = to_owner(
+                grad_up_w.reshape(width, -1), grad_down_w.reshape(width, -1), split_mlp,
+                flat(grad_context) if layer else low,
+            )
+        if layer == 0:
+            *grad_context[-1], mlp_sums[1] = lax.optimization_barrier(
+                (*grad_context[-1], mlp_sums[1])
+            )
+        grad_context = flat(grad_context)
+        if layer == 0:
+            with jax.named_scope("B1wattn"):
+                attn_parts = send_attn(pack, grad_context)
+            *grad_context, mlp_parts = lax.optimization_barrier((*grad_context, mlp_parts))
+            mlp_sums[0] = dp_sum(mlp_parts)[0]
+        grad_proj = attend_back(flat(proj), context, log_sums, grad_context, info, plan)
+        if layer == 1:
+            with jax.named_scope("OUTROWS"):
+                ready = lax.optimization_barrier((*outputs, *grad_context))[:sections]
+                for index in range(sections):
+                    out_rows[index] = placed(ready[index], index)
+        if layer == 1:
+            grad_proj, mlp_parts = lax.optimization_barrier((grad_proj, mlp_parts))
+            mlp_sums[1] = dp_sum(mlp_parts)[0]
+        else:
+            grad_proj, attn_parts = lax.optimization_barrier((grad_proj, attn_parts))
+        with jax.named_scope(f"B{layer}wattn"):
+            grad_attn_w = mm(joined(inputs), grad_proj, TN, bf16)
+            grad_out_w = mm(context, joined(grad_attn), TN, bf16)
+            pack = jnp.concatenate([grad_attn_w, grad_out_w.reshape(width, -1)], 1)
+        if layer == 0:
+            grad_proj = after(grad_proj, pack)
+        grad_low = []
+        grad_proj_parts = cut(grad_proj)
+        if layer == 0:
+            *grad_proj_parts[-1], mlp_sums[0] = lax.optimization_barrier(
+                (*grad_proj_parts[-1], mlp_sums[0])
+            )
+        with jax.named_scope(f"B{layer}in"):
+            sums = scatter_all(
                 [
-                    (mm(piece, down_w, NT) * slope.astype(f32)).astype(bf16)
-                    for piece, slope in zip(grad_mlp[p], slopes[p])
-                ]
+                    scatter_begin(
+                        [mm(piece, attn_w, NT) for piece in part],
+                        (),
+                    )
+                    for part in grad_proj_parts
+                ],
+                split_attn,
             )
-            grad_hidden = scatter([mm(piece, up_w, NT) for piece in grad_up[p]], split_mlp) + grad_two
-            grad_one, sums = norm_backward(grad_hidden, *norms_one[p], gains[0])
-            sums_one = sums_one + sums
-            grads_one.append(grad_one)
-            grad_attn.append(gather(grad_one.astype(bf16), split_attn))
-            grad_context.append([mm(piece, out_w, NT, bf16) for piece in grad_attn[p]])
-        norm_sums[layer] = jnp.stack([sums_one, sums_two])
-        grad_mlp, grad_up = joined(grad_mlp), joined(grad_up)
-        grad_down_w = mm(joined(acts), grad_mlp, TN, bf16)
-        grad_up_w = mm(joined(hidden_rows), grad_up, TN, bf16)
-        mlp_terms = (to_owner(grad_up_w, split_mlp), to_owner(grad_down_w, split_mlp))
-        dp_sum(layer, (2, 3), mlp_terms)
-        grad_proj = attend_back(flat(proj), context, log_sums, flat(grad_context), info, plan)
-        grad_attn_w = mm(joined(inputs), grad_proj, TN, bf16)
-        grad_out_w = mm(context, joined(grad_attn), TN, bf16)
-        attn_terms = (to_owner(grad_attn_w, split_attn), to_owner(grad_out_w, split_attn))
-        dp_sum(layer, (0, 1), attn_terms)
+        for p in range(parts):
+            with jax.named_scope(f"B{layer}in"):
+                value = gated(sums[p], grad_low[-1]) if p else sums[p]
+                grad_low.append((value + grads_one[p]).astype(bf16))
+        grad_out = [piece.astype(f32) for piece in grad_low]
         if layer == 0:
-            grad_proj = after(grad_proj, grad_attn_w)
-        grad_low = []
-        for p, part in enumerate(cut(grad_proj)):
-            grad_in = scatter([mm(piece, attn_w, NT) for piece in part], split_attn) + grads_one[p]
-            grad_low.append(grad_in.astype(bf16))
-        grad_out = [piece.astype(f32) for piece in grad_low]
-        input_grads[layer] = jnp.concatenate(grad_low, 0)
-
-    def pick(values):
-        return jnp.where(section == 0, values[0], values[1])
-
-    def placed_rows(chunks):
-        result = []
-        for index in range(micro):
-            arrived = []
-            for layer in range(sections):
-                moved = route(chunks[layer], lambda s, a, b: (layer, s, b) if a == index else None)
-                stays = (section == layer) & ByLane.home & (row == index)
-                arrived.append(jnp.where(stays, chunks[layer], moved))
-            result.append(pick(arrived))
-        return jnp.stack(result)[None, :, None]
-
-    def placed_weight(index, split):
-        terms = [weight_sums[layer][index] for layer in range(sections)]
+            with jax.named_scope("B0wattn"):
+                last_parts = send_attn(pack, ())
+                attn_sums[1], attn_sums[0] = dp_sum(attn_parts, last_parts)
+        with jax.named_scope("GRADROWS"):
+            grad_rows[layer] = placed(jnp.concatenate(grad_low, 0), layer)
+
+    def stacked_rows(by_layer):
+        return jnp.stack([pick([by_layer[0][m], by_layer[1][m]]) for m in range(micro)])[None, :, None]
+
+    def placed_weight(terms, split):
         mine = pick(terms)
         theirs = other_core(pick(terms[::-1]))
         first = jnp.where(split.home, mine, theirs)
         second = jnp.where(split.home, theirs, mine)
-        return jnp.concatenate([first, second], 0).astype(f32)
+        return first.astype(f32), second.astype(f32)
 
     def dp_butterfly(value, combine):
         if copies & (copies - 1):
@@ -958,18 +1121,27 @@
             distance *= 2
         return value
 
-    norm_sum = pick(norm_sums) + other_core(pick(norm_sums[::-1]))
-    if crossed:
-        norm_sum = norm_sum + other_row(norm_sum)
-        norm_sum = norm_sum + other_lane(norm_sum)
-    else:
-        norm_sum = lax.psum(norm_sum, "tensor")
-    norm_sum = dp_butterfly(norm_sum, jnp.add)
-
-    peak_all = jnp.stack(peaks)
-    peak_all = jnp.maximum(peak_all, other_row(peak_all))
-    peak_all = dp_butterfly(peak_all, jnp.maximum)
-    peak_here = jnp.where(ByLane.home, pick(peak_all), other_core(pick(peak_all[::-1])))
+    with jax.named_scope("NORMSUM"):
+        mine = [
+            jnp.stack([sum(sums_one[1:], sums_one[0]), sum(sums_two[1:], sums_two[0])])
+            for sums_one, sums_two in norm_sums
+        ]
+        mine = lax.optimization_barrier((*mine, last_parts))[:sections]
+        norm_sum = pick(mine) + other_core(pick(mine[::-1]))
+        if crossed:
+            norm_sum = norm_sum + other_row(norm_sum)
+            norm_sum = norm_sum + other_lane(norm_sum)
+        else:
+            norm_sum = lax.psum(norm_sum, "tensor")
+        norm_sum = dp_butterfly(norm_sum, jnp.add)
+    with jax.named_scope("PEAK"):
+        peak_all = lax.optimization_barrier((*flat(peaks), last_parts))[:-1]
+        peak_all = jnp.stack(
+            [jnp.max(value.reshape(heads, -1), 1) for value in peak_all]
+        ).reshape(sections, 2, heads)
+        peak_all = jnp.maximum(peak_all, other_row(peak_all))
+        peak_all = dp_butterfly(peak_all, jnp.maximum)
+        peak_here = jnp.where(ByLane.home, pick(peak_all), other_core(pick(peak_all[::-1])))
     factors = jnp.sqrt(clip_limit / jnp.maximum(peak_here, clip_limit))
     columns = jnp.repeat(factors, HEAD, axis=1)
     attn_local = w_attn[0].astype(f32)
@@ -982,13 +1154,28 @@
         ],
         1,
     )
+    out_rows, grad_rows = stacked_rows(out_rows), stacked_rows(grad_rows)
+    grad_up_w, grad_down_w = placed_weight(mlp_sums, split_mlp)
+    attn_sums = [
+        gated(term, out_rows, grad_rows, grad_up_w, grad_down_w, norm_sum, clipped)
+        for term in attn_sums
+    ]
+    mine, theirs = pick(attn_sums), other_core(pick(attn_sums[::-1]))
+    blocks, each = w_attn.shape[2:]
+    home = split_attn.home.astype(jnp.int32).reshape(1)
+    grad_attn_w = unpack(home, mine, theirs, blocks, each).transpose(1, 0, 2)
+    halves = [half[:, blocks * each :].reshape(-1, w_out.shape[2]) for half in (mine, theirs)]
+    grad_out_w = jnp.where(
+        split_attn.home, jnp.concatenate(halves, 0), jnp.concatenate(halves[::-1], 0)
+    ).astype(f32)
+
     return (
-        placed_rows(outputs),
-        placed_rows(input_grads),
-        placed_weight(0, split_attn).reshape(1, width, 6, -1),
-        placed_weight(1, split_attn)[None],
-        placed_weight(2, split_mlp)[None],
-        placed_weight(3, split_mlp)[None],
+        out_rows,
+        grad_rows,
+        grad_attn_w[None],
+        grad_out_w.reshape(w_out.shape),
+        grad_up_w.reshape(w_up.shape),
+        grad_down_w.reshape(w_down.shape),
         norm_sum[:, 0][None],
         norm_sum[:, 1][None],
         clipped[None],

time: 1170 us -> 1080 us (0.923)
  waiting for transfers between devices: 366 us -> 305 us
  starting transfers between devices: 233 us -> 174 us
  between operations: 17.4 us -> 44.3 us
  matrix products: 173 us -> 155 us
  other arithmetic: 120 us -> 135 us
    ppermute x77 -> x63, waiting for transfers between devices: 307 us -> 186 us  [route(): return lax.ppermute(value, joint, pairs)]
    psum x4 -> x3, waiting for transfers between devices: 49.8 us -> 102 us  [dp_sum(): earlier = lax.psum(tuple(terms), 'dp')]
    ppermute x71 -> x69, starting transfers between devices: 87.4 us -> 37.3 us  [other_core(): return lax.ppermute(value, 'section', [(0, 1), (1, 0)])]
    dot_general x72, matrix products: 173 us -> 155 us  [mm(): lax.dot_general(left, right, dims, preferred_element_type=jnp.float32)]
    slice x34 -> x82, local copies, waits for them, and re-layouts: 17.7 us -> 35 us  [the longest x41 24.8 us: gated(): corner = lax.slice(other, (0,) * other.ndim, (1,) * other.ndim)]
    ppermute x77 -> x63, starting transfers between devices: 132 us -> 116 us  [route(): return lax.ppermute(value, joint, pairs)]
    unnamed x362 -> x352, local copies, waits for them, and re-layouts: 46.6 us -> 34 us
    convert_element_type x22 -> x23, other arithmetic: 23.1 us -> 26.6 us  [the longest x3 13.8 us: gated(): return (value.astype(jnp.float32) + zero).astype(value.dtype)]
  transfers between devices with their start and end apart: 156 -> 139, of which waited for: 48 -> 44; matrix products, arithmetic and copies ran while one was open for 29% -> 31% of each run, Pallas kernels for 15% -> 14%
where the time goes in v2:
time: 1080 us; the launch traced here: 1070 us
  waiting for transfers between devices  305 us (28%)
  starting transfers between devices  174 us (16%)
  Pallas kernels  161 us (15%)
  matrix products  155 us (14%)
  other arithmetic  135 us (12%)
  local copies, waits for them, and re-layouts  90.8 us (8%)
  between operations  44.3 us (4%)
    ppermute x63, waiting for transfers between devices, route(): return lax.ppermute(value, joint, pairs)  186 us
    dot_general x72, matrix products, mm(): lax.dot_general(left, right, dims, preferred_element_type=jnp.float32)  155 us
    ppermute x63, starting transfers between devices, route(): return lax.ppermute(value, joint, pairs)  116 us
    psum x3, waiting for transfers between devices, dp_sum(): earlier = lax.psum(tuple(terms), 'dp')  102 us
    pallas_call x2, Pallas kernels, attend_back(): pl.pallas_call(partial(attend_back_kernel, heads, plan, (len(proj), len(g...  94.4 us
    pallas_call x2, Pallas kernels, attend(): pl.pallas_call(partial(attend_kernel, heads, plan, len(proj)), out_shape=...  58.2 us
    ppermute x69, starting transfers between devices, other_core(): return lax.ppermute(value, 'section', [(0, 1), (1, 0)])  37.3 us
    unnamed x352, local copies, waits for them, and re-layouts  34 us
  transfers between devices with their start and end apart: 139, of which 44 were waited for; matrix products, arithmetic and copies ran while one was open for 31% of the time, Pallas kernels for 14%

profile of v2, /device:TPU:0, one launch (start us, length us, event | category | flops | bytes accessed | tf_op | source)
XLA Modules:
  0.0 1065.3 jit_solution(896954973227172324)
XLA Ops:
  111.5 29.1 %attend.2 = (bf16[2048,256]{1,0:T(8,128)(2,1)}, f32[4,2048]{1,0:T(4,128)}, f32[1,128]{1,0:T(1,128)}, f32[1,1024]{1,0:T(1,128)}, f32[1,128]{1,0:T(1,128)}) custom-call(s32[2]{0:T(128)} %pad_add_fusion.order_ref, s32[8]{0:T(128)} %get-tuple-element.73.first_ref, s32[8]{0:T(128)} %get-tuple-element.74.last_ref, ...), custom_call_target="tpu_custom_call" | custom-call | flops 10737418240 | bytes 7340032 | tf_op jit(solution)/shard_map/attend/pallas_call | solution.py:277
  163.8 10.8 %collective-permute-done.17 = bf16[256,1024]{1,0:T(8,128)(2,1)S(1)} collective-permute-done((bf16[256,1024]{1,0:T(8,128)(2,1)S(1)}, bf16[256,1024]{1,0:T(8,128)(2,1)S(1)}, u32[]{:S(2)}, u32[]{:S(2)}) %collective-permute-start.17) | collective-permute-done | bytes 524320 | tf_op jit(solution)/shard_map/F0out/shop/ppermute | solution.py:721
  177.3 7.7 collective-permute-done.26
  226.9 10.2 collective-permute-done.35
  247.0 9.1 collective-permute-done.38
  283.5 29.2 %attend.3 = (bf16[2048,256]{1,0:T(8,128)(2,1)}, f32[4,2048]{1,0:T(4,128)}, f32[1,128]{1,0:T(1,128)}, f32[1,1024]{1,0:T(1,128)}, f32[1,128]{1,0:T(1,128)}) custom-call(s32[2]{0:T(128)} %pad_add_fusion.order_ref, s32[8]{0:T(128)} %get-tuple-element.73.first_ref, s32[8]{0:T(128)} %get-tuple-element.74.last_ref, ...), custom_call_target="tpu_custom_call" | custom-call | flops 10737418240 | bytes 7340032 | tf_op jit(solution)/shard_map/attend/pallas_call | solution.py:277
  326.5 11.0 %collective-permute-done.45 = bf16[256,1024]{1,0:T(8,128)(2,1)S(1)} collective-permute-done((bf16[256,1024]{1,0:T(8,128)(2,1)S(1)}, bf16[256,1024]{1,0:T(8,128)(2,1)S(1)}, u32[]{:S(2)}, u32[]{:S(2)}) %collective-permute-start.45) | collective-permute-done | bytes 524320 | tf_op jit(solution)/shard_map/F1out/shop/ppermute | solution.py:721
  362.4 8.3 collective-permute-done.55
  382.1 10.0 collective-permute-done.54
  404.8 9.3 collective-permute-done.63
  425.9 9.3 collective-permute-done.67
  442.5 8.1 fusion.75
  479.2 9.8 collective-permute-done.77
  519.1 47.1 %attend_back.2 = bf16[2048,1536]{1,0:T(8,128)(2,1)} custom-call(s32[2]{0:T(128)} %pad_add_fusion.order_ref, s32[8]{0:T(128)} %get-tuple-element.73.first_ref, s32[8]{0:T(128)} %get-tuple-element.74.last_ref, bf16[512,1536]{1,0:T(8,128)(2,1)} %convolution_convert_fusion.5.refs_0_, bf16[512,1536]{1,0:T(8,128)(2,1)} %convolution_convert_fusion.4.refs_1_, ...), custom_call_target="tpu_custom_call" | custom-call | flops 2147483648 | bytes 2097152 | tf_op jit(solution)/shard_map/attend_back/pallas_call | solution.py:543
  635.5 9.7 collective-permute-done.97
  684.1 8.5 convolution_convert_fusion.1
  733.2 9.8 collective-permute-done.109
  747.5 47.3 %attend_back.3 = bf16[2048,1536]{1,0:T(8,128)(2,1)} custom-call(s32[2]{0:T(128)} %pad_add_fusion.order_ref, s32[8]{0:T(128)} %get-tuple-element.73.first_ref, s32[8]{0:T(128)} %get-tuple-element.74.last_ref, bf16[512,1536]{1,0:T(8,128)(2,1)} %convolution_convert_fusion.9.refs_0_, bf16[512,1536]{1,0:T(8,128)(2,1)} %convolution_convert_fusion.8.refs_1_, ...), custom_call_target="tpu_custom_call" | custom-call | flops 2147483648 | bytes 2097152 | tf_op jit(solution)/shard_map/attend_back/pallas_call | solution.py:543
  798.4 8.9 convolution_convert_fusion
  823.1 20.3 %all-reduce.7.cloned.1.call-done = bf16[1024,1024]{1,0:T(8,128)(2,1)} async-done(((bf16[1024,1024]{1,0:T(8,128)(2,1)}), bf16[1024,1024]{1,0:T(8,128)(2,1)}) %all-reduce.7.cloned.1.call-update) | async-done | bytes 2097168 | tf_op jit(solution)/shard_map/psum | solution.py:971
  880.3 17.9 %collective-permute-start.133 = (f32[2,2,4]{2,1,0:T(2,128)S(1)}, f32[2,2,4]{2,1,0:T(2,128)S(1)}, u32[]{:S(2)}, u32[]{:S(2)}) collective-permute-start(f32[2,2,4]{2,1,0:T(2,128)S(1)} %max.17), channel_id=1, source_target_pairs={{0,8},{4,12},{8,0},{12,4},{1,9},{5,13},{9,1},{13,5},{2,10},{6,14},... | collective-permute-start | bytes 200 | tf_op jit(solution)/shard_map/PEAK/ppermute | solution.py:1120
  924.7 14.8 %slice_multiply_fusion.2 = (f32[1024,1,256]{2,1,0:T(1,128)}, f32[1024,1,256]{2,1,0:T(1,128)S(1)}, f32[1024,1,256]{2,1,0:T(1,128)}, f32[1024,1,256]{2,1,0:T(1,128)}) fusion(f32[1024,6,256]{2,1,0:T(8,128)} %bitcast_convert_fusion, f32[256]{0:T(256)S(1)} %broadcast_in_dim.52, f32[256]{0:T(256)S(1)} %broadcast_in_dim.55), kind=kLoop, calls=%fused_computation.195 | loop fusion | flops 1048576 | bytes 8390656 | tf_op jit(solution)/shard_map/mul | solution.py:1151
  953.4 81.9 %all-reduce.9.cloned.1.call-done = (bf16[512,1792]{1,0:T(8,128)(2,1)}, bf16[512,1792]{1,0:T(8,128)(2,1)}) async-done(((bf16[512,1792]{1,0:T(8,128)(2,1)}, bf16[512,1792]{1,0:T(8,128)(2,1)}), (bf16[512,1792]{1,0:T(8,128)(2,1)}, bf16[512,1792]{1,0:T(8,128)(2,1)})) %all-reduce.9.cloned.1.call-update) | async-done | bytes 3670032 | tf_op jit(solution)/shard_map/B0wattn/psum | solution.py:971
  1050.5 8.0 unpack.1
  (962 shorter events, 584.9 us)
Async XLA Ops:
  7.2 702.9 %all-reduce.5.cloned.1.call-start = ((), (), s32[]{:S(2)}) async-start(), calls=%async_computation | async-start | bytes 4194304 | tf_op jit(solution)/shard_map/psum | solution.py:971
  18.7 57.7 %collective-permute-start.2 = (bf16[1024,1536]{0,1:T(8,128)(2,1)S(1)}, bf16[1024,1536]{0,1:T(8,128)(2,1)}, u32[]{:S(2)}, u32[]{:S(2)}) collective-permute-start(bf16[1024,1536]{0,1:T(8,128)(2,1)S(1)} %bitcast.189), channel_id=1, source_target_pairs={{0,2},{1,3},{2,16},{3,17},{4,6},{5,7},{6,20},{7,21},{8,10},{9,11},... | collective-permute-start | bytes 9437192 | tf_op jit(solution)/shard_map/W0attn/ppermute | solution.py:721
  21.7 54.7 %collective-permute-start.1 = (bf16[1024,1536]{0,1:T(8,128)(2,1)S(1)}, bf16[1024,1536]{0,1:T(8,128)(2,1)}, u32[]{:S(2)}, u32[]{:S(2)}) collective-permute-start(bf16[1024,1536]{0,1:T(8,128)(2,1)S(1)} %bitcast.190), channel_id=1, source_target_pairs={{2,18},{3,19},{6,22},{7,23},{10,26},{11,27},{14,30},{15,31}} | collective-permute-start | bytes 9437192 | tf_op jit(solution)/shard_map/W0attn/ppermute | solution.py:721
  95.5 45.1 %collective-permute-start.14 = (bf16[1024,1792]{0,1:T(8,128)(2,1)}, bf16[1024,1792]{0,1:T(8,128)(2,1)}, u32[]{:S(2)}, u32[]{:S(2)}) collective-permute-start(bf16[1024,1792]{0,1:T(8,128)(2,1)} %pad_maximum_fusion.2), channel_id=1, source_target_pairs={{16,2},{17,3},{18,16},{19,17},{20,6},{21,7},{22,20},{23,21},{24,10... | collective-permute-start | bytes 11010056 | tf_op jit(solution)/shard_map/W1attn/ppermute | solution.py:721
  98.1 42.6 %collective-permute-start.13 = (bf16[1024,1792]{0,1:T(8,128)(2,1)}, bf16[1024,1792]{0,1:T(8,128)(2,1)}, u32[]{:S(2)}, u32[]{:S(2)}) collective-permute-start(bf16[1024,1792]{0,1:T(8,128)(2,1)} %pad_maximum_fusion.2), channel_id=1, source_target_pairs={{16,0},{17,1},{20,4},{21,5},{24,8},{25,9},{28,12},{29,13}} | collective-permute-start | bytes 11010056 | tf_op jit(solution)/shard_map/W1attn/ppermute | solution.py:721
  99.3 49.5 %collective-permute-start.12 = (bf16[1024,2048]{1,0:T(8,128)(2,1)}, bf16[1024,2048]{1,0:T(8,128)(2,1)}, u32[]{:S(2)}, u32[]{:S(2)}) collective-permute-start(bf16[1024,2048]{1,0:T(8,128)(2,1)} %pad_maximum_fusion.1), channel_id=1, source_target_pairs={{0,1},{1,16},{2,3},{3,18},{4,5},{5,20},{6,7},{7,22},{8,9},{9,24},{... | collective-permute-start | bytes 12582920 | tf_op jit(solution)/shard_map/W0mlp/ppermute | solution.py:721
  104.6 44.3 %collective-permute-start.11 = (bf16[1024,2048]{1,0:T(8,128)(2,1)}, bf16[1024,2048]{1,0:T(8,128)(2,1)}, u32[]{:S(2)}, u32[]{:S(2)}) collective-permute-start(bf16[1024,2048]{1,0:T(8,128)(2,1)} %pad_maximum_fusion.1), channel_id=1, source_target_pairs={{1,17},{3,19},{5,21},{7,23},{9,25},{11,27},{13,29},{15,31}} | collective-permute-start | bytes 12582920 | tf_op jit(solution)/shard_map/W0mlp/ppermute | solution.py:721
  265.1 47.6 %collective-permute-start.41 = (bf16[1024,2048]{1,0:T(8,128)(2,1)}, bf16[1024,2048]{1,0:T(8,128)(2,1)}, u32[]{:S(2)}, u32[]{:S(2)}) collective-permute-start(bf16[1024,2048]{1,0:T(8,128)(2,1)} %pad_maximum_fusion.1), channel_id=1, source_target_pairs={{16,1},{17,16},{18,3},{19,18},{20,5},{21,20},{22,7},{23,22},{24,9}... | collective-permute-start | bytes 12582920 | tf_op jit(solution)/shard_map/W1mlp/ppermute | solution.py:721
  267.9 44.8 %collective-permute-start.40 = (bf16[1024,2048]{1,0:T(8,128)(2,1)}, bf16[1024,2048]{1,0:T(8,128)(2,1)}, u32[]{:S(2)}, u32[]{:S(2)}) collective-permute-start(bf16[1024,2048]{1,0:T(8,128)(2,1)} %pad_maximum_fusion.1), channel_id=1, source_target_pairs={{16,0},{18,2},{20,4},{22,6},{24,8},{26,10},{28,12},{30,14}} | collective-permute-start | bytes 12582920 | tf_op jit(solution)/shard_map/W1mlp/ppermute | solution.py:721
  495.3 75.6 %collective-permute-start.84 = (bf16[1024,1024]{1,0:T(8,128)(2,1)}, bf16[1024,1024]{1,0:T(8,128)(2,1)}, u32[]{:S(2)}, u32[]{:S(2)}) collective-permute-start(bf16[1024,1024]{1,0:T(8,128)(2,1)} %fusion.81), channel_id=1, source_target_pairs={{1,16},{3,18},{16,1},{18,3},{5,20},{7,22},{20,5},{22,7},{9,24},{11... | collective-permute-start | bytes 6291464 | tf_op jit(solution)/shard_map/B1wmlp/ppermute | solution.py:721
  506.0 64.9 %collective-permute-start.83 = (bf16[1024,1024]{1,0:T(8,128)(2,1)}, bf16[1024,1024]{1,0:T(8,128)(2,1)}, u32[]{:S(2)}, u32[]{:S(2)}) collective-permute-start(bf16[1024,1024]{1,0:T(8,128)(2,1)} %add_convert_fusion.3), channel_id=1, source_target_pairs={{0,16},{1,0},{2,18},{3,2},{16,17},{17,1},{18,19},{19,3},{4,20},{5,... | collective-permute-start | bytes 6291464 | tf_op jit(solution)/shard_map/B1wmlp/ppermute | solution.py:721
  506.9 59.3 %collective-permute-start.79 = (bf16[512,1024]{1,0:T(8,128)(2,1)}, bf16[512,1024]{1,0:T(8,128)(2,1)}, u32[]{:S(2)}, u32[]{:S(2)}) collective-permute-start(bf16[512,1024]{1,0:T(8,128)(2,1)} %pad_maximum_fusion.7), channel_id=1, source_target_pairs={{16,2},{17,3},{20,6},{21,7},{24,10},{25,11},{28,14},{29,15}} | collective-permute-start | bytes 3145736 | tf_op jit(solution)/shard_map/OUTROWS/ppermute | solution.py:721
  508.6 57.7 %collective-permute-start.82 = (bf16[512,1024]{1,0:T(8,128)(2,1)}, bf16[512,1024]{1,0:T(8,128)(2,1)}, u32[]{:S(2)}, u32[]{:S(2)}) collective-permute-start(bf16[512,1024]{1,0:T(8,128)(2,1)} %pad_maximum_fusion.9), channel_id=1, source_target_pairs={{2,16},{3,17},{6,20},{7,21},{10,24},{11,25},{14,28},{15,29}} | collective-permute-start | bytes 3145736 | tf_op jit(solution)/shard_map/OUTROWS/ppermute | solution.py:721
  510.2 56.1 %collective-permute-start.80 = (bf16[512,1024]{1,0:T(8,128)(2,1)}, bf16[512,1024]{1,0:T(8,128)(2,1)}, u32[]{:S(2)}, u32[]{:S(2)}) collective-permute-start(bf16[512,1024]{1,0:T(8,128)(2,1)} %pad_maximum_fusion.9), channel_id=1, source_target_pairs={{0,16},{1,17},{16,18},{17,19},{4,20},{5,21},{20,22},{21,23},{8,24}... | collective-permute-start | bytes 3145736 | tf_op jit(solution)/shard_map/OUTROWS/ppermute | solution.py:721
  595.4 248.1 %all-reduce.7.cloned.1.call-start = ((), (), s32[]{:S(2)}) async-start(), calls=%async_computation.1 | async-start | bytes 4194304 | tf_op jit(solution)/shard_map/psum | solution.py:971
  719.2 75.6 %collective-permute-start.111 = (bf16[512,1792]{1,0:T(8,128)(2,1)}, bf16[512,1792]{1,0:T(8,128)(2,1)}, u32[]{:S(2)}, u32[]{:S(2)}) collective-permute-start(bf16[512,1792]{1,0:T(8,128)(2,1)} %get-tuple-element.215), channel_id=1, source_target_pairs={{0,16},{1,17},{2,0},{3,1},{16,18},{17,19},{18,2},{19,3},{4,20},{5,... | collective-permute-start | bytes 5505032 | tf_op jit(solution)/shard_map/B1wattn/ppermute | solution.py:721
  719.2 75.6 %collective-permute-start.112 = (bf16[512,1792]{1,0:T(8,128)(2,1)}, bf16[512,1792]{1,0:T(8,128)(2,1)}, u32[]{:S(2)}, u32[]{:S(2)}) collective-permute-start(bf16[512,1792]{1,0:T(8,128)(2,1)} %get-tuple-element.216), channel_id=1, source_target_pairs={{2,16},{3,17},{16,2},{17,3},{6,20},{7,21},{20,6},{21,7},{10,24},{1... | collective-permute-start | bytes 5505032 | tf_op jit(solution)/shard_map/B1wattn/ppermute | solution.py:721
  722.3 219.6 %collective-permute-start.122 = (bf16[512,1024]{1,0:T(8,128)(2,1)}, bf16[512,1024]{1,0:T(8,128)(2,1)}, u32[]{:S(2)}, u32[]{:S(2)}) collective-permute-start(bf16[512,1024]{1,0:T(8,128)(2,1)} %pad_maximum_fusion.11), channel_id=1, source_target_pairs={{2,16},{3,17},{6,20},{7,21},{10,24},{11,25},{14,28},{15,29}} | collective-permute-start | bytes 3145736 | tf_op jit(solution)/shard_map/GRADROWS/ppermute | solution.py:721
  728.6 213.3 %collective-permute-start.120 = (bf16[512,1024]{1,0:T(8,128)(2,1)}, bf16[512,1024]{1,0:T(8,128)(2,1)}, u32[]{:S(2)}, u32[]{:S(2)}) collective-permute-start(bf16[512,1024]{1,0:T(8,128)(2,1)} %pad_maximum_fusion.11), channel_id=1, source_target_pairs={{0,16},{1,17},{16,18},{17,19},{4,20},{5,21},{20,22},{21,23},{8,24}... | collective-permute-start | bytes 3145736 | tf_op jit(solution)/shard_map/GRADROWS/ppermute | solution.py:721
  747.4 287.8 %all-reduce.9.cloned.1.call-start = ((), (), s32[]{:S(2)}) async-start(), calls=%async_computation.2 | async-start | bytes 7340032 | tf_op jit(solution)/shard_map/B0wattn/psum | solution.py:971
  812.7 42.3 %collective-permute-start.123 = (bf16[512,1792]{1,0:T(8,128)(2,1)}, bf16[512,1792]{1,0:T(8,128)(2,1)}, u32[]{:S(2)}, u32[]{:S(2)}) collective-permute-start(bf16[512,1792]{1,0:T(8,128)(2,1)} %get-tuple-element.207), channel_id=1, source_target_pairs={{0,16},{1,17},{2,0},{3,1},{16,18},{17,19},{18,2},{19,3},{4,20},{5,... | collective-permute-start | bytes 5505032 | tf_op jit(solution)/shard_map/B0wattn/ppermute | solution.py:721
  813.2 43.3 %collective-permute-start.124 = (bf16[512,1792]{1,0:T(8,128)(2,1)}, bf16[512,1792]{1,0:T(8,128)(2,1)}, u32[]{:S(2)}, u32[]{:S(2)}) collective-permute-start(bf16[512,1792]{1,0:T(8,128)(2,1)} %get-tuple-element.208), channel_id=1, source_target_pairs={{2,16},{3,17},{16,2},{17,3},{6,20},{7,21},{20,6},{21,7},{10,24},{1... | collective-permute-start | bytes 5505032 | tf_op jit(solution)/shard_map/B0wattn/ppermute | solution.py:721
  819.2 49.2 %collective-permute-start.113 = (bf16[256,1024]{1,0:T(8,128)(2,1)}, bf16[256,1024]{1,0:T(8,128)(2,1)}, u32[]{:S(2)}, u32[]{:S(2)}) collective-permute-start(bf16[256,1024]{1,0:T(8,128)(2,1)} %slice.1245), channel_id=1, source_target_pairs={{0,16},{16,0},{1,17},{17,1},{2,18},{18,2},{3,19},{19,3},{4,20},{20... | collective-permute-start | bytes 1572872 | tf_op jit(solution)/shard_map/B0in/ssec2/ppermute | solution.py:724
  860.3 56.0 %collective-permute-start.117 = (bf16[256,1024]{1,0:T(8,128)(2,1)}, bf16[256,1024]{1,0:T(8,128)(2,1)}, u32[]{:S(2)}, u32[]{:S(2)}) collective-permute-start(bf16[256,1024]{1,0:T(8,128)(2,1)} %slice.1242), channel_id=1, source_target_pairs={{0,16},{16,0},{1,17},{17,1},{2,18},{18,2},{3,19},{19,3},{4,20},{20... | collective-permute-start | bytes 1572872 | tf_op jit(solution)/shard_map/B0in/ssec2/ppermute | solution.py:724
  (269 other events, 3625.1 us)
Sparse Core Ops, SparseCore 0:
  595.4 98.5 all-reduce.4
  747.6 95.8 all-reduce.6
  898.4 136.8 all-reduce.8

commit v3 on v2

--- a/solution.py
+++ b/solution.py
@@ -679,6 +679,29 @@
     )(home, mine, theirs)
 
 
+def clip_kernel(kept, weight_ref, factor_ref, out_ref):
+    for index, block in enumerate(kept):
+        out_ref[:, index, :] = weight_ref[block].astype(jnp.float32) * factor_ref[index // 2]
+
+
+def clip_weights(weight, factors):
+    blocks, length, each = weight.shape
+    kept = (0, 1, 3, 4)
+    tile = min(128, length)
+    return pl.pallas_call(
+        partial(clip_kernel, kept),
+        out_shape=jax.ShapeDtypeStruct((length, len(kept), each), jnp.float32),
+        grid=(length // tile,),
+        in_specs=[
+            pl.BlockSpec((blocks, tile, each), lambda step: (0, step, 0)),
+            pl.BlockSpec((2, 1, each), lambda step: (0, 0, 0)),
+        ],
+        out_specs=pl.BlockSpec((tile, len(kept), each), lambda step: (step, 0, 0)),
+        compiler_params=pltpu.CompilerParams(dimension_semantics=("arbitrary",)),
+        name="clip_weights",
+    )(weight, factors)
+
+
 def gated(value, *others):
     zero = 0.0
     for other in others:
@@ -836,8 +859,10 @@
         def within(s, a, b):
             return (split.keeper(s, a, b), a, b) if s == layer else None
 
-        far = route(weight, across)
-        near = route(weight, within)
+        return route(weight, within), route(weight, across)
+
+    def chosen(weight, arrived, layer, split):
+        near, far = arrived
         return jnp.where(split.home, jnp.where(section == layer, weight, near), far)
 
     attn_table = w_attn[0].reshape(width, -1)
@@ -860,10 +885,9 @@
         hops = part_rows(jnp.where(ByLane.home, early, late))
     attn_weights = [None] * sections
     mlp_weights = [None] * sections
+    attn_pack = jnp.concatenate([attn_table, w_out[0].reshape(width, -1)], 1)
     with jax.named_scope("W0attn"):
-        first_weight = fetch(attn_table, 0, split_attn)
-    with jax.named_scope("W0out"):
-        second_weight = fetch(after(w_out[0], *hops), 0, split_attn)
+        first_pack = chosen(attn_pack, fetch(attn_pack, 0, split_attn), 0, split_attn)
     with jax.named_scope("W0mlp"):
         arriving = fetch(after(mlp_pack, *own, *hops), 0, split_mlp)
 
@@ -872,11 +896,8 @@
     flags = lax.dynamic_index_in_dim(global_flags[:, 0], row, 0, False)
     order = jnp.stack([section, lane if crossed else jnp.zeros_like(lane)]).astype(jnp.int32)
     info = sequence_info(docs, flags, order, heads)
-    attn_pack = jnp.concatenate([attn_table, w_out[0].reshape(width, -1)], 1)
-    first_weight, second_weight, attn_pack, mlp_pack, *info = lax.optimization_barrier(
-        (first_weight, second_weight, attn_pack, mlp_pack, *info)
-    )
-    attn_weights[0] = (first_weight, second_weight)
+    first_pack, mlp_pack, *info = lax.optimization_barrier((first_pack, mlp_pack, *info))
+    attn_weights[0] = attn_unpack(first_pack)
 
     gains_own = jnp.stack([ln_gain[0], ln_bias[0]])
     gains_other = other_core(gains_own)
@@ -898,14 +919,15 @@
             with jax.named_scope("W1attn"):
                 pack = fetch(after(attn_pack, *flat(proj)), 1, split_attn)
             context, arriving, pack = lax.optimization_barrier((context, arriving, pack))
-            mlp_weights[0], attn_weights[1] = mlp_unpack(arriving), attn_unpack(pack)
+            mlp_weights[0] = mlp_unpack(chosen(mlp_pack, arriving, 0, split_mlp))
+            attn_weights[1] = attn_unpack(chosen(attn_pack, pack, 1, split_attn))
         else:
             with jax.named_scope("W1mlp"):
                 pack = fetch(after(mlp_pack, *flat(proj)), 1, split_mlp)
             with jax.named_scope("COT"):
                 mine, moved = own_rows(after(cotangent, *flat(proj)))
             context, pack, mine, moved = lax.optimization_barrier((context, pack, mine, moved))
-            mlp_weights[1] = mlp_unpack(pack)
+            mlp_weights[1] = mlp_unpack(chosen(mlp_pack, pack, 1, split_mlp))
             grad_out = part_rows(jnp.where(ByLane.home, mine, moved).astype(f32))
         up_w, down_w = mlp_weights[layer]
         with jax.named_scope(f"F{layer}out"):
@@ -1144,16 +1166,7 @@
         peak_here = jnp.where(ByLane.home, pick(peak_all), other_core(pick(peak_all[::-1])))
     factors = jnp.sqrt(clip_limit / jnp.maximum(peak_here, clip_limit))
     columns = jnp.repeat(factors, HEAD, axis=1)
-    attn_local = w_attn[0].astype(f32)
-    clipped = jnp.stack(
-        [
-            attn_local[:, 0] * columns[0][None, :],
-            attn_local[:, 1] * columns[0][None, :],
-            attn_local[:, 3] * columns[1][None, :],
-            attn_local[:, 4] * columns[1][None, :],
-        ],
-        1,
-    )
+    clipped = clip_weights(w_attn[0].transpose(1, 0, 2), columns[:, None, :])
     out_rows, grad_rows = stacked_rows(out_rows), stacked_rows(grad_rows)
     grad_up_w, grad_down_w = placed_weight(mlp_sums, split_mlp)
     attn_sums = [

time: 1080 us -> 1050 us (0.972)
  waiting for transfers between devices: 305 us -> 285 us
  other arithmetic: 135 us -> 121 us
  starting transfers between devices: 174 us -> 160 us
  local copies, waits for them, and re-layouts: 90.8 us -> 102 us
    psum x3, waiting for transfers between devices: 102 us -> 73.3 us  [dp_sum(): earlier = lax.psum(tuple(terms), 'dp')]
    ppermute x63 -> x61, starting transfers between devices: 116 us -> 99.3 us  [route(): return lax.ppermute(value, joint, pairs)]
    mul x1 -> x0, other arithmetic: 14.8 us -> none  [shards(): attn_local[:, 1] * columns[0][None, :]]
    ppermute x63 -> x61, waiting for transfers between devices: 186 us -> 199 us  [route(): return lax.ppermute(value, joint, pairs)]
    unnamed x352 -> x394, local copies, waits for them, and re-layouts: 34 us -> 39.1 us
  transfers between devices with their start and end apart: 139 -> 137, of which waited for: 44 -> 43; matrix products, arithmetic and copies ran while one was open for 31% -> 32% of each run, Pallas kernels for 14% -> 15%
where the time goes in v3:
time: 1050 us; the launch traced here: 1040 us
  waiting for transfers between devices  285 us (27%)
  Pallas kernels  167 us (16%)
  starting transfers between devices  160 us (15%)
  matrix products  156 us (15%)
  other arithmetic  121 us (12%)
  local copies, waits for them, and re-layouts  102 us (10%)
  between operations  44.9 us (4%)
    ppermute x61, waiting for transfers between devices, route(): return lax.ppermute(value, joint, pairs)  199 us
    dot_general x72, matrix products, mm(): lax.dot_general(left, right, dims, preferred_element_type=jnp.float32)  156 us
    ppermute x61, starting transfers between devices, route(): return lax.ppermute(value, joint, pairs)  99.3 us
    pallas_call x2, Pallas kernels, attend_back(): pl.pallas_call(partial(attend_back_kernel, heads, plan, (len(proj), len(g...  94.2 us
    psum x3, waiting for transfers between devices, dp_sum(): earlier = lax.psum(tuple(terms), 'dp')  73.3 us
    pallas_call x2, Pallas kernels, attend(): pl.pallas_call(partial(attend_kernel, heads, plan, len(proj)), out_shape=...  58.3 us
    ppermute x69, starting transfers between devices, other_core(): return lax.ppermute(value, 'section', [(0, 1), (1, 0)])  41.3 us
    unnamed x394, local copies, waits for them, and re-layouts  39.1 us
  transfers between devices with their start and end apart: 137, of which 43 were waited for; matrix products, arithmetic and copies ran while one was open for 32% of the time, Pallas kernels for 15%

profile of v3, /device:TPU:0, one launch (start us, length us, event | category | flops | bytes accessed | tf_op | source)
XLA Modules:
  0.0 1036.6 jit_solution(3556880734014491346)
XLA Ops:
  41.7 13.5 %collective-permute-done.4 = bf16[512,1024]{1,0:T(8,128)(2,1)} collective-permute-done((bf16[512,1024]{1,0:T(8,128)(2,1)}, bf16[512,1024]{1,0:T(8,128)(2,1)}, u32[]{:S(2)}, u32[]{:S(2)}) %collective-permute-start.4) | collective-permute-done | bytes 1048608 | tf_op jit(solution)/shard_map/ppermute | solution.py:744
  92.8 12.1 %collective-permute-start.11 = (bf16[1024,1792]{0,1:T(8,128)(2,1)}, bf16[1024,1792]{0,1:T(8,128)(2,1)}, u32[]{:S(2)}, u32[]{:S(2)}) collective-permute-start(bf16[1024,1792]{0,1:T(8,128)(2,1)} %pad_maximum_fusion.2), channel_id=1, source_target_pairs={{16,0},{17,1},{20,4},{21,5},{24,8},{25,9},{28,12},{29,13}} | collective-permute-start | bytes 11010056 | tf_op jit(solution)/shard_map/W1attn/ppermute | solution.py:744
  119.6 29.2 %attend.2 = (bf16[2048,256]{1,0:T(8,128)(2,1)}, f32[4,2048]{1,0:T(4,128)}, f32[1,128]{1,0:T(1,128)}, f32[1,1024]{1,0:T(1,128)}, f32[1,128]{1,0:T(1,128)}) custom-call(s32[2]{0:T(128)} %pad_add_fusion.order_ref, s32[8]{0:T(128)} %get-tuple-element.72.first_ref, s32[8]{0:T(128)} %get-tuple-element.73.last_ref, ...), custom_call_target="tpu_custom_call" | custom-call | flops 10737418240 | bytes 7340032 | tf_op jit(solution)/shard_map/attend/pallas_call | solution.py:277
  225.4 11.4 %collective-permute-done.33 = bf16[256,1024]{1,0:T(8,128)(2,1)S(1)} collective-permute-done((bf16[256,1024]{1,0:T(8,128)(2,1)S(1)}, bf16[256,1024]{1,0:T(8,128)(2,1)S(1)}, u32[]{:S(2)}, u32[]{:S(2)}) %collective-permute-start.33) | collective-permute-done | bytes 524320 | tf_op jit(solution)/shard_map/F1in/ghop/ppermute | solution.py:744
  273.2 29.2 %attend.3 = (bf16[2048,256]{1,0:T(8,128)(2,1)}, f32[4,2048]{1,0:T(4,128)}, f32[1,128]{1,0:T(1,128)}, f32[1,1024]{1,0:T(1,128)}, f32[1,128]{1,0:T(1,128)}) custom-call(s32[2]{0:T(128)} %pad_add_fusion.order_ref, s32[8]{0:T(128)} %get-tuple-element.72.first_ref, s32[8]{0:T(128)} %get-tuple-element.73.last_ref, ...), custom_call_target="tpu_custom_call" | custom-call | flops 10737418240 | bytes 7340032 | tf_op jit(solution)/shard_map/attend/pallas_call | solution.py:277
  305.3 12.9 %collective-permute-start.50 = (bf16[256,1024]{1,0:T(8,128)(2,1)S(1)}, bf16[256,1024]{1,0:T(8,128)(2,1)S(1)}, u32[]{:S(2)}, u32[]{:S(2)}) collective-permute-start(bf16[256,1024]{1,0:T(8,128)(2,1)S(1)} %slice.1246), channel_id=1, source_target_pairs={{0,16},{16,0},{1,17},{17,1},{2,18},{18,2},{3,19},{19,3},{4,20},{20... | collective-permute-start | bytes 1572872 | tf_op jit(solution)/shard_map/F1out/ssec2/ppermute | solution.py:747
  330.3 10.1 collective-permute-done.43
  363.9 9.8 collective-permute-done.53
  383.9 11.2 %collective-permute-done.52 = bf16[256,1024]{1,0:T(8,128)(2,1)S(1)} collective-permute-done((bf16[256,1024]{1,0:T(8,128)(2,1)S(1)}, bf16[256,1024]{1,0:T(8,128)(2,1)S(1)}, u32[]{:S(2)}, u32[]{:S(2)}) %collective-permute-start.52) | collective-permute-done | bytes 524320 | tf_op jit(solution)/shard_map/F1mlp/shop/ppermute | solution.py:744
  408.6 8.6 collective-permute-done.61
  428.9 9.3 collective-permute-done.65
  513.9 47.0 %attend_back.2 = bf16[2048,1536]{1,0:T(8,128)(2,1)} custom-call(s32[2]{0:T(128)} %pad_add_fusion.order_ref, s32[8]{0:T(128)} %get-tuple-element.72.first_ref, s32[8]{0:T(128)} %get-tuple-element.73.last_ref, bf16[512,1536]{1,0:T(8,128)(2,1)} %convolution_convert_fusion.5.refs_0_, bf16[512,1536]{1,0:T(8,128)(2,1)} %convolution_convert_fusion.4.refs_1_, ...), custom_call_target="tpu_custom_call" | custom-call | flops 2147483648 | bytes 2097152 | tf_op jit(solution)/shard_map/attend_back/pallas_call | solution.py:543
  622.9 9.7 collective-permute-done.95
  652.7 7.7 fusion.78
  672.4 8.5 convolution_convert_fusion.1
  713.1 18.2 %collective-permute-done.107 = bf16[1024,1024]{1,0:T(8,128)(2,1)} collective-permute-done((bf16[1024,1024]{1,0:T(8,128)(2,1)}, bf16[1024,1024]{1,0:T(8,128)(2,1)}, u32[]{:S(2)}, u32[]{:S(2)}) %collective-permute-start.107) | collective-permute-done | bytes 2097184 | tf_op jit(solution)/shard_map/B0wmlp/ppermute | solution.py:744
  735.8 47.3 %attend_back.3 = bf16[2048,1536]{1,0:T(8,128)(2,1)} custom-call(s32[2]{0:T(128)} %pad_add_fusion.order_ref, s32[8]{0:T(128)} %get-tuple-element.72.first_ref, s32[8]{0:T(128)} %get-tuple-element.73.last_ref, bf16[512,1536]{1,0:T(8,128)(2,1)} %convolution_convert_fusion.9.refs_0_, bf16[512,1536]{1,0:T(8,128)(2,1)} %convolution_convert_fusion.8.refs_1_, ...), custom_call_target="tpu_custom_call" | custom-call | flops 2147483648 | bytes 2097152 | tf_op jit(solution)/shard_map/attend_back/pallas_call | solution.py:543
  786.8 8.9 convolution_convert_fusion
  808.2 19.7 %all-reduce.7.cloned.1.call-done = bf16[1024,1024]{1,0:T(8,128)(2,1)} async-done(((bf16[1024,1024]{1,0:T(8,128)(2,1)}), bf16[1024,1024]{1,0:T(8,128)(2,1)}) %all-reduce.7.cloned.1.call-update) | async-done | bytes 2097168 | tf_op jit(solution)/shard_map/psum | solution.py:993
  843.6 9.8 collective-permute-start.124
  861.6 15.7 %collective-permute-start.130 = (f32[2,2,4]{2,1,0:T(2,128)S(1)}, f32[2,2,4]{2,1,0:T(2,128)S(1)}, u32[]{:S(2)}, u32[]{:S(2)}) collective-permute-start(f32[2,2,4]{2,1,0:T(2,128)S(1)} %max.16), channel_id=1, source_target_pairs={{0,4},{4,0},{8,12},{12,8},{1,5},{5,1},{9,13},{13,9},{2,6},{6,2},{1... | collective-permute-start | bytes 200 | tf_op jit(solution)/shard_map/PEAK/ppermute | solution.py:1142
  901.9 9.9 collective-permute-done.116
  957.6 53.7 %all-reduce.9.cloned.1.call-done = (bf16[512,1792]{1,0:T(8,128)(2,1)}, bf16[512,1792]{1,0:T(8,128)(2,1)}) async-done(((bf16[512,1792]{1,0:T(8,128)(2,1)}, bf16[512,1792]{1,0:T(8,128)(2,1)}), (bf16[512,1792]{1,0:T(8,128)(2,1)}, bf16[512,1792]{1,0:T(8,128)(2,1)})) %all-reduce.9.cloned.1.call-update) | async-done | bytes 3670032 | tf_op jit(solution)/shard_map/B0wattn/psum | solution.py:993
  1021.8 8.0 unpack.1
  (995 shorter events, 570.7 us)
Async XLA Ops:
  7.2 688.9 %all-reduce.5.cloned.1.call-start = ((), (), s32[]{:S(2)}) async-start(), calls=%async_computation | async-start | bytes 4194304 | tf_op jit(solution)/shard_map/psum | solution.py:993
  23.2 51.6 %collective-permute-start.2 = (bf16[1024,1792]{0,1:T(8,128)(2,1)}, bf16[1024,1792]{0,1:T(8,128)(2,1)}, u32[]{:S(2)}, u32[]{:S(2)}) collective-permute-start(bf16[1024,1792]{0,1:T(8,128)(2,1)} %pad_maximum_fusion.2), channel_id=1, source_target_pairs={{0,2},{1,3},{2,16},{3,17},{4,6},{5,7},{6,20},{7,21},{8,10},{9,11},... | collective-permute-start | bytes 11010056 | tf_op jit(solution)/shard_map/W0attn/ppermute | solution.py:744
  26.3 48.5 %collective-permute-start.1 = (bf16[1024,1792]{0,1:T(8,128)(2,1)}, bf16[1024,1792]{0,1:T(8,128)(2,1)}, u32[]{:S(2)}, u32[]{:S(2)}) collective-permute-start(bf16[1024,1792]{0,1:T(8,128)(2,1)} %pad_maximum_fusion.2), channel_id=1, source_target_pairs={{2,18},{3,19},{6,22},{7,23},{10,26},{11,27},{14,30},{15,31}} | collective-permute-start | bytes 11010056 | tf_op jit(solution)/shard_map/W0attn/ppermute | solution.py:744
  66.6 82.2 %collective-permute-start.10 = (bf16[1024,2048]{1,0:T(8,128)(2,1)}, bf16[1024,2048]{1,0:T(8,128)(2,1)}, u32[]{:S(2)}, u32[]{:S(2)}) collective-permute-start(bf16[1024,2048]{1,0:T(8,128)(2,1)} %pad_maximum_fusion.1), channel_id=1, source_target_pairs={{0,1},{1,16},{2,3},{3,18},{4,5},{5,20},{6,7},{7,22},{8,9},{9,24},{... | collective-permute-start | bytes 12582920 | tf_op jit(solution)/shard_map/W0mlp/ppermute | solution.py:744
  72.2 76.6 %collective-permute-start.9 = (bf16[1024,2048]{1,0:T(8,128)(2,1)}, bf16[1024,2048]{1,0:T(8,128)(2,1)}, u32[]{:S(2)}, u32[]{:S(2)}) collective-permute-start(bf16[1024,2048]{1,0:T(8,128)(2,1)} %pad_maximum_fusion.1), channel_id=1, source_target_pairs={{1,17},{3,19},{5,21},{7,23},{9,25},{11,27},{13,29},{15,31}} | collective-permute-start | bytes 12582920 | tf_op jit(solution)/shard_map/W0mlp/ppermute | solution.py:744
  90.3 58.4 %collective-permute-start.12 = (bf16[1024,1792]{0,1:T(8,128)(2,1)}, bf16[1024,1792]{0,1:T(8,128)(2,1)}, u32[]{:S(2)}, u32[]{:S(2)}) collective-permute-start(bf16[1024,1792]{0,1:T(8,128)(2,1)} %pad_maximum_fusion.2), channel_id=1, source_target_pairs={{16,2},{17,3},{18,16},{19,17},{20,6},{21,7},{22,20},{23,21},{24,10... | collective-permute-start | bytes 11010056 | tf_op jit(solution)/shard_map/W1attn/ppermute | solution.py:744
  92.8 55.9 %collective-permute-start.11 = (bf16[1024,1792]{0,1:T(8,128)(2,1)}, bf16[1024,1792]{0,1:T(8,128)(2,1)}, u32[]{:S(2)}, u32[]{:S(2)}) collective-permute-start(bf16[1024,1792]{0,1:T(8,128)(2,1)} %pad_maximum_fusion.2), channel_id=1, source_target_pairs={{16,0},{17,1},{20,4},{21,5},{24,8},{25,9},{28,12},{29,13}} | collective-permute-start | bytes 11010056 | tf_op jit(solution)/shard_map/W1attn/ppermute | solution.py:744
  265.3 37.2 %collective-permute-start.39 = (bf16[1024,2048]{1,0:T(8,128)(2,1)}, bf16[1024,2048]{1,0:T(8,128)(2,1)}, u32[]{:S(2)}, u32[]{:S(2)}) collective-permute-start(bf16[1024,2048]{1,0:T(8,128)(2,1)} %pad_maximum_fusion.1), channel_id=1, source_target_pairs={{16,1},{17,16},{18,3},{19,18},{20,5},{21,20},{22,7},{23,22},{24,9}... | collective-permute-start | bytes 12582920 | tf_op jit(solution)/shard_map/W1mlp/ppermute | solution.py:744
  267.9 34.5 %collective-permute-start.38 = (bf16[1024,2048]{1,0:T(8,128)(2,1)}, bf16[1024,2048]{1,0:T(8,128)(2,1)}, u32[]{:S(2)}, u32[]{:S(2)}) collective-permute-start(bf16[1024,2048]{1,0:T(8,128)(2,1)} %pad_maximum_fusion.1), channel_id=1, source_target_pairs={{16,0},{18,2},{20,4},{22,6},{24,8},{26,10},{28,12},{30,14}} | collective-permute-start | bytes 12582920 | tf_op jit(solution)/shard_map/W1mlp/ppermute | solution.py:744
  305.3 38.5 %collective-permute-start.50 = (bf16[256,1024]{1,0:T(8,128)(2,1)S(1)}, bf16[256,1024]{1,0:T(8,128)(2,1)S(1)}, u32[]{:S(2)}, u32[]{:S(2)}) collective-permute-start(bf16[256,1024]{1,0:T(8,128)(2,1)S(1)} %slice.1246), channel_id=1, source_target_pairs={{0,16},{16,0},{1,17},{17,1},{2,18},{18,2},{3,19},{19,3},{4,20},{20... | collective-permute-start | bytes 1572872 | tf_op jit(solution)/shard_map/F1out/ssec2/ppermute | solution.py:747
  482.8 78.1 %collective-permute-start.82 = (bf16[1024,1024]{1,0:T(8,128)(2,1)}, bf16[1024,1024]{1,0:T(8,128)(2,1)}, u32[]{:S(2)}, u32[]{:S(2)}) collective-permute-start(bf16[1024,1024]{1,0:T(8,128)(2,1)} %fusion.81), channel_id=1, source_target_pairs={{1,16},{3,18},{16,1},{18,3},{5,20},{7,22},{20,5},{22,7},{9,24},{11... | collective-permute-start | bytes 6291464 | tf_op jit(solution)/shard_map/B1wmlp/ppermute | solution.py:744
  504.5 56.4 %collective-permute-start.81 = (bf16[1024,1024]{1,0:T(8,128)(2,1)}, bf16[1024,1024]{1,0:T(8,128)(2,1)}, u32[]{:S(2)}, u32[]{:S(2)}) collective-permute-start(bf16[1024,1024]{1,0:T(8,128)(2,1)} %add_convert_fusion.3), channel_id=1, source_target_pairs={{0,16},{1,0},{2,18},{3,2},{16,17},{17,1},{18,19},{19,3},{4,20},{5,... | collective-permute-start | bytes 6291464 | tf_op jit(solution)/shard_map/B1wmlp/ppermute | solution.py:744
  584.4 243.5 %all-reduce.7.cloned.1.call-start = ((), (), s32[]{:S(2)}) async-start(), calls=%async_computation.1 | async-start | bytes 4194304 | tf_op jit(solution)/shard_map/psum | solution.py:993
  690.4 40.9 %collective-permute-start.107 = (bf16[1024,1024]{1,0:T(8,128)(2,1)}, bf16[1024,1024]{1,0:T(8,128)(2,1)}, u32[]{:S(2)}, u32[]{:S(2)}) collective-permute-start(bf16[1024,1024]{1,0:T(8,128)(2,1)} %add_convert_fusion.1), channel_id=1, source_target_pairs={{0,16},{1,0},{2,18},{3,2},{16,17},{17,1},{18,19},{19,3},{4,20},{5,... | collective-permute-start | bytes 6291464 | tf_op jit(solution)/shard_map/B0wmlp/ppermute | solution.py:744
  704.5 78.7 %collective-permute-start.109 = (bf16[512,1792]{1,0:T(8,128)(2,1)}, bf16[512,1792]{1,0:T(8,128)(2,1)}, u32[]{:S(2)}, u32[]{:S(2)}) collective-permute-start(bf16[512,1792]{1,0:T(8,128)(2,1)} %get-tuple-element.215), channel_id=1, source_target_pairs={{0,16},{1,17},{2,0},{3,1},{16,18},{17,19},{18,2},{19,3},{4,20},{5,... | collective-permute-start | bytes 5505032 | tf_op jit(solution)/shard_map/B1wattn/ppermute | solution.py:744
  705.7 77.5 %collective-permute-start.110 = (bf16[512,1792]{1,0:T(8,128)(2,1)}, bf16[512,1792]{1,0:T(8,128)(2,1)}, u32[]{:S(2)}, u32[]{:S(2)}) collective-permute-start(bf16[512,1792]{1,0:T(8,128)(2,1)} %get-tuple-element.216), channel_id=1, source_target_pairs={{2,16},{3,17},{16,2},{17,3},{6,20},{7,21},{20,6},{21,7},{10,24},{1... | collective-permute-start | bytes 5505032 | tf_op jit(solution)/shard_map/B1wattn/ppermute | solution.py:744
  735.8 275.4 %all-reduce.9.cloned.1.call-start = ((), (), s32[]{:S(2)}) async-start(), calls=%async_computation.2 | async-start | bytes 7340032 | tf_op jit(solution)/shard_map/B0wattn/psum | solution.py:993
  800.4 83.4 %collective-permute-start.111 = (bf16[256,1024]{1,0:T(8,128)(2,1)}, bf16[256,1024]{1,0:T(8,128)(2,1)}, u32[]{:S(2)}, u32[]{:S(2)}) collective-permute-start(bf16[256,1024]{1,0:T(8,128)(2,1)} %slice.1231), channel_id=1, source_target_pairs={{0,16},{16,0},{1,17},{17,1},{2,18},{18,2},{3,19},{19,3},{4,20},{20... | collective-permute-start | bytes 1572872 | tf_op jit(solution)/shard_map/B0in/ssec2/ppermute | solution.py:747
  803.1 34.7 %collective-permute-start.122 = (bf16[512,1792]{1,0:T(8,128)(2,1)}, bf16[512,1792]{1,0:T(8,128)(2,1)}, u32[]{:S(2)}, u32[]{:S(2)}) collective-permute-start(bf16[512,1792]{1,0:T(8,128)(2,1)} %get-tuple-element.208), channel_id=1, source_target_pairs={{2,16},{3,17},{16,2},{17,3},{6,20},{7,21},{20,6},{21,7},{10,24},{1... | collective-permute-start | bytes 5505032 | tf_op jit(solution)/shard_map/B0wattn/ppermute | solution.py:744
  808.0 76.6 %collective-permute-start.113 = (bf16[256,1024]{1,0:T(8,128)(2,1)}, bf16[256,1024]{1,0:T(8,128)(2,1)}, u32[]{:S(2)}, u32[]{:S(2)}) collective-permute-start(bf16[256,1024]{1,0:T(8,128)(2,1)} %fusion.115), channel_id=1, source_target_pairs={{0,1},{1,0},{2,3},{3,2},{16,17},{17,16},{18,19},{19,18},{4,5},{5,4... | collective-permute-start | bytes 1572872 | tf_op jit(solution)/shard_map/B0in/shop/ppermute | solution.py:744
  837.2 48.1 %collective-permute-start.114 = (bf16[256,1024]{1,0:T(8,128)(2,1)}, bf16[256,1024]{1,0:T(8,128)(2,1)}, u32[]{:S(2)}, u32[]{:S(2)}) collective-permute-start(bf16[256,1024]{1,0:T(8,128)(2,1)} %slice.1229), channel_id=1, source_target_pairs={{0,16},{16,0},{1,17},{17,1},{2,18},{18,2},{3,19},{19,3},{4,20},{20... | collective-permute-start | bytes 1572872 | tf_op jit(solution)/shard_map/B0in/ssec/ppermute | solution.py:747
  837.7 47.7 %collective-permute-start.115 = (bf16[256,1024]{1,0:T(8,128)(2,1)}, bf16[256,1024]{1,0:T(8,128)(2,1)}, u32[]{:S(2)}, u32[]{:S(2)}) collective-permute-start(bf16[256,1024]{1,0:T(8,128)(2,1)} %slice.1228), channel_id=1, source_target_pairs={{0,16},{16,0},{1,17},{17,1},{2,18},{18,2},{3,19},{19,3},{4,20},{20... | collective-permute-start | bytes 1572872 | tf_op jit(solution)/shard_map/B0in/ssec2/ppermute | solution.py:747
  885.4 34.6 %collective-permute-start.78 = (bf16[512,1024]{1,0:T(8,128)(2,1)S(1)}, bf16[512,1024]{1,0:T(8,128)(2,1)S(1)}, u32[]{:S(2)}, u32[]{:S(2)}) collective-permute-start(bf16[512,1024]{1,0:T(8,128)(2,1)S(1)} %copy-done.41), channel_id=1, source_target_pairs={{0,16},{1,17},{16,18},{17,19},{4,20},{5,21},{20,22},{21,23},{8,24}... | collective-permute-start | bytes 3145736 | tf_op jit(solution)/shard_map/OUTROWS/ppermute | solution.py:744
  911.8 37.8 %collective-permute-start.123 = (bf16[1024,1024]{1,0:T(8,128)(2,1)}, bf16[1024,1024]{1,0:T(8,128)(2,1)}, u32[]{:S(2)}, u32[]{:S(2)}) collective-permute-start(bf16[1024,1024]{1,0:T(8,128)(2,1)} %broadcast_select_fusion), channel_id=1, source_target_pairs={{0,16},{16,0},{1,17},{17,1},{2,18},{18,2},{3,19},{19,3},{4,20},{20... | collective-permute-start | bytes 6291464 | tf_op jit(solution)/shard_map/ppermute | solution.py:747
  (287 other events, 3581.8 us)
Sparse Core Ops, SparseCore 0:
  584.4 93.0 all-reduce.4
  735.9 91.9 all-reduce.6
  860.1 151.0 all-reduce.8

commit v4 on v3

--- a/solution.py
+++ b/solution.py
@@ -662,7 +662,7 @@
 
 def unpack(home, mine, theirs, blocks, each):
     half, columns = mine.shape
-    tile = min(128, half)
+    tile = min(256, half)
     per_half = half // tile
     source = pl.BlockSpec((tile, columns), lambda step, _: (lax.rem(step, per_half), 0))
     return pl.pallas_call(
@@ -1148,7 +1148,7 @@
             jnp.stack([sum(sums_one[1:], sums_one[0]), sum(sums_two[1:], sums_two[0])])
             for sums_one, sums_two in norm_sums
         ]
-        mine = lax.optimization_barrier((*mine, last_parts))[:sections]
+        mine = [gated(term, grad_low[-1]) for term in mine]
         norm_sum = pick(mine) + other_core(pick(mine[::-1]))
         if crossed:
             norm_sum = norm_sum + other_row(norm_sum)

time: 1050 us -> 1040 us (level)
  starting transfers between devices: 160 us -> 121 us
  Pallas kernels: 167 us -> 187 us
    ppermute x4, starting transfers between devices: 19.1 us -> 0.09 us  [dp_butterfly(): value = combine(value, lax.ppermute(value, 'dp', pairs))]
    pallas_call x2, Pallas kernels: 94.2 us -> 108 us  [attend_back(): pl.pallas_call(partial(attend_back_kernel, heads, plan, (len(proj), len(g...]
    ppermute x69, starting transfers between devices: 41.3 us -> 27.8 us  [other_core(): return lax.ppermute(value, 'section', [(0, 1), (1, 0)])]
    unnamed x394 -> x384, local copies, waits for them, and re-layouts: 39.1 us -> 37.2 us
    slice x41 -> x42, local copies, waits for them, and re-layouts: 24.9 us -> 26 us  [gated(): corner = lax.slice(other, (0,) * other.ndim, (1,) * other.ndim)]
  transfers between devices with their start and end apart: 137 -> 137, of which waited for: 43 -> 43; matrix products, arithmetic and copies ran while one was open for 32% -> 32% of each run, Pallas kernels for 15% -> 18%
where the time goes in v4:
time: 1040 us; the launch traced here: 1020 us
  waiting for transfers between devices  295 us (28%)
  Pallas kernels  187 us (18%)
  matrix products  156 us (15%)
  starting transfers between devices  121 us (12%)
  other arithmetic  121 us (12%)
  local copies, waits for them, and re-layouts  98.6 us (9%)
  between operations  45.5 us (4%)
    ppermute x61, waiting for transfers between devices, route(): return lax.ppermute(value, joint, pairs)  200 us
    dot_general x72, matrix products, mm(): lax.dot_general(left, right, dims, preferred_element_type=jnp.float32)  156 us
    pallas_call x2, Pallas kernels, attend_back(): pl.pallas_call(partial(attend_back_kernel, heads, plan, (len(proj), len(g...  108 us
    ppermute x61, starting transfers between devices, route(): return lax.ppermute(value, joint, pairs)  92.6 us
    psum x3, waiting for transfers between devices, dp_sum(): earlier = lax.psum(tuple(terms), 'dp')  72.1 us
    pallas_call x2, Pallas kernels, attend(): pl.pallas_call(partial(attend_kernel, heads, plan, len(proj)), out_shape=...  66.5 us
    unnamed x384, local copies, waits for them, and re-layouts  37.2 us
    ppermute x69, starting transfers between devices, other_core(): return lax.ppermute(value, 'section', [(0, 1), (1, 0)])  27.8 us
  transfers between devices with their start and end apart: 137, of which 43 were waited for; matrix products, arithmetic and copies ran while one was open for 32% of the time, Pallas kernels for 18%

profile of v4, /device:TPU:0, one launch (start us, length us, event | category | flops | bytes accessed | tf_op | source)
XLA Modules:
  0.0 1023.7 jit_solution(12662795645037036883)
XLA Ops:
  41.7 13.5 %collective-permute-done.4 = bf16[512,1024]{1,0:T(8,128)(2,1)} collective-permute-done((bf16[512,1024]{1,0:T(8,128)(2,1)}, bf16[512,1024]{1,0:T(8,128)(2,1)}, u32[]{:S(2)}, u32[]{:S(2)}) %collective-permute-start.4) | collective-permute-done | bytes 1048608 | tf_op jit(solution)/shard_map/ppermute | solution.py:744
  112.2 33.3 %attend.2 = (bf16[2048,256]{1,0:T(8,128)(2,1)}, f32[4,2048]{1,0:T(4,128)}, f32[1,128]{1,0:T(1,128)}, f32[1,1024]{1,0:T(1,128)}, f32[1,128]{1,0:T(1,128)}) custom-call(s32[2]{0:T(128)} %pad_add_fusion.order_ref, s32[8]{0:T(128)} %get-tuple-element.70.first_ref, s32[8]{0:T(128)} %get-tuple-element.71.last_ref, ...), custom_call_target="tpu_custom_call" | custom-call | flops 10737418240 | bytes 7340032 | tf_op jit(solution)/shard_map/attend/pallas_call | solution.py:277
  170.8 7.0 collective-permute-done.24
  193.7 7.0 collective-permute-done.26
  221.7 11.4 %collective-permute-done.33 = bf16[256,1024]{1,0:T(8,128)(2,1)S(1)} collective-permute-done((bf16[256,1024]{1,0:T(8,128)(2,1)S(1)}, bf16[256,1024]{1,0:T(8,128)(2,1)S(1)}, u32[]{:S(2)}, u32[]{:S(2)}) %collective-permute-start.33) | collective-permute-done | bytes 524320 | tf_op jit(solution)/shard_map/F1in/ghop/ppermute | solution.py:744
  269.6 33.3 %attend.3 = (bf16[2048,256]{1,0:T(8,128)(2,1)}, f32[4,2048]{1,0:T(4,128)}, f32[1,128]{1,0:T(1,128)}, f32[1,1024]{1,0:T(1,128)}, f32[1,128]{1,0:T(1,128)}) custom-call(s32[2]{0:T(128)} %pad_add_fusion.order_ref, s32[8]{0:T(128)} %get-tuple-element.70.first_ref, s32[8]{0:T(128)} %get-tuple-element.71.last_ref, ...), custom_call_target="tpu_custom_call" | custom-call | flops 10737418240 | bytes 7340032 | tf_op jit(solution)/shard_map/attend/pallas_call | solution.py:277
  305.8 8.7 collective-permute-start.50
  326.6 11.2 %collective-permute-done.43 = bf16[256,1024]{1,0:T(8,128)(2,1)S(1)} collective-permute-done((bf16[256,1024]{1,0:T(8,128)(2,1)S(1)}, bf16[256,1024]{1,0:T(8,128)(2,1)S(1)}, u32[]{:S(2)}, u32[]{:S(2)}) %collective-permute-start.43) | collective-permute-done | bytes 524320 | tf_op jit(solution)/shard_map/F1out/shop/ppermute | solution.py:744
  341.3 7.1 collective-permute-done.51
  361.2 9.8 collective-permute-done.53
  381.2 11.2 %collective-permute-done.52 = bf16[256,1024]{1,0:T(8,128)(2,1)S(1)} collective-permute-done((bf16[256,1024]{1,0:T(8,128)(2,1)S(1)}, bf16[256,1024]{1,0:T(8,128)(2,1)S(1)}, u32[]{:S(2)}, u32[]{:S(2)}) %collective-permute-start.52) | collective-permute-done | bytes 524320 | tf_op jit(solution)/shard_map/F1mlp/shop/ppermute | solution.py:744
  406.4 8.0 collective-permute-done.61
  426.2 9.3 collective-permute-done.65
  443.8 7.1 fusion.75
  474.8 11.4 %collective-permute-done.75 = bf16[256,1024]{1,0:T(8,128)(2,1)S(1)} collective-permute-done((bf16[256,1024]{1,0:T(8,128)(2,1)S(1)}, bf16[256,1024]{1,0:T(8,128)(2,1)S(1)}, u32[]{:S(2)}, u32[]{:S(2)}) %collective-permute-start.75) | collective-permute-done | bytes 524320 | tf_op jit(solution)/shard_map/B1ctx1/ghop/ppermute | solution.py:744
  507.9 53.7 %attend_back.2 = bf16[2048,1536]{1,0:T(8,128)(2,1)} custom-call(s32[2]{0:T(128)} %pad_add_fusion.order_ref, s32[8]{0:T(128)} %get-tuple-element.70.first_ref, s32[8]{0:T(128)} %get-tuple-element.71.last_ref, bf16[512,1536]{1,0:T(8,128)(2,1)} %convolution_convert_fusion.5.refs_0_, bf16[512,1536]{1,0:T(8,128)(2,1)} %convolution_convert_fusion.4.refs_1_, ...), custom_call_target="tpu_custom_call" | custom-call | flops 2147483648 | bytes 2097152 | tf_op jit(solution)/shard_map/attend_back/pallas_call | solution.py:543
  623.9 9.7 collective-permute-done.95
  653.5 7.7 fusion.78
  672.7 8.7 convolution_convert_fusion.1
  717.5 14.3 %collective-permute-done.107 = bf16[1024,1024]{1,0:T(8,128)(2,1)} collective-permute-done((bf16[1024,1024]{1,0:T(8,128)(2,1)}, bf16[1024,1024]{1,0:T(8,128)(2,1)}, u32[]{:S(2)}, u32[]{:S(2)}) %collective-permute-start.107) | collective-permute-done | bytes 2097184 | tf_op jit(solution)/shard_map/B0wmlp/ppermute | solution.py:744
  736.3 54.2 %attend_back.3 = bf16[2048,1536]{1,0:T(8,128)(2,1)} custom-call(s32[2]{0:T(128)} %pad_add_fusion.order_ref, s32[8]{0:T(128)} %get-tuple-element.70.first_ref, s32[8]{0:T(128)} %get-tuple-element.71.last_ref, bf16[512,1536]{1,0:T(8,128)(2,1)} %convolution_convert_fusion.9.refs_0_, bf16[512,1536]{1,0:T(8,128)(2,1)} %convolution_convert_fusion.8.refs_1_, ...), custom_call_target="tpu_custom_call" | custom-call | flops 2147483648 | bytes 2097152 | tf_op jit(solution)/shard_map/attend_back/pallas_call | solution.py:543
  804.5 7.4 convolution_convert_fusion
  830.9 9.2 collective-permute-done.113
  930.8 69.4 %all-reduce.9.cloned.1.call-done = (bf16[512,1792]{1,0:T(8,128)(2,1)}, bf16[512,1792]{1,0:T(8,128)(2,1)}) async-done(((bf16[512,1792]{1,0:T(8,128)(2,1)}, bf16[512,1792]{1,0:T(8,128)(2,1)}), (bf16[512,1792]{1,0:T(8,128)(2,1)}, bf16[512,1792]{1,0:T(8,128)(2,1)})) %all-reduce.9.cloned.1.call-update) | async-done | bytes 3670032 | tf_op jit(solution)/shard_map/B0wattn/psum | solution.py:993
  (984 shorter events, 554.8 us)
Async XLA Ops:
  7.2 690.5 %all-reduce.5.cloned.1.call-start = ((), (), s32[]{:S(2)}) async-start(), calls=%async_computation | async-start | bytes 4194304 | tf_op jit(solution)/shard_map/psum | solution.py:993
  23.2 51.8 %collective-permute-start.2 = (bf16[1024,1792]{0,1:T(8,128)(2,1)}, bf16[1024,1792]{0,1:T(8,128)(2,1)}, u32[]{:S(2)}, u32[]{:S(2)}) collective-permute-start(bf16[1024,1792]{0,1:T(8,128)(2,1)} %pad_maximum_fusion.2), channel_id=1, source_target_pairs={{0,2},{1,3},{2,16},{3,17},{4,6},{5,7},{6,20},{7,21},{8,10},{9,11},... | collective-permute-start | bytes 11010056 | tf_op jit(solution)/shard_map/W0attn/ppermute | solution.py:744
  26.4 48.6 %collective-permute-start.1 = (bf16[1024,1792]{0,1:T(8,128)(2,1)}, bf16[1024,1792]{0,1:T(8,128)(2,1)}, u32[]{:S(2)}, u32[]{:S(2)}) collective-permute-start(bf16[1024,1792]{0,1:T(8,128)(2,1)} %pad_maximum_fusion.2), channel_id=1, source_target_pairs={{2,18},{3,19},{6,22},{7,23},{10,26},{11,27},{14,30},{15,31}} | collective-permute-start | bytes 11010056 | tf_op jit(solution)/shard_map/W0attn/ppermute | solution.py:744
  66.5 79.0 %collective-permute-start.10 = (bf16[1024,2048]{1,0:T(8,128)(2,1)}, bf16[1024,2048]{1,0:T(8,128)(2,1)}, u32[]{:S(2)}, u32[]{:S(2)}) collective-permute-start(bf16[1024,2048]{1,0:T(8,128)(2,1)} %pad_maximum_fusion.1), channel_id=1, source_target_pairs={{0,1},{1,16},{2,3},{3,18},{4,5},{5,20},{6,7},{7,22},{8,9},{9,24},{... | collective-permute-start | bytes 12582920 | tf_op jit(solution)/shard_map/W0mlp/ppermute | solution.py:744
  72.2 73.3 %collective-permute-start.9 = (bf16[1024,2048]{1,0:T(8,128)(2,1)}, bf16[1024,2048]{1,0:T(8,128)(2,1)}, u32[]{:S(2)}, u32[]{:S(2)}) collective-permute-start(bf16[1024,2048]{1,0:T(8,128)(2,1)} %pad_maximum_fusion.1), channel_id=1, source_target_pairs={{1,17},{3,19},{5,21},{7,23},{9,25},{11,27},{13,29},{15,31}} | collective-permute-start | bytes 12582920 | tf_op jit(solution)/shard_map/W0mlp/ppermute | solution.py:744
  90.4 55.1 %collective-permute-start.12 = (bf16[1024,1792]{0,1:T(8,128)(2,1)}, bf16[1024,1792]{0,1:T(8,128)(2,1)}, u32[]{:S(2)}, u32[]{:S(2)}) collective-permute-start(bf16[1024,1792]{0,1:T(8,128)(2,1)} %pad_maximum_fusion.2), channel_id=1, source_target_pairs={{16,2},{17,3},{18,16},{19,17},{20,6},{21,7},{22,20},{23,21},{24,10... | collective-permute-start | bytes 11010056 | tf_op jit(solution)/shard_map/W1attn/ppermute | solution.py:744
  93.0 52.5 %collective-permute-start.11 = (bf16[1024,1792]{0,1:T(8,128)(2,1)}, bf16[1024,1792]{0,1:T(8,128)(2,1)}, u32[]{:S(2)}, u32[]{:S(2)}) collective-permute-start(bf16[1024,1792]{0,1:T(8,128)(2,1)} %pad_maximum_fusion.2), channel_id=1, source_target_pairs={{16,0},{17,1},{20,4},{21,5},{24,8},{25,9},{28,12},{29,13}} | collective-permute-start | bytes 11010056 | tf_op jit(solution)/shard_map/W1attn/ppermute | solution.py:744
  261.6 41.3 %collective-permute-start.39 = (bf16[1024,2048]{1,0:T(8,128)(2,1)}, bf16[1024,2048]{1,0:T(8,128)(2,1)}, u32[]{:S(2)}, u32[]{:S(2)}) collective-permute-start(bf16[1024,2048]{1,0:T(8,128)(2,1)} %pad_maximum_fusion.1), channel_id=1, source_target_pairs={{16,1},{17,16},{18,3},{19,18},{20,5},{21,20},{22,7},{23,22},{24,9}... | collective-permute-start | bytes 12582920 | tf_op jit(solution)/shard_map/W1mlp/ppermute | solution.py:744
  264.3 38.6 %collective-permute-start.38 = (bf16[1024,2048]{1,0:T(8,128)(2,1)}, bf16[1024,2048]{1,0:T(8,128)(2,1)}, u32[]{:S(2)}, u32[]{:S(2)}) collective-permute-start(bf16[1024,2048]{1,0:T(8,128)(2,1)} %pad_maximum_fusion.1), channel_id=1, source_target_pairs={{16,0},{18,2},{20,4},{22,6},{24,8},{26,10},{28,12},{30,14}} | collective-permute-start | bytes 12582920 | tf_op jit(solution)/shard_map/W1mlp/ppermute | solution.py:744
  266.8 36.1 %collective-permute-start.40 = (bf16[512,1024]{1,0:T(8,128)(2,1)}, bf16[512,1024]{1,0:T(8,128)(2,1)S(1)}, u32[]{:S(2)}, u32[]{:S(2)}) collective-permute-start(bf16[512,1024]{1,0:T(8,128)(2,1)} %get-tuple-element.281), channel_id=1, source_target_pairs={{0,2},{1,3},{18,16},{19,17},{4,6},{5,7},{22,20},{23,21},{8,10},{9,... | collective-permute-start | bytes 3145736 | tf_op jit(solution)/shard_map/COT/ppermute | solution.py:744
  305.8 35.4 %collective-permute-start.50 = (bf16[256,1024]{1,0:T(8,128)(2,1)S(1)}, bf16[256,1024]{1,0:T(8,128)(2,1)S(1)}, u32[]{:S(2)}, u32[]{:S(2)}) collective-permute-start(bf16[256,1024]{1,0:T(8,128)(2,1)S(1)} %slice.1252), channel_id=1, source_target_pairs={{0,16},{16,0},{1,17},{17,1},{2,18},{18,2},{3,19},{19,3},{4,20},{20... | collective-permute-start | bytes 1572872 | tf_op jit(solution)/shard_map/F1out/ssec2/ppermute | solution.py:747
  472.5 89.1 %collective-permute-start.82 = (bf16[1024,1024]{1,0:T(8,128)(2,1)}, bf16[1024,1024]{1,0:T(8,128)(2,1)}, u32[]{:S(2)}, u32[]{:S(2)}) collective-permute-start(bf16[1024,1024]{1,0:T(8,128)(2,1)} %fusion.81), channel_id=1, source_target_pairs={{1,16},{3,18},{16,1},{18,3},{5,20},{7,22},{20,5},{22,7},{9,24},{11... | collective-permute-start | bytes 6291464 | tf_op jit(solution)/shard_map/B1wmlp/ppermute | solution.py:744
  497.3 64.3 %collective-permute-start.81 = (bf16[1024,1024]{1,0:T(8,128)(2,1)}, bf16[1024,1024]{1,0:T(8,128)(2,1)}, u32[]{:S(2)}, u32[]{:S(2)}) collective-permute-start(bf16[1024,1024]{1,0:T(8,128)(2,1)} %add_convert_fusion.3), channel_id=1, source_target_pairs={{0,16},{1,0},{2,18},{3,2},{16,17},{17,1},{18,19},{19,3},{4,20},{5,... | collective-permute-start | bytes 6291464 | tf_op jit(solution)/shard_map/B1wmlp/ppermute | solution.py:744
  585.2 234.2 %all-reduce.7.cloned.1.call-start = ((), (), s32[]{:S(2)}) async-start(), calls=%async_computation.1 | async-start | bytes 4194304 | tf_op jit(solution)/shard_map/psum | solution.py:993
  681.3 36.2 %collective-permute-start.108 = (bf16[1024,1024]{1,0:T(8,128)(2,1)}, bf16[1024,1024]{1,0:T(8,128)(2,1)}, u32[]{:S(2)}, u32[]{:S(2)}) collective-permute-start(bf16[1024,1024]{1,0:T(8,128)(2,1)} %fusion.78), channel_id=1, source_target_pairs={{1,16},{3,18},{16,1},{18,3},{5,20},{7,22},{20,5},{22,7},{9,24},{11... | collective-permute-start | bytes 6291464 | tf_op jit(solution)/shard_map/B0wmlp/ppermute | solution.py:744
  692.5 39.3 %collective-permute-start.107 = (bf16[1024,1024]{1,0:T(8,128)(2,1)}, bf16[1024,1024]{1,0:T(8,128)(2,1)}, u32[]{:S(2)}, u32[]{:S(2)}) collective-permute-start(bf16[1024,1024]{1,0:T(8,128)(2,1)} %add_convert_fusion.1), channel_id=1, source_target_pairs={{0,16},{1,0},{2,18},{3,2},{16,17},{17,1},{18,19},{19,3},{4,20},{5,... | collective-permute-start | bytes 6291464 | tf_op jit(solution)/shard_map/B0wmlp/ppermute | solution.py:744
  706.8 83.7 %collective-permute-start.109 = (bf16[512,1792]{1,0:T(8,128)(2,1)}, bf16[512,1792]{1,0:T(8,128)(2,1)}, u32[]{:S(2)}, u32[]{:S(2)}) collective-permute-start(bf16[512,1792]{1,0:T(8,128)(2,1)} %get-tuple-element.211), channel_id=1, source_target_pairs={{0,16},{1,17},{2,0},{3,1},{16,18},{17,19},{18,2},{19,3},{4,20},{5,... | collective-permute-start | bytes 5505032 | tf_op jit(solution)/shard_map/B1wattn/ppermute | solution.py:744
  707.9 82.6 %collective-permute-start.110 = (bf16[512,1792]{1,0:T(8,128)(2,1)}, bf16[512,1792]{1,0:T(8,128)(2,1)}, u32[]{:S(2)}, u32[]{:S(2)}) collective-permute-start(bf16[512,1792]{1,0:T(8,128)(2,1)} %get-tuple-element.212), channel_id=1, source_target_pairs={{2,16},{3,17},{16,2},{17,3},{6,20},{7,21},{20,6},{21,7},{10,24},{1... | collective-permute-start | bytes 5505032 | tf_op jit(solution)/shard_map/B1wattn/ppermute | solution.py:744
  736.2 264.0 %all-reduce.9.cloned.1.call-start = ((), (), s32[]{:S(2)}) async-start(), calls=%async_computation.2 | async-start | bytes 7340032 | tf_op jit(solution)/shard_map/B0wattn/psum | solution.py:993
  814.7 38.6 %collective-permute-start.121 = (bf16[512,1792]{1,0:T(8,128)(2,1)}, bf16[512,1792]{1,0:T(8,128)(2,1)S(1)}, u32[]{:S(2)}, u32[]{:S(2)}) collective-permute-start(bf16[512,1792]{1,0:T(8,128)(2,1)} %get-tuple-element.203), channel_id=1, source_target_pairs={{0,16},{1,17},{2,0},{3,1},{16,18},{17,19},{18,2},{19,3},{4,20},{5,... | collective-permute-start | bytes 5505032 | tf_op jit(solution)/shard_map/B0wattn/ppermute | solution.py:744
  814.7 38.6 %collective-permute-start.122 = (bf16[512,1792]{1,0:T(8,128)(2,1)}, bf16[512,1792]{1,0:T(8,128)(2,1)}, u32[]{:S(2)}, u32[]{:S(2)}) collective-permute-start(bf16[512,1792]{1,0:T(8,128)(2,1)} %get-tuple-element.204), channel_id=1, source_target_pairs={{2,16},{3,17},{16,2},{17,3},{6,20},{7,21},{20,6},{21,7},{10,24},{1... | collective-permute-start | bytes 5505032 | tf_op jit(solution)/shard_map/B0wattn/ppermute | solution.py:744
  840.1 47.7 %collective-permute-start.79 = (bf16[512,1024]{1,0:T(8,128)(2,1)}, bf16[512,1024]{1,0:T(8,128)(2,1)}, u32[]{:S(2)}, u32[]{:S(2)}) collective-permute-start(bf16[512,1024]{1,0:T(8,128)(2,1)} %pad_maximum_fusion.7), channel_id=1, source_target_pairs={{2,0},{3,1},{18,2},{19,3},{6,4},{7,5},{22,6},{23,7},{10,8},{11,9},... | collective-permute-start | bytes 3145736 | tf_op jit(solution)/shard_map/OUTROWS/ppermute | solution.py:744
  845.0 43.9 %collective-permute-start.77 = (bf16[512,1024]{1,0:T(8,128)(2,1)}, bf16[512,1024]{1,0:T(8,128)(2,1)}, u32[]{:S(2)}, u32[]{:S(2)}) collective-permute-start(bf16[512,1024]{1,0:T(8,128)(2,1)} %pad_maximum_fusion.7), channel_id=1, source_target_pairs={{16,2},{17,3},{20,6},{21,7},{24,10},{25,11},{28,14},{29,15}} | collective-permute-start | bytes 3145736 | tf_op jit(solution)/shard_map/OUTROWS/ppermute | solution.py:744
  887.8 35.3 %collective-permute-start.123 = (bf16[1024,1024]{1,0:T(8,128)(2,1)}, bf16[1024,1024]{1,0:T(8,128)(2,1)}, u32[]{:S(2)}, u32[]{:S(2)}) collective-permute-start(bf16[1024,1024]{1,0:T(8,128)(2,1)} %broadcast_select_fusion), channel_id=1, source_target_pairs={{0,16},{16,0},{1,17},{17,1},{2,18},{18,2},{3,19},{19,3},{4,20},{20... | collective-permute-start | bytes 6291464 | tf_op jit(solution)/shard_map/ppermute | solution.py:747
  (282 other events, 3467.0 us)
Sparse Core Ops, SparseCore 0:
  585.3 84.0 all-reduce.4
  736.3 83.0 all-reduce.6
  859.2 140.9 all-reduce.8

commit v5 on v4

--- a/solution.py
+++ b/solution.py
@@ -1157,7 +1157,7 @@
             norm_sum = lax.psum(norm_sum, "tensor")
         norm_sum = dp_butterfly(norm_sum, jnp.add)
     with jax.named_scope("PEAK"):
-        peak_all = lax.optimization_barrier((*flat(peaks), last_parts))[:-1]
+        peak_all = [gated(value, grad_low[-1]) for value in flat(peaks)]
         peak_all = jnp.stack(
             [jnp.max(value.reshape(heads, -1), 1) for value in peak_all]
         ).reshape(sections, 2, heads)

time: 1040 us -> 1040 us (level)
  starting transfers between devices: 121 us -> 159 us
  Pallas kernels: 187 us -> 166 us
  waiting for transfers between devices: 295 us -> 283 us
    ppermute x61, starting transfers between devices: 92.6 us -> 120 us  [route(): return lax.ppermute(value, joint, pairs)]
    pallas_call x2, Pallas kernels: 108 us -> 94.7 us  [attend_back(): pl.pallas_call(partial(attend_back_kernel, heads, plan, (len(proj), len(g...]
    unnamed x384 -> x388, local copies, waits for them, and re-layouts: 37.2 us -> 38.5 us
  transfers between devices with their start and end apart: 137 -> 137, of which waited for: 43 -> 42; matrix products, arithmetic and copies ran while one was open for 32% -> 32% of each run, Pallas kernels for 18% -> 16%
where the time goes in v5:
time: 1040 us; the launch traced here: 1030 us
  waiting for transfers between devices  283 us (27%)
  Pallas kernels  166 us (16%)
  starting transfers between devices  159 us (15%)
  matrix products  156 us (15%)
  other arithmetic  120 us (12%)
  local copies, waits for them, and re-layouts  101 us (10%)
  between operations  45.4 us (4%)
    ppermute x61, waiting for transfers between devices, route(): return lax.ppermute(value, joint, pairs)  193 us
    dot_general x72, matrix products, mm(): lax.dot_general(left, right, dims, preferred_element_type=jnp.float32)  156 us
    ppermute x61, starting transfers between devices, route(): return lax.ppermute(value, joint, pairs)  120 us
    pallas_call x2, Pallas kernels, attend_back(): pl.pallas_call(partial(attend_back_kernel, heads, plan, (len(proj), len(g...  94.7 us
    psum x3, waiting for transfers between devices, dp_sum(): earlier = lax.psum(tuple(terms), 'dp')  71.9 us
    pallas_call x2, Pallas kernels, attend(): pl.pallas_call(partial(attend_kernel, heads, plan, len(proj)), out_shape=...  58.4 us
    unnamed x388, local copies, waits for them, and re-layouts  38.5 us
    ppermute x69, starting transfers between devices, other_core(): return lax.ppermute(value, 'section', [(0, 1), (1, 0)])  33.9 us
  transfers between devices with their start and end apart: 137, of which 42 were waited for; matrix products, arithmetic and copies ran while one was open for 32% of the time, Pallas kernels for 16%

profile of v5, /device:TPU:0, one launch (start us, length us, event | category | flops | bytes accessed | tf_op | source)
XLA Modules:
  0.0 1031.2 jit_solution(3295157193091555573)
XLA Ops:
  41.7 13.5 %collective-permute-done.4 = bf16[512,1024]{1,0:T(8,128)(2,1)} collective-permute-done((bf16[512,1024]{1,0:T(8,128)(2,1)}, bf16[512,1024]{1,0:T(8,128)(2,1)}, u32[]{:S(2)}, u32[]{:S(2)}) %collective-permute-start.4) | collective-permute-done | bytes 1048608 | tf_op jit(solution)/shard_map/ppermute | solution.py:744
  92.8 12.1 %collective-permute-start.11 = (bf16[1024,1792]{0,1:T(8,128)(2,1)}, bf16[1024,1792]{0,1:T(8,128)(2,1)}, u32[]{:S(2)}, u32[]{:S(2)}) collective-permute-start(bf16[1024,1792]{0,1:T(8,128)(2,1)} %pad_maximum_fusion.2), channel_id=1, source_target_pairs={{16,0},{17,1},{20,4},{21,5},{24,8},{25,9},{28,12},{29,13}} | collective-permute-start | bytes 11010056 | tf_op jit(solution)/shard_map/W1attn/ppermute | solution.py:744
  119.6 29.2 %attend.2 = (bf16[2048,256]{1,0:T(8,128)(2,1)}, f32[4,2048]{1,0:T(4,128)}, f32[1,128]{1,0:T(1,128)}, f32[1,1024]{1,0:T(1,128)}, f32[1,128]{1,0:T(1,128)}) custom-call(s32[2]{0:T(128)} %pad_add_fusion.order_ref, s32[8]{0:T(128)} %get-tuple-element.66.first_ref, s32[8]{0:T(128)} %get-tuple-element.67.last_ref, ...), custom_call_target="tpu_custom_call" | custom-call | flops 10737418240 | bytes 7340032 | tf_op jit(solution)/shard_map/attend/pallas_call | solution.py:277
  227.8 9.9 collective-permute-done.33
  275.6 29.2 %attend.3 = (bf16[2048,256]{1,0:T(8,128)(2,1)}, f32[4,2048]{1,0:T(4,128)}, f32[1,128]{1,0:T(1,128)}, f32[1,1024]{1,0:T(1,128)}, f32[1,128]{1,0:T(1,128)}) custom-call(s32[2]{0:T(128)} %pad_add_fusion.order_ref, s32[8]{0:T(128)} %get-tuple-element.66.first_ref, s32[8]{0:T(128)} %get-tuple-element.67.last_ref, ...), custom_call_target="tpu_custom_call" | custom-call | flops 10737418240 | bytes 7340032 | tf_op jit(solution)/shard_map/attend/pallas_call | solution.py:277
  307.7 11.4 %collective-permute-start.50 = (bf16[256,1024]{1,0:T(8,128)(2,1)S(1)}, bf16[256,1024]{1,0:T(8,128)(2,1)S(1)}, u32[]{:S(2)}, u32[]{:S(2)}) collective-permute-start(bf16[256,1024]{1,0:T(8,128)(2,1)S(1)} %slice.1256), channel_id=1, source_target_pairs={{0,16},{16,0},{1,17},{17,1},{2,18},{18,2},{3,19},{19,3},{4,20},{20... | collective-permute-start | bytes 1572872 | tf_op jit(solution)/shard_map/F1out/ssec2/ppermute | solution.py:747
  331.2 10.1 collective-permute-done.43
  366.2 8.3 collective-permute-done.53
  386.0 10.0 collective-permute-done.52
  410.0 8.1 collective-permute-done.61
  429.7 9.3 collective-permute-done.65
  447.3 7.0 fusion.75
  479.7 11.4 %collective-permute-done.75 = bf16[256,1024]{1,0:T(8,128)(2,1)S(1)} collective-permute-done((bf16[256,1024]{1,0:T(8,128)(2,1)S(1)}, bf16[256,1024]{1,0:T(8,128)(2,1)S(1)}, u32[]{:S(2)}, u32[]{:S(2)}) %collective-permute-start.75) | collective-permute-done | bytes 524320 | tf_op jit(solution)/shard_map/B1ctx1/ghop/ppermute | solution.py:744
  516.6 47.0 %attend_back.2 = bf16[2048,1536]{1,0:T(8,128)(2,1)} custom-call(s32[2]{0:T(128)} %pad_add_fusion.order_ref, s32[8]{0:T(128)} %get-tuple-element.66.first_ref, s32[8]{0:T(128)} %get-tuple-element.67.last_ref, bf16[512,1536]{1,0:T(8,128)(2,1)} %convolution_convert_fusion.5.refs_0_, bf16[512,1536]{1,0:T(8,128)(2,1)} %convolution_convert_fusion.4.refs_1_, ...), custom_call_target="tpu_custom_call" | custom-call | flops 2147483648 | bytes 2097152 | tf_op jit(solution)/shard_map/attend_back/pallas_call | solution.py:543
  610.5 9.3 collective-permute-done.89
  631.1 9.7 collective-permute-done.95
  660.7 7.7 fusion.78
  680.4 8.5 convolution_convert_fusion.1
  721.2 18.1 %collective-permute-done.107 = bf16[1024,1024]{1,0:T(8,128)(2,1)} collective-permute-done((bf16[1024,1024]{1,0:T(8,128)(2,1)}, bf16[1024,1024]{1,0:T(8,128)(2,1)}, u32[]{:S(2)}, u32[]{:S(2)}) %collective-permute-start.107) | collective-permute-done | bytes 2097184 | tf_op jit(solution)/shard_map/B0wmlp/ppermute | solution.py:744
  743.8 47.7 %attend_back.3 = bf16[2048,1536]{1,0:T(8,128)(2,1)} custom-call(s32[2]{0:T(128)} %pad_add_fusion.order_ref, s32[8]{0:T(128)} %get-tuple-element.66.first_ref, s32[8]{0:T(128)} %get-tuple-element.67.last_ref, bf16[512,1536]{1,0:T(8,128)(2,1)} %convolution_convert_fusion.9.refs_0_, bf16[512,1536]{1,0:T(8,128)(2,1)} %convolution_convert_fusion.8.refs_1_, ...), custom_call_target="tpu_custom_call" | custom-call | flops 2147483648 | bytes 2097152 | tf_op jit(solution)/shard_map/attend_back/pallas_call | solution.py:543
  805.7 8.7 convolution_convert_fusion
  819.4 9.7 all-reduce.7.cloned.1.call-done
  856.1 11.2 %collective-permute-done.116 = bf16[256,1024]{1,0:T(8,128)(2,1)} collective-permute-done((bf16[256,1024]{1,0:T(8,128)(2,1)}, bf16[256,1024]{1,0:T(8,128)(2,1)}, u32[]{:S(2)}, u32[]{:S(2)}) %collective-permute-start.116) | collective-permute-done | bytes 524320 | tf_op jit(solution)/shard_map/B0in/shop/ppermute | solution.py:744
  945.6 62.2 %all-reduce.9.cloned.1.call-done = (bf16[512,1792]{1,0:T(8,128)(2,1)}, bf16[512,1792]{1,0:T(8,128)(2,1)}) async-done(((bf16[512,1792]{1,0:T(8,128)(2,1)}, bf16[512,1792]{1,0:T(8,128)(2,1)}), (bf16[512,1792]{1,0:T(8,128)(2,1)}, bf16[512,1792]{1,0:T(8,128)(2,1)})) %all-reduce.9.cloned.1.call-update) | async-done | bytes 3670032 | tf_op jit(solution)/shard_map/B0wattn/psum | solution.py:993
  (987 shorter events, 576.6 us)
Async XLA Ops:
  7.2 696.9 %all-reduce.5.cloned.1.call-start = ((), (), s32[]{:S(2)}) async-start(), calls=%async_computation | async-start | bytes 4194304 | tf_op jit(solution)/shard_map/psum | solution.py:993
  23.2 51.6 %collective-permute-start.2 = (bf16[1024,1792]{0,1:T(8,128)(2,1)}, bf16[1024,1792]{0,1:T(8,128)(2,1)}, u32[]{:S(2)}, u32[]{:S(2)}) collective-permute-start(bf16[1024,1792]{0,1:T(8,128)(2,1)} %pad_maximum_fusion.2), channel_id=1, source_target_pairs={{0,2},{1,3},{2,16},{3,17},{4,6},{5,7},{6,20},{7,21},{8,10},{9,11},... | collective-permute-start | bytes 11010056 | tf_op jit(solution)/shard_map/W0attn/ppermute | solution.py:744
  26.3 48.4 %collective-permute-start.1 = (bf16[1024,1792]{0,1:T(8,128)(2,1)}, bf16[1024,1792]{0,1:T(8,128)(2,1)}, u32[]{:S(2)}, u32[]{:S(2)}) collective-permute-start(bf16[1024,1792]{0,1:T(8,128)(2,1)} %pad_maximum_fusion.2), channel_id=1, source_target_pairs={{2,18},{3,19},{6,22},{7,23},{10,26},{11,27},{14,30},{15,31}} | collective-permute-start | bytes 11010056 | tf_op jit(solution)/shard_map/W0attn/ppermute | solution.py:744
  66.6 82.2 %collective-permute-start.10 = (bf16[1024,2048]{1,0:T(8,128)(2,1)}, bf16[1024,2048]{1,0:T(8,128)(2,1)}, u32[]{:S(2)}, u32[]{:S(2)}) collective-permute-start(bf16[1024,2048]{1,0:T(8,128)(2,1)} %pad_maximum_fusion.1), channel_id=1, source_target_pairs={{0,1},{1,16},{2,3},{3,18},{4,5},{5,20},{6,7},{7,22},{8,9},{9,24},{... | collective-permute-start | bytes 12582920 | tf_op jit(solution)/shard_map/W0mlp/ppermute | solution.py:744
  72.1 76.7 %collective-permute-start.9 = (bf16[1024,2048]{1,0:T(8,128)(2,1)}, bf16[1024,2048]{1,0:T(8,128)(2,1)}, u32[]{:S(2)}, u32[]{:S(2)}) collective-permute-start(bf16[1024,2048]{1,0:T(8,128)(2,1)} %pad_maximum_fusion.1), channel_id=1, source_target_pairs={{1,17},{3,19},{5,21},{7,23},{9,25},{11,27},{13,29},{15,31}} | collective-permute-start | bytes 12582920 | tf_op jit(solution)/shard_map/W0mlp/ppermute | solution.py:744
  90.3 58.5 %collective-permute-start.12 = (bf16[1024,1792]{0,1:T(8,128)(2,1)}, bf16[1024,1792]{0,1:T(8,128)(2,1)}, u32[]{:S(2)}, u32[]{:S(2)}) collective-permute-start(bf16[1024,1792]{0,1:T(8,128)(2,1)} %pad_maximum_fusion.2), channel_id=1, source_target_pairs={{16,2},{17,3},{18,16},{19,17},{20,6},{21,7},{22,20},{23,21},{24,10... | collective-permute-start | bytes 11010056 | tf_op jit(solution)/shard_map/W1attn/ppermute | solution.py:744
  92.8 56.0 %collective-permute-start.11 = (bf16[1024,1792]{0,1:T(8,128)(2,1)}, bf16[1024,1792]{0,1:T(8,128)(2,1)}, u32[]{:S(2)}, u32[]{:S(2)}) collective-permute-start(bf16[1024,1792]{0,1:T(8,128)(2,1)} %pad_maximum_fusion.2), channel_id=1, source_target_pairs={{16,0},{17,1},{20,4},{21,5},{24,8},{25,9},{28,12},{29,13}} | collective-permute-start | bytes 11010056 | tf_op jit(solution)/shard_map/W1attn/ppermute | solution.py:744
  266.2 38.6 %collective-permute-start.39 = (bf16[1024,2048]{1,0:T(8,128)(2,1)}, bf16[1024,2048]{1,0:T(8,128)(2,1)}, u32[]{:S(2)}, u32[]{:S(2)}) collective-permute-start(bf16[1024,2048]{1,0:T(8,128)(2,1)} %pad_maximum_fusion.1), channel_id=1, source_target_pairs={{16,1},{17,16},{18,3},{19,18},{20,5},{21,20},{22,7},{23,22},{24,9}... | collective-permute-start | bytes 12582920 | tf_op jit(solution)/shard_map/W1mlp/ppermute | solution.py:744
  268.8 36.0 %collective-permute-start.38 = (bf16[1024,2048]{1,0:T(8,128)(2,1)}, bf16[1024,2048]{1,0:T(8,128)(2,1)}, u32[]{:S(2)}, u32[]{:S(2)}) collective-permute-start(bf16[1024,2048]{1,0:T(8,128)(2,1)} %pad_maximum_fusion.1), channel_id=1, source_target_pairs={{16,0},{18,2},{20,4},{22,6},{24,8},{26,10},{28,12},{30,14}} | collective-permute-start | bytes 12582920 | tf_op jit(solution)/shard_map/W1mlp/ppermute | solution.py:744
  271.3 33.5 %collective-permute-start.40 = (bf16[512,1024]{1,0:T(8,128)(2,1)}, bf16[512,1024]{1,0:T(8,128)(2,1)S(1)}, u32[]{:S(2)}, u32[]{:S(2)}) collective-permute-start(bf16[512,1024]{1,0:T(8,128)(2,1)} %get-tuple-element.273), channel_id=1, source_target_pairs={{0,2},{1,3},{18,16},{19,17},{4,6},{5,7},{22,20},{23,21},{8,10},{9,... | collective-permute-start | bytes 3145736 | tf_op jit(solution)/shard_map/COT/ppermute | solution.py:744
  307.7 38.5 %collective-permute-start.50 = (bf16[256,1024]{1,0:T(8,128)(2,1)S(1)}, bf16[256,1024]{1,0:T(8,128)(2,1)S(1)}, u32[]{:S(2)}, u32[]{:S(2)}) collective-permute-start(bf16[256,1024]{1,0:T(8,128)(2,1)S(1)} %slice.1256), channel_id=1, source_target_pairs={{0,16},{16,0},{1,17},{17,1},{2,18},{18,2},{3,19},{19,3},{4,20},{20... | collective-permute-start | bytes 1572872 | tf_op jit(solution)/shard_map/F1out/ssec2/ppermute | solution.py:747
  477.4 86.2 %collective-permute-start.82 = (bf16[1024,1024]{1,0:T(8,128)(2,1)}, bf16[1024,1024]{1,0:T(8,128)(2,1)}, u32[]{:S(2)}, u32[]{:S(2)}) collective-permute-start(bf16[1024,1024]{1,0:T(8,128)(2,1)} %fusion.81), channel_id=1, source_target_pairs={{1,16},{3,18},{16,1},{18,3},{5,20},{7,22},{20,5},{22,7},{9,24},{11... | collective-permute-start | bytes 6291464 | tf_op jit(solution)/shard_map/B1wmlp/ppermute | solution.py:744
  502.0 61.6 %collective-permute-start.81 = (bf16[1024,1024]{1,0:T(8,128)(2,1)}, bf16[1024,1024]{1,0:T(8,128)(2,1)}, u32[]{:S(2)}, u32[]{:S(2)}) collective-permute-start(bf16[1024,1024]{1,0:T(8,128)(2,1)} %add_convert_fusion.3), channel_id=1, source_target_pairs={{0,16},{1,0},{2,18},{3,2},{16,17},{17,1},{18,19},{19,3},{4,20},{5,... | collective-permute-start | bytes 6291464 | tf_op jit(solution)/shard_map/B1wmlp/ppermute | solution.py:744
  587.2 241.9 %all-reduce.7.cloned.1.call-start = ((), (), s32[]{:S(2)}) async-start(), calls=%async_computation.1 | async-start | bytes 4194304 | tf_op jit(solution)/shard_map/psum | solution.py:993
  698.3 41.0 %collective-permute-start.107 = (bf16[1024,1024]{1,0:T(8,128)(2,1)}, bf16[1024,1024]{1,0:T(8,128)(2,1)}, u32[]{:S(2)}, u32[]{:S(2)}) collective-permute-start(bf16[1024,1024]{1,0:T(8,128)(2,1)} %add_convert_fusion.1), channel_id=1, source_target_pairs={{0,16},{1,0},{2,18},{3,2},{16,17},{17,1},{18,19},{19,3},{4,20},{5,... | collective-permute-start | bytes 6291464 | tf_op jit(solution)/shard_map/B0wmlp/ppermute | solution.py:744
  712.6 79.0 %collective-permute-start.109 = (bf16[512,1792]{1,0:T(8,128)(2,1)}, bf16[512,1792]{1,0:T(8,128)(2,1)}, u32[]{:S(2)}, u32[]{:S(2)}) collective-permute-start(bf16[512,1792]{1,0:T(8,128)(2,1)} %get-tuple-element.203), channel_id=1, source_target_pairs={{0,16},{1,17},{2,0},{3,1},{16,18},{17,19},{18,2},{19,3},{4,20},{5,... | collective-permute-start | bytes 5505032 | tf_op jit(solution)/shard_map/B1wattn/ppermute | solution.py:744
  713.7 77.8 %collective-permute-start.110 = (bf16[512,1792]{1,0:T(8,128)(2,1)}, bf16[512,1792]{1,0:T(8,128)(2,1)}, u32[]{:S(2)}, u32[]{:S(2)}) collective-permute-start(bf16[512,1792]{1,0:T(8,128)(2,1)} %get-tuple-element.204), channel_id=1, source_target_pairs={{2,16},{3,17},{16,2},{17,3},{6,20},{7,21},{20,6},{21,7},{10,24},{1... | collective-permute-start | bytes 5505032 | tf_op jit(solution)/shard_map/B1wattn/ppermute | solution.py:744
  743.7 264.1 %all-reduce.9.cloned.1.call-start = ((), (), s32[]{:S(2)}) async-start(), calls=%async_computation.2 | async-start | bytes 7340032 | tf_op jit(solution)/shard_map/B0wattn/psum | solution.py:993
  805.2 38.4 %collective-permute-start.111 = (bf16[256,1024]{1,0:T(8,128)(2,1)}, bf16[256,1024]{1,0:T(8,128)(2,1)}, u32[]{:S(2)}, u32[]{:S(2)}) collective-permute-start(bf16[256,1024]{1,0:T(8,128)(2,1)} %slice.1241), channel_id=1, source_target_pairs={{0,16},{16,0},{1,17},{17,1},{2,18},{18,2},{3,19},{19,3},{4,20},{20... | collective-permute-start | bytes 1572872 | tf_op jit(solution)/shard_map/B0in/ssec2/ppermute | solution.py:747
  817.3 35.5 %collective-permute-start.121 = (bf16[512,1792]{1,0:T(8,128)(2,1)}, bf16[512,1792]{1,0:T(8,128)(2,1)S(1)}, u32[]{:S(2)}, u32[]{:S(2)}) collective-permute-start(bf16[512,1792]{1,0:T(8,128)(2,1)} %get-tuple-element.195), channel_id=1, source_target_pairs={{0,16},{1,17},{2,0},{3,1},{16,18},{17,19},{18,2},{19,3},{4,20},{5,... | collective-permute-start | bytes 5505032 | tf_op jit(solution)/shard_map/B0wattn/ppermute | solution.py:744
  817.3 36.7 %collective-permute-start.122 = (bf16[512,1792]{1,0:T(8,128)(2,1)}, bf16[512,1792]{1,0:T(8,128)(2,1)}, u32[]{:S(2)}, u32[]{:S(2)}) collective-permute-start(bf16[512,1792]{1,0:T(8,128)(2,1)} %get-tuple-element.196), channel_id=1, source_target_pairs={{2,16},{3,17},{16,2},{17,3},{6,20},{7,21},{20,6},{21,7},{10,24},{1... | collective-permute-start | bytes 5505032 | tf_op jit(solution)/shard_map/B0wattn/ppermute | solution.py:744
  839.1 62.5 %collective-permute-start.79 = (bf16[512,1024]{1,0:T(8,128)(2,1)}, bf16[512,1024]{1,0:T(8,128)(2,1)}, u32[]{:S(2)}, u32[]{:S(2)}) collective-permute-start(bf16[512,1024]{1,0:T(8,128)(2,1)} %pad_maximum_fusion.7), channel_id=1, source_target_pairs={{2,0},{3,1},{18,2},{19,3},{6,4},{7,5},{22,6},{23,7},{10,8},{11,9},... | collective-permute-start | bytes 3145736 | tf_op jit(solution)/shard_map/OUTROWS/ppermute | solution.py:744
  843.6 60.3 %collective-permute-start.77 = (bf16[512,1024]{1,0:T(8,128)(2,1)}, bf16[512,1024]{1,0:T(8,128)(2,1)}, u32[]{:S(2)}, u32[]{:S(2)}) collective-permute-start(bf16[512,1024]{1,0:T(8,128)(2,1)} %pad_maximum_fusion.7), channel_id=1, source_target_pairs={{16,2},{17,3},{20,6},{21,7},{24,10},{25,11},{28,14},{29,15}} | collective-permute-start | bytes 3145736 | tf_op jit(solution)/shard_map/OUTROWS/ppermute | solution.py:744
  900.5 37.3 %collective-permute-start.123 = (bf16[1024,1024]{1,0:T(8,128)(2,1)}, bf16[1024,1024]{1,0:T(8,128)(2,1)}, u32[]{:S(2)}, u32[]{:S(2)}) collective-permute-start(bf16[1024,1024]{1,0:T(8,128)(2,1)} %broadcast_select_fusion), channel_id=1, source_target_pairs={{0,16},{16,0},{1,17},{17,1},{2,18},{18,2},{3,19},{19,3},{4,20},{20... | collective-permute-start | bytes 6291464 | tf_op jit(solution)/shard_map/ppermute | solution.py:747
  (284 other events, 3554.8 us)
Sparse Core Ops, SparseCore 0:
  587.3 91.6 all-reduce.4
  743.8 85.2 all-reduce.6
  856.2 151.6 all-reduce.8
